TPU v7x, 256 devices: a whole 4x4x8 slice. The times are simulated.
256 devices in a mesh: row: 32 (over y, z_lo, x), col: 8 (over z_hi, core).
Axes of the slice: x: 4, y: 4, z: 8 (z_hi: 4, z_lo: 2; z = z_hi * 2 + z_lo), core: 2. Of those that a mesh axis runs over, the one named last changes fastest.
Arguments:
- noise: bfloat16 [8, 2, 32, 2048], P(None, None, 'row', 'col'), may hold values from -6 to 6
- diag_factor: bfloat16 [2, 32, 2048, 2048], P(None, 'row', 'col'), may hold values from -0.125 to 0.125
- left_factor: bfloat16 [32, 64, 64, 2048], P('row', None, None, 'col'), may hold values from -0.09375 to 0.09375
- right_factor: bfloat16 [32, 64, 64, 2048], P('row', None, None, 'col'), may hold values from -0.125 to 0.125
- tile_ranks: int32 [32, 64], P('row'), may hold values from 1 to 64
- pair_first: int32 [32, 8, 4096], P('row', 'col'), may hold values from 4096 to 8191
- pair_partner: int32 [32, 8, 4096], P('row', 'col'), may hold values from 0 to 8191, as said below
- bin_ids: int32 [32, 8, 4096], P('row', 'col'), may hold values from 0 to 127, as said below
Outputs:
- samples: float32 [8, 2, 32, 2048], P(None, None, 'row', 'col')
- variogram: float32 [8, 128], replicated
Inputs may be any that keep to these rules, and one draw needn't show every extreme that they name: Pairs of the first tile-row pair (r = 0) have pair_partner of 4096 or more. `bin_ids`: bins may hold no pair.
All inputs are finite; a program needn't handle non-finite values.
Results may differ from a plain program's by a relative error of at most 0.0012.
Values may be sent and summed in bfloat16 or wider, within the bound.
No kernel may reach another device: no remote copies, remote signals or barrier semaphores. Data moves between devices by JAX's collectives and lax.ppermute only.
A program may use at most 64 MiB of HBM per device.

v0:
```python
import functools

import jax
import jax.numpy as jnp
from jax import lax
from jax.sharding import Mesh
from jax.sharding import PartitionSpec as P

NBIN = 128
PAIRS = 4096
ROW = ("row_0", "row_1", "row_2")
COL = ("col_0", "col_1")
ROW_COL = ("row_0", "row_1", "row_2", "col_0", "col_1")


def from_everyone(x, axis):
    peers = lax.axis_size(axis)
    return lax.all_to_all(jnp.broadcast_to(x[None], (peers, *x.shape)), axis, 0, 0, tiled=True)


def laid_out(pieces, dim):
    pieces = jnp.moveaxis(pieces, 0, dim)
    dims = pieces.shape
    return pieces.reshape(*dims[:dim], dims[dim] * dims[dim + 1], *dims[dim + 2 :])


def gather_directly(x, axis, dim):
    pieces = from_everyone(x, axis)
    return laid_out(pieces, dim)


def over_copies(x, axis):
    everything = from_everyone(x, axis)
    return jnp.sum(everything, axis=0)


def shifted(value, axis, steps):
    count = lax.axis_size(axis)
    leading, last = (max(0, -steps), min(count, count - steps))
    return lax.ppermute(value, axis, [(source, source + steps) for source in range(leading, last)])


def one_axis_at_a_time(x, axes):
    return functools.reduce(lax.psum, axes, x)


def body(
    noise, diag_factor, left_factor, right_factor, tile_ranks, pair_first, pair_partner, bin_ids
):
    row_at = lax.axis_index(ROW)
    col_at = lax.axis_index(COL)
    row_count = lax.axis_size(ROW)
    col_count = lax.axis_size(COL)
    tile_count = 2 * row_count
    samples_n = noise.shape[0]
    shard_len = noise.shape[3]
    tile_len = shard_len * col_count
    columns = gather_directly(noise, ROW, 2)
    segments = jnp.concatenate([columns[:, 0], columns[:, 1][:, ::-1]], axis=1)
    own_noise = gather_directly(noise, COL, 3)[:, :, 0]
    slot_ids = jnp.arange(tile_count, dtype=jnp.int32)
    source = jnp.where(slot_ids < row_at, slot_ids, slot_ids - row_at)
    chosen = jnp.take(segments, source, axis=1)
    partial_proj = jnp.einsum(
        "skt,kqt->ksq", chosen, right_factor[0], preferred_element_type=jnp.float32
    )
    projected = over_copies(partial_proj, COL)
    rank_dim = right_factor.shape[2]
    in_rank = jnp.arange(rank_dim, dtype=jnp.int32)[None, :] < tile_ranks[0][:, None]
    coeffs = jnp.where(in_rank[:, None, :], projected, 0.0).astype(jnp.bfloat16)
    select = jnp.stack(
        [slot_ids < row_at, (slot_ids >= row_at) & (slot_ids < tile_count - 1)]
    ).astype(jnp.bfloat16)
    weighted = select[:, :, None, None] * coeffs[None]
    weighted = jnp.transpose(weighted, (0, 2, 1, 3)).reshape(2, samples_n, tile_count * rank_dim)
    factor_rows = left_factor[0].reshape(tile_count * rank_dim, shard_len)
    off_diag = jnp.einsum("hsm,mt->sht", weighted, factor_rows, preferred_element_type=jnp.float32)
    global_rows = col_at * shard_len + jnp.arange(shard_len, dtype=jnp.int32)
    col_ids = jnp.arange(tile_len, dtype=jnp.int32)
    tile_rows = diag_factor[:, 0]
    effective = jnp.where(
        col_ids[None, :] < global_rows[:, None], tile_rows, jnp.zeros((), jnp.bfloat16)
    )
    effective = effective + (col_ids[None, :] == global_rows[:, None]).astype(jnp.bfloat16)[None]
    on_diag = jnp.einsum("sht,hit->shi", own_noise, effective, preferred_element_type=jnp.float32)
    samples = (on_diag + off_diag)[:, :, None, :]
    own_tiles = gather_directly(samples, COL, 3)
    prev_tiles = shifted(own_tiles.astype(jnp.bfloat16), ROW, 1).astype(own_tiles.dtype)
    pooled = jnp.concatenate(
        [prev_tiles[:, 0, 0], prev_tiles[:, 1, 0], own_tiles[:, 0, 0], own_tiles[:, 1, 0]], axis=1
    )
    first_idx = pair_first[0, 0]
    second_idx = pair_partner[0, 0]
    bin_local = bin_ids[0, 0]
    differ = jnp.take(pooled, first_idx, axis=1) - jnp.take(pooled, second_idx, axis=1)
    half_sq = 0.5 * differ * differ
    block_len = min(2048, PAIRS)
    bin_range = jnp.arange(NBIN, dtype=jnp.int32)
    bin_sums = jnp.zeros((samples_n, NBIN), jnp.float32)
    bin_counts = jnp.zeros((NBIN,), jnp.float32)
    for block_id in range(PAIRS // block_len):
        block_bins = bin_local[block_id * block_len : (block_id + 1) * block_len]
        onehot = (block_bins[:, None] == bin_range[None, :]).astype(jnp.float32)
        block_sq = half_sq[:, block_id * block_len : (block_id + 1) * block_len]
        bin_sums = bin_sums + jnp.dot(
            block_sq, onehot, precision=lax.Precision.HIGHEST, preferred_element_type=jnp.float32
        )
        bin_counts = bin_counts + jnp.sum(onehot, axis=0)
    totals, counts = (
        one_axis_at_a_time(bin_sums, ROW_COL),
        one_axis_at_a_time(bin_counts, ROW_COL),
    )
    variogram = totals / jnp.maximum(counts, 1.0)[None, :]
    return (samples, variogram)


def solution(mesh):
    split = Mesh(mesh.devices.reshape(4, 2, 4, 4, 2), ("row_0", "row_1", "row_2", "col_0", "col_1"))
    return jax.shard_map(
        body,
        mesh=split,
        in_specs=(
            P(None, None, ROW, COL),
            P(None, ROW, COL, None),
            P(ROW, None, None, COL),
            P(ROW, None, None, COL),
            P(ROW, None),
            P(ROW, COL, None),
            P(ROW, COL, None),
            P(ROW, COL, None),
        ),
        out_specs=(P(None, None, ROW, COL), P()),
        check_vma=False,
    )
```

profile of v0, /device:TPU:1, one launch (start us, length us, event | category | flops | bytes accessed | tf_op | source)
XLA Modules:
  0.0 184.6 jit_solution(1885283668157041908)
XLA Ops:
  0.6 0.0 copy-start
  0.6 1.7 broadcast_in_dim.87
  2.3 9.2 %all-to-all-start.1 = ((bf16[32,8,2,1,256]{4,2,1,3,0:T(2,128)(2,1)}), bf16[32,8,2,1,256]{4,2,1,3,0:T(2,128)(2,1)S(1)}, u32[]{:S(2)}, u32[]{:S(2)}) async-start(bf16[32,8,2,1,256]{4,2,1,3,0:T(2,128)(2,1)} %broadcast_in_dim.87), calls=%async_computation.1 | async-start | bytes 524288 | tf_op jit(solution)/shard_map/all_to_all | solution.py:18
  11.5 0.7 copy.51
  12.3 0.1 mul.46
  12.4 0.1 mul.47
  12.5 0.7 iota_compare_fusion.6
  13.2 6.3 %all-to-all-done.1 = bf16[32,8,2,1,256]{4,2,1,3,0:T(2,128)(2,1)S(1)} async-done(((bf16[32,8,2,1,256]{4,2,1,3,0:T(2,128)(2,1)}), bf16[32,8,2,1,256]{4,2,1,3,0:T(2,128)(2,1)S(1)}, u32[]{:S(2)}, u32[]{:S(2)}) %all-to-all-start.1) | async-done | bytes 262176 | tf_op jit(solution)/shard_map/all_to_all | solution.py:18
  19.5 0.6 broadcast_in_dim.84
  20.2 9.7 %all-to-all-start = ((bf16[8,8,2,1,256]{4,1,2,3,0:T(8,128)(2,1)}), bf16[8,8,2,1,256]{4,1,2,3,0:T(8,128)(2,1)S(1)}, u32[]{:S(2)}, u32[]{:S(2)}) async-start(bf16[8,8,2,1,256]{4,1,2,3,0:T(8,128)(2,1)} %broadcast_in_dim.84), calls=%async_computation | async-start | bytes 131072 | tf_op jit(solution)/shard_map/all_to_all | solution.py:18
  29.8 0.1 copy.66
  29.9 0.1 copy.55
  30.1 0.6 gather_fusion
  30.7 2.3 %fusion = f32[64,8,64]{2,1,0:T(8,128)S(1)} fusion(bf16[1,64,64,256]{3,2,1,0:T(8,128)(2,1)} %param.13, bf16[64,8,256]{2,1,0:T(8,128)(2,1)S(1)} %gather_fusion, pred[64]{0:T(512)(128)(4,1)S(1)} %compare_and_fusion.2), kind=kOutput, calls=%fused_computation.5 | convolution fusion | flops 16908288 | bytes 2490432 | tf_op jit(solution)/shard_map/skt,kqt->ksq/dot_general | solution.py:64
  33.0 1.5 broadcast_in_dim.89
  34.5 0.0 copy-start.3
  34.5 0.0 copy-start.2
  34.5 0.0 copy-start.4
  34.5 3.4 %reshape.195 = f32[8,1,32768]{2,1,0:T(1,128)} reshape(f32[8,64,8,64]{3,2,1,0:T(8,128)} %broadcast_in_dim.89) | data formatting | bytes 2097152
  37.9 0.0 all-to-all-done
  37.9 7.2 %all-to-all-start.2 = ((f32[8,1,32768]{2,1,0:T(1,128)}), f32[8,1,32768]{2,1,0:T(1,128)S(1)}, u32[]{:S(2)}, u32[]{:S(2)}) async-start(f32[8,1,32768]{2,1,0:T(1,128)} %reshape.195), calls=%async_computation.2 | async-start | bytes 2097152 | tf_op jit(solution)/shard_map/all_to_all | solution.py:18
  45.1 0.0 copy-done.3
  45.1 0.0 copy-done.2
  45.2 0.0 copy-done.4
  45.2 0.7 fusion.5
  45.9 2.2 %fusion.7 = f32[8,2,256]{2,0,1:T(8,128)S(1)} fusion(bf16[8,2,2048]{2,0,1:T(8,128)(2,1)S(1)} %bitcast.80, bf16[2,1,256,2048]{3,2,1,0:T(8,128)(2,1)} %param.11, pred[256,2048]{1,0:T(8,128)(4,1)S(1)} %get-tuple-element.34, bf16[256,2048]{1,0:T(8,128)(2,1)S(1)} %get-tuple-element.33), kind=kOutput, calls=%fused_computation.14 | convolution fusion | flops 18874368 | bytes 3751936 | tf_op jit(solution)/shard_map/sht,hit->shi/dot_general | solution.py:85
  48.1 23.5 %all-to-all-done.2 = f32[8,1,32768]{2,1,0:T(1,128)S(1)} async-done(((f32[8,1,32768]{2,1,0:T(1,128)}), f32[8,1,32768]{2,1,0:T(1,128)S(1)}, u32[]{:S(2)}, u32[]{:S(2)}) %all-to-all-start.2) | async-done | bytes 1048608 | tf_op jit(solution)/shard_map/all_to_all | solution.py:18
  71.6 0.0 copy-start.1
  71.6 1.0 copy-done.1
  72.6 0.5 broadcast.154
  73.1 4.4 %reduce = f32[8,32768]{1,0:T(8,128)S(1)} reduce(f32[8,1,32768]{2,1,0:T(1,128)} %copy-done.1, f32[]{:T(128)} %broadcast.154), dimensions={1}, to_apply=%all_to_all.14.reduce_sub_computation | reduce | bytes 2097156 | tf_op jit(solution)/shard_map/all_to_all | solution.py:18
  77.4 2.2 %reshape.196 = f32[8,64,8,64]{3,2,1,0:T(8,128)} reshape(f32[8,32768]{1,0:T(8,128)S(1)} %reduce) | data formatting | bytes 2097152
  79.6 1.7 reduce_sum.27
  81.4 0.1 fusion.21
  81.5 0.2 mul.49
  81.6 0.0 copy-done
  81.7 0.4 fusion.10
  82.0 0.7 broadcast_in_dim.92
  82.7 5.8 %all-to-all-start.3 = ((f32[8,8,2,1,256]{4,1,3,2,0:T(8,128)}), f32[8,8,2,1,256]{4,1,3,2,0:T(8,128)S(1)}, u32[]{:S(2)}, u32[]{:S(2)}) async-start(f32[8,8,2,1,256]{4,1,3,2,0:T(8,128)} %broadcast_in_dim.92), calls=%async_computation.3 | async-start | bytes 262144 | tf_op jit(solution)/shard_map/all_to_all | solution.py:18
  88.5 1.2 convert_reduce_fusion
  89.7 0.6 copy.61
  90.4 6.2 %all-to-all-done.3 = f32[8,8,2,1,256]{4,1,3,2,0:T(8,128)S(1)} async-done(((f32[8,8,2,1,256]{4,1,3,2,0:T(8,128)}), f32[8,8,2,1,256]{4,1,3,2,0:T(8,128)S(1)}, u32[]{:S(2)}, u32[]{:S(2)}) %all-to-all-start.3) | async-done | bytes 131104 | tf_op jit(solution)/shard_map/all_to_all | solution.py:18
  96.6 0.1 copy.57
  96.7 2.5 %collective-permute-start = (bf16[8,2,1,2048]{3,0,2,1:T(8,128)(2,1)S(1)}, bf16[8,2,1,2048]{3,0,2,1:T(8,128)(2,1)S(1)}, u32[]{:S(2)}, u32[]{:S(2)}) collective-permute-start(bf16[8,2,1,2048]{3,0,2,1:T(8,128)(2,1)S(1)} %convert_bitcast_fusion), channel_id=1, source_target_pairs={{0,8},{8,16},{16,24},{24,32},{32,40},{40,48},{48,56},{56,64},{64,7... | collective-permute-start | bytes 196616 | tf_op jit(solution)/shard_map/ppermute | solution.py:40
  99.2 1.1 collective-permute-done
  100.4 2.6 %copy.59 = f32[8,8192]{0,1:T(8,128)} copy(f32[8,8192]{1,0:T(8,128)S(1)} %pad_maximum_fusion.1) | data formatting | bytes 524288 | tf_op jit(solution)/shard_map/concatenate | solution.py:89
  103.0 16.3 %gather_fusion.1 = f32[4096,8]{1,0:T(8,128)} fusion(f32[8,8192]{0,1:T(8,128)} %copy.59, s32[4096]{0:T(1024)S(1)} %fusion.26), kind=kCustom, calls=%fused_computation.clone | custom fusion | bytes 278528 | tf_op jit(solution)/shard_map/jit(_take)/gather | solution.py:95
  119.3 16.3 %gather_fusion.2 = f32[4096,8]{1,0:T(8,128)} fusion(f32[8,8192]{0,1:T(8,128)} %copy.59, s32[4096]{0:T(1024)S(1)} %fusion.27), kind=kCustom, calls=%fused_computation.1.clone | custom fusion | bytes 278528 | tf_op jit(solution)/shard_map/jit(_take)/gather | solution.py:95
  135.5 5.1 %multiply_multiply_fusion = f32[8,4096]{0,1:T(8,128)S(1)} fusion(f32[4096,8]{1,0:T(8,128)} %gather_fusion.2, f32[4096,8]{1,0:T(8,128)} %gather_fusion.1, pred[4096]{0:T(1024)(128)(4,1)S(1)} %get-tuple-element.37, pred[4096]{0:T(1024)(128)(4,1)S(1)} %get-tuple-element.38), kind=kLoop, calls=%fused_computation.3 | loop fusion | flops 163840 | bytes 401408 | tf_op jit(solution)/shard_map/mul | solution.py:96
  140.7 1.2 fusion.12
  141.9 1.3 convolution_add_fusion
  143.2 11.7 %all-reduce.2 = (f32[8,128]{1,0:T(8,128)S(1)}, f32[128]{0:T(128)S(1)}) all-reduce(f32[8,128]{1,0:T(8,128)S(1)} %convolution_add_fusion, f32[128]{0:T(128)S(1)} %add.96), channel_id=1, replica_groups=mesh['row_0'=4,'row_1'=2,'row_2'=4,'col_0'=4,'col_1'=2] {'row_0'}, use_global_device_ids=true, to_apply=%region_1.3 | all-reduce | flops 1152 | bytes 9216 | tf_op jit(solution)/shard_map/psum | solution.py:44
  154.9 4.1 %all-reduce.4 = (f32[8,128]{1,0:T(8,128)S(1)}, f32[128]{0:T(128)S(1)}) all-reduce(f32[8,128]{1,0:T(8,128)S(1)} %get-tuple-element.21, f32[128]{0:T(128)S(1)} %get-tuple-element.22), channel_id=1, replica_groups=mesh['row_0'=4,'row_1'=2,'row_2'=4,'col_0'=4,'col_1'=2] {'row_1'}, use_global_device_ids=true, to_apply=%region_2.4 | all-reduce | flops 1152 | bytes 9216 | tf_op jit(solution)/shard_map/psum | solution.py:44
  158.9 6.1 %all-reduce.1 = (f32[8,128]{1,0:T(8,128)S(1)}, f32[128]{0:T(128)S(1)}) all-reduce(f32[8,128]{1,0:T(8,128)S(1)} %get-tuple-element.25, f32[128]{0:T(128)S(1)} %get-tuple-element.26), channel_id=1, replica_groups=mesh['row_0'=4,'row_1'=2,'row_2'=4,'col_0'=4,'col_1'=2] {'row_2'}, use_global_device_ids=true, to_apply=%region_3.5 | all-reduce | flops 1152 | bytes 9216 | tf_op jit(solution)/shard_map/psum | solution.py:44
  165.0 7.8 %all-reduce = (f32[8,128]{1,0:T(8,128)S(1)}, f32[128]{0:T(128)S(1)}) all-reduce(f32[8,128]{1,0:T(8,128)S(1)} %get-tuple-element.19, f32[128]{0:T(128)S(1)} %get-tuple-element.20), channel_id=1, replica_groups=mesh['row_0'=4,'row_1'=2,'row_2'=4,'col_0'=4,'col_1'=2] {'col_0'}, use_global_device_ids=true, to_apply=%region_4.6 | all-reduce | flops 1152 | bytes 9216 | tf_op jit(solution)/shard_map/psum | solution.py:44
  172.8 11.2 %all-reduce.3 = (f32[8,128]{1,0:T(8,128)S(1)}, f32[128]{0:T(128)S(1)}) all-reduce(f32[8,128]{1,0:T(8,128)S(1)} %get-tuple-element.17, f32[128]{0:T(128)S(1)} %get-tuple-element.18), channel_id=1, replica_groups=mesh['row_0'=4,'row_1'=2,'row_2'=4,'col_0'=4,'col_1'=2] {'col_1'}, use_global_device_ids=true, to_apply=%region_5.7 | all-reduce | flops 1152 | bytes 9216 | tf_op jit(solution)/shard_map/psum | solution.py:44
  184.0 0.6 broadcast_divide_fusion
  (25 shorter events, 0.3 us)
Async XLA Ops:
  0.6 81.0 %copy-start = (bf16[1,64,64,256]{3,2,1,0:T(8,128)(2,1)S(1)}, bf16[1,64,64,256]{3,2,1,0:T(8,128)(2,1)}, u32[]{:S(2)}) copy-start(bf16[1,64,64,256]{3,2,1,0:T(8,128)(2,1)} %param.12) | copy-start | bytes 6291460
  2.3 17.2 %all-to-all-start.1 = ((bf16[32,8,2,1,256]{4,2,1,3,0:T(2,128)(2,1)}), bf16[32,8,2,1,256]{4,2,1,3,0:T(2,128)(2,1)S(1)}, u32[]{:S(2)}, u32[]{:S(2)}) async-start(bf16[32,8,2,1,256]{4,2,1,3,0:T(2,128)(2,1)} %broadcast_in_dim.87), calls=%async_computation.1 | async-start | bytes 524288 | tf_op jit(solution)/shard_map/all_to_all | solution.py:18
  20.2 17.7 %all-to-all-start = ((bf16[8,8,2,1,256]{4,1,2,3,0:T(8,128)(2,1)}), bf16[8,8,2,1,256]{4,1,2,3,0:T(8,128)(2,1)S(1)}, u32[]{:S(2)}, u32[]{:S(2)}) async-start(bf16[8,8,2,1,256]{4,1,2,3,0:T(8,128)(2,1)} %broadcast_in_dim.84), calls=%async_computation | async-start | bytes 131072 | tf_op jit(solution)/shard_map/all_to_all | solution.py:18
  34.5 10.6 %copy-start.3 = (s32[1,1,4096]{2,1,0:T(1,128)S(1)}, s32[1,1,4096]{2,1,0:T(1,128)}, u32[]{:S(2)}) copy-start(s32[1,1,4096]{2,1,0:T(1,128)} %param.15) | copy-start | bytes 49156
  34.5 10.6 %copy-start.2 = (s32[1,1,4096]{2,1,0:T(1,128)S(1)}, s32[1,1,4096]{2,1,0:T(1,128)}, u32[]{:S(2)}) copy-start(s32[1,1,4096]{2,1,0:T(1,128)} %param.16) | copy-start | bytes 49156
  34.5 10.7 %copy-start.4 = (s32[1,1,4096]{2,1,0:T(1,128)S(1)}, s32[1,1,4096]{2,1,0:T(1,128)}, u32[]{:S(2)}) copy-start(s32[1,1,4096]{2,1,0:T(1,128)} %param.17) | copy-start | bytes 49156
  37.9 33.7 %all-to-all-start.2 = ((f32[8,1,32768]{2,1,0:T(1,128)}), f32[8,1,32768]{2,1,0:T(1,128)S(1)}, u32[]{:S(2)}, u32[]{:S(2)}) async-start(f32[8,1,32768]{2,1,0:T(1,128)} %reshape.195), calls=%async_computation.2 | async-start | bytes 2097152 | tf_op jit(solution)/shard_map/all_to_all | solution.py:18
  71.6 1.0 copy-start.1
  82.7 13.9 %all-to-all-start.3 = ((f32[8,8,2,1,256]{4,1,3,2,0:T(8,128)}), f32[8,8,2,1,256]{4,1,3,2,0:T(8,128)S(1)}, u32[]{:S(2)}, u32[]{:S(2)}) async-start(f32[8,8,2,1,256]{4,1,3,2,0:T(8,128)} %broadcast_in_dim.92), calls=%async_computation.3 | async-start | bytes 262144 | tf_op jit(solution)/shard_map/all_to_all | solution.py:18
  96.7 3.7 %collective-permute-start = (bf16[8,2,1,2048]{3,0,2,1:T(8,128)(2,1)S(1)}, bf16[8,2,1,2048]{3,0,2,1:T(8,128)(2,1)S(1)}, u32[]{:S(2)}, u32[]{:S(2)}) collective-permute-start(bf16[8,2,1,2048]{3,0,2,1:T(8,128)(2,1)S(1)} %convert_bitcast_fusion), channel_id=1, source_target_pairs={{0,8},{8,16},{16,24},{24,32},{32,40},{40,48},{48,56},{56,64},{64,7... | collective-permute-start | bytes 196616 | tf_op jit(solution)/shard_map/ppermute | solution.py:40
where the time goes:
time: 186 us; the launch traced here: 185 us
  local copies, waits for them, and re-layouts  49.3 us (27%)
  blocking collectives  40.8 us (22%)
  waiting for transfers between devices  37.1 us (20%)
  starting transfers between devices  34.4 us (18%)
  other arithmetic  14.6 us (8%)
  matrix products  7.39 us (4%)
    psum x5, blocking collectives, one_axis_at_a_time(): return functools.reduce(lax.psum, axes, x)  40.8 us
    all_to_all x4, waiting for transfers between devices, from_everyone(): lax.all_to_all(jnp.broadcast_to(x[None], (peers, *x.shape)), axis, 0, 0,...  36 us
    all_to_all x4, starting transfers between devices, from_everyone(): lax.all_to_all(jnp.broadcast_to(x[None], (peers, *x.shape)), axis, 0, 0,...  31.9 us
    gather x1, local copies, waits for them, and re-layouts, body(): jnp.take(pooled, second_idx, axis=1)  16.3 us
    gather x1, local copies, waits for them, and re-layouts, body(): jnp.take(pooled, first_idx, axis=1) - jnp.take(pooled, second_idx, axis=1)  16.3 us
    unnamed x13, local copies, waits for them, and re-layouts  7.21 us
    broadcast_in_dim x5, local copies, waits for them, and re-layouts, from_everyone(): jnp.broadcast_to(x[None], (peers, *x.shape))  5.16 us
    mul x1, other arithmetic, body(): half_sq = 0.5 * differ * differ  5.14 us
  transfers between devices with their start and end apart: 5, of which 4 were waited for; matrix products, arithmetic and copies ran while one was open for 8% of the time, Pallas kernels for 0%

commit v1 on v0

v1 whole, which is shorter than its diff:
```python
import functools

import jax
import jax.numpy as jnp
from jax import lax
from jax.experimental import pallas as pl
from jax.experimental.pallas import tpu as pltpu
from jax.sharding import Mesh
from jax.sharding import PartitionSpec as P

NBIN = 128
ROW = ("row_0", "row_1", "row_2")
COL = ("col_0", "col_1")
XY = ("row_0", "row_2")
ZC = ("row_1", "col_0", "col_1")
F32 = jnp.float32
BF16 = jnp.bfloat16


def exchange(copies, axis):
    return lax.all_to_all(copies, axis, 0, 0, tiled=True)


def copies_of(x, axis):
    return jnp.broadcast_to(x[None], (lax.axis_size(axis), *x.shape))


def nt_dot(a, b):
    return lax.dot_general(a, b, (((1,), (1,)), ((), ())), preferred_element_type=F32)


def call(kernel, out_shape, in_specs, flops=1, **kw):
    return pl.pallas_call(
        kernel,
        out_shape=out_shape,
        in_specs=in_specs,
        cost_estimate=pl.CostEstimate(flops=flops, bytes_accessed=1 << 20, transcendentals=0),
        **kw,
    )


VM = pl.BlockSpec(memory_space=pltpu.VMEM)
SM = pl.BlockSpec(memory_space=pltpu.SMEM)


def project_kernel(place, columns, right, keep, send):
    row, core = place[0], place[1]
    tiles = 2 * columns.shape[0]
    groups = right.shape[0] // 8
    lane = lax.broadcasted_iota(jnp.int32, (8, 128), 1)
    for half, out in ((core, keep), (1 - core, send)):
        def step(g, carry, half=half, out=out):
            base = (half * groups + g) * 4
            blocks = []
            low = []
            for n in range(4):
                slot = base + n
                tile = jnp.where(slot < row, slot, slot - row)
                first = tile < tiles // 2
                blocks.append(columns[jnp.where(first, tile, tiles - 1 - tile)])
                low.append(first)
            factor = right[pl.ds(base, 4)].reshape(256, 256)
            full = nt_dot(jnp.concatenate(blocks, axis=0), factor)
            parts = []
            for n in range(4):
                cols = full[16 * n : 16 * n + 16, 128 * (n // 2) : 128 * (n // 2) + 128]
                parts.append(jnp.where(low[n], cols[:8], cols[8:]))
            out[2 * g] = jnp.where(lane < 64, parts[0], parts[1])
            out[2 * g + 1] = jnp.where(lane < 64, parts[2], parts[3])
            return carry
        lax.fori_loop(0, groups, step, 0, unroll=4)


def coeff_kernel(place, ranks, sums, out):
    core = place[1]
    lane = lax.broadcasted_iota(jnp.int32, (8, 128), 1)
    left = lane < 64
    blocks = sums.shape[1]
    for i in range(blocks):
        slot = 2 * (core * blocks + i)
        total = sums[0, i] + sums[1, i] + sums[2, i] + sums[3, i]
        limit = jnp.where(left, ranks[0, slot], ranks[0, slot + 1] + 64)
        out[i] = jnp.where(lane < limit, total, 0.0).astype(BF16)


def on_diag_kernel(place, noise, diag, out):
    col = place[2]
    span = noise.shape[2]
    i_at = lax.broadcasted_iota(jnp.int32, (span, span), 0)
    j_at = lax.broadcasted_iota(jnp.int32, (span, span), 1)
    gap = j_at - i_at
    own = noise[col].astype(F32)
    acc = [own[:8], own[8:]]
    for piece in range(noise.shape[0]):
        below = gap < (col - piece) * span
        for h in range(2):
            tile = diag[h, :, piece * span : (piece + 1) * span]
            tile = jnp.where(below, tile.astype(F32), 0.0).astype(BF16)
            acc[h] = acc[h] + nt_dot(noise[piece], tile)[8 * h : 8 * h + 8]
    out[...] = jnp.concatenate(acc, axis=0)


def sample_kernel(place, mine, theirs, left, on_diag, out):
    row, core = place[0], place[1]
    blocks = mine.shape[0]
    last = 4 * blocks - 1
    lane = lax.broadcasted_iota(jnp.int32, (8, 128), 1)
    side = jnp.where(lane < 64, 0, 1)
    acc = on_diag[...]
    for half, coeffs in ((core, mine), (1 - core, theirs)):
        rows = []
        for i in range(blocks):
            slot = 2 * (half * blocks + i) + side
            c = coeffs[i].astype(F32)
            upper = jnp.where(slot < row, c, 0.0)
            lower = jnp.where((slot >= row) & (slot < last), c, 0.0)
            rows.append(jnp.concatenate([upper, lower], axis=0).astype(BF16))
        weights = jnp.concatenate(rows, axis=1)
        factor = left[pl.ds(half * blocks, blocks)].reshape(blocks * 128, left.shape[2])
        acc = acc + jnp.dot(weights, factor, preferred_element_type=F32)
    for n in range(out.shape[0]):
        out[n] = acc


def lookup(table, idx):
    low = idx & 127
    bit = [((idx >> (7 + n)) & 1) == 1 for n in range(5)]

    def tree(level, number):
        if level < 0:
            h, piece, half = number >> 4, (number >> 1) & 7, number & 1
            source = table[piece, 8 * h : 8 * h + 8, 128 * half : 128 * half + 128]
            return jnp.take_along_axis(source, low, axis=1, mode="promise_in_bounds")
        zero = tree(level - 1, number)
        one = tree(level - 1, number | (1 << level))
        return jnp.where(bit[level], one, zero)

    return tree(4, 0)


def own_kernel(table, first, partner, out):
    def step(n, carry):
        at = pl.multiple_of(n * 128, 128)
        a = jnp.broadcast_to(first[:, pl.ds(at, 128)], (8, 128))
        b = jnp.broadcast_to(partner[:, pl.ds(at, 128)], (8, 128))
        other = jnp.where(b >= 4096, lookup(table, b), 0.0)
        out[:, pl.ds(at, 128)] = lookup(table, a) - other
        return carry

    lax.fori_loop(0, first.shape[1] // 128, step, 0)


def bin_kernel(prev, partner, base, bins, out, table, pieces, onehot):
    table[...] = prev[...].astype(F32)
    bin_at = lax.broadcasted_iota(jnp.int32, (NBIN, 128), 0)

    def step(n, carry):
        at = pl.multiple_of(n * 128, 128)
        b = jnp.broadcast_to(partner[:, pl.ds(at, 128)], (8, 128))
        differ = base[:, pl.ds(at, 128)] - jnp.where(b < 4096, lookup(table, b), 0.0)
        value = 0.5 * differ * differ
        top = value.astype(BF16).astype(F32)
        rest = value - top
        mid = rest.astype(BF16).astype(F32)
        stack = jnp.concatenate([top, mid, rest - mid, jnp.ones_like(value)], axis=0)
        pieces[:, pl.ds(at, 128)] = stack.astype(BF16)
        ids = jnp.broadcast_to(bins[:, pl.ds(at, 128)], (NBIN, 128))
        onehot[:, pl.ds(at, 128)] = jnp.where(ids == bin_at, 1.0, 0.0).astype(BF16)
        return carry

    lax.fori_loop(0, partner.shape[1] // 128, step, 0)
    total = nt_dot(pieces[...], onehot[...])
    sums = (total[:8] + total[8:16]) + total[16:24]
    result = jnp.concatenate([sums, total[24:]], axis=0)
    for n in range(out.shape[0]):
        out[n] = result


def merge_kernel(parts, out):
    total = parts[0]
    for n in range(1, parts.shape[0]):
        total = total + parts[n]
    for n in range(out.shape[0]):
        out[n] = total


def finish_kernel(parts, out):
    total = parts[0]
    for n in range(1, parts.shape[0]):
        total = total + parts[n]
    out[...] = total[:8] / jnp.maximum(total[8:], 1.0)


def sds(shape, dtype):
    return jax.ShapeDtypeStruct(shape, dtype)


def body(
    noise, diag_factor, left_factor, right_factor, tile_ranks, pair_first, pair_partner, bin_ids
):
    row_at = lax.axis_index(ROW)
    col_at = lax.axis_index(COL)
    core_at = lax.axis_index("col_1")
    rows = lax.axis_size(ROW)
    cols = lax.axis_size(COL)
    place = jnp.stack([row_at, core_at, col_at]).astype(jnp.int32)
    span = noise.shape[3]
    swap = [(0, 1), (1, 0)]

    local = jnp.transpose(noise[:, :, 0], (1, 0, 2)).reshape(16, span)
    columns = exchange(copies_of(local, ROW), ROW)
    own_noise = exchange(copies_of(local, COL), COL)

    keep, send = call(
        project_kernel,
        (sds((16, 8, 128), F32), sds((16, 8, 128), F32)),
        [SM, VM, VM],
        flops=1 << 28,
        name="project",
    )(place, columns, right_factor[0])
    received = lax.ppermute(send, "col_1", swap)
    sums = exchange(copies_of(keep + received, "col_0"), "col_0")
    on_diag = call(on_diag_kernel, sds((16, span), F32), [SM, VM, VM], flops=1 << 28, name="ondiag")(
        place, own_noise, diag_factor[:, 0]
    )
    mine = call(coeff_kernel, sds((16, 8, 128), BF16), [SM, SM, VM], name="coeffs")(
        place, tile_ranks, sums
    )
    theirs = lax.ppermute(mine, "col_1", swap)
    copies = call(
        sample_kernel,
        sds((cols, 16, span), F32),
        [SM, VM, VM, VM, VM],
        flops=1 << 26,
        name="samples",
    )(place, mine, theirs, left_factor[0].reshape(32, 128, span), on_diag)
    samples = jnp.transpose(copies[0].reshape(2, 8, span), (1, 0, 2))[:, :, None]

    own_tiles = exchange(copies, COL)
    prev_tiles = lax.ppermute(
        own_tiles.astype(BF16), ROW, [(source, source + 1) for source in range(rows - 1)]
    )
    first, partner, bins = pair_first[0], pair_partner[0], bin_ids[0]
    pairs = first.shape[1]
    base = call(own_kernel, sds((8, pairs), F32), [VM, VM, VM], flops=1 << 26, name="own")(
        own_tiles, first, partner
    )
    partial = call(
        bin_kernel,
        sds((lax.axis_size(ZC), 16, NBIN), F32),
        [VM, VM, VM, VM],
        flops=1 << 26,
        scratch_shapes=[
            pltpu.VMEM((cols, 16, span), F32),
            pltpu.VMEM((32, pairs), BF16),
            pltpu.VMEM((NBIN, pairs), BF16),
        ],
        name="bins",
    )(prev_tiles, partner, base, bins)
    merged = call(merge_kernel, sds((lax.axis_size(XY), 16, NBIN), F32), [VM], name="merge")(
        exchange(partial, ZC)
    )
    variogram = call(finish_kernel, sds((8, NBIN), F32), [VM], name="finish")(exchange(merged, XY))
    return (samples, variogram)


def solution(mesh):
    split = Mesh(mesh.devices.reshape(4, 2, 4, 4, 2), ("row_0", "row_1", "row_2", "col_0", "col_1"))
    return jax.shard_map(
        body,
        mesh=split,
        in_specs=(
            P(None, None, ROW, COL),
            P(None, ROW, COL, None),
            P(ROW, None, None, COL),
            P(ROW, None, None, COL),
            P(ROW, None),
            P(ROW, COL, None),
            P(ROW, COL, None),
            P(ROW, COL, None),
        ),
        out_specs=(P(None, None, ROW, COL), P()),
        check_vma=False,
    )
```

time: 186 us -> 124 us (0.67)
  local copies, waits for them, and re-layouts: 49.3 us -> 6.61 us
  Pallas kernels: 0 us -> 26 us
  waiting for transfers between devices: 37.1 us -> 20.3 us
  other arithmetic: 14.6 us -> 1.46 us
  starting transfers between devices: 34.4 us -> 24.9 us
  matrix products: 7.39 us -> 0 us
  blocking collectives: 40.8 us -> 42.9 us
    all_to_all x0 -> x3, blocking collectives: none -> 42.9 us  [exchange(): return lax.all_to_all(copies, axis, 0, 0, tiled=True)]
    psum x5 -> x0, blocking collectives: 40.8 us -> none  [one_axis_at_a_time(): return functools.reduce(lax.psum, axes, x)]
    gather x3 -> x0, local copies, waits for them, and re-layouts: 33.1 us -> none  [the longest x1 16.3 us: body(): jnp.take(pooled, second_idx, axis=1)]
    pallas_call x0 -> x8, Pallas kernels: none -> 26 us  [the longest x1 6.26 us: body(): call(own_kernel, sds((8, pairs), F32), [VM, VM, VM], flops=1 << 26, name=...]
    all_to_all x4 -> x3, waiting for transfers between devices: 36 us -> 19.2 us  [exchange(): return lax.all_to_all(copies, axis, 0, 0, tiled=True)]
    all_to_all x4 -> x3, starting transfers between devices: 31.9 us -> 20.4 us  [exchange(): return lax.all_to_all(copies, axis, 0, 0, tiled=True)]
    dot_general x5 -> x0, matrix products: 7.39 us -> none  [the longest x2 2.48 us: body(): jnp.dot(block_sq, onehot, precision=lax.Precision.HIGHEST, preferred_elem...]
    mul x1 -> x0, other arithmetic: 5.14 us -> none  [body(): half_sq = 0.5 * differ * differ]
  transfers between devices with their start and end apart: 5 -> 6, of which waited for: 4 -> 4; matrix products, arithmetic and copies ran while one was open for 8% -> 2% of each run, Pallas kernels for 0% -> 9%
where the time goes in v1:
time: 124 us; the launch traced here: 123 us
  blocking collectives  42.9 us (35%)
  Pallas kernels  26 us (21%)
  starting transfers between devices  24.9 us (20%)
  waiting for transfers between devices  20.3 us (16%)
  local copies, waits for them, and re-layouts  6.61 us (5%)
  other arithmetic  1.46 us (1%)
    all_to_all x3, blocking collectives, exchange(): return lax.all_to_all(copies, axis, 0, 0, tiled=True)  42.9 us
    all_to_all x3, starting transfers between devices, exchange(): return lax.all_to_all(copies, axis, 0, 0, tiled=True)  20.4 us
    all_to_all x3, waiting for transfers between devices, exchange(): return lax.all_to_all(copies, axis, 0, 0, tiled=True)  19.2 us
    pallas_call x1, Pallas kernels, body(): call(own_kernel, sds((8, pairs), F32), [VM, VM, VM], flops=1 << 26, name=...  6.26 us
    pallas_call x1, Pallas kernels, body(): call(bin_kernel, sds((lax.axis_size(ZC), 16, NBIN), F32), [VM, VM, VM, VM...  5.94 us
    unnamed x13, local copies, waits for them, and re-layouts  3.9 us
    pallas_call x1, Pallas kernels, body(): call(project_kernel, (sds((16, 8, 128), F32), sds((16, 8, 128), F32)), [S...  3.47 us
    pallas_call x1, Pallas kernels, body(): call(on_diag_kernel, sds((16, span), F32), [SM, VM, VM], flops=1 << 28, n...  2.9 us
  transfers between devices with their start and end apart: 6, of which 4 were waited for; matrix products, arithmetic and copies ran while one was open for 2% of the time, Pallas kernels for 9%

profile of v1, /device:TPU:1, one launch (start us, length us, event | category | flops | bytes accessed | tf_op | source)
XLA Modules:
  0.0 122.9 jit_solution(13075811954891156205)
XLA Ops:
  0.6 0.7 copy.16
  1.3 0.7 broadcast_in_dim.22
  2.0 9.2 %all-to-all-start = ((bf16[32,16,256]{2,1,0:T(8,128)(2,1)}), bf16[32,16,256]{2,1,0:T(8,128)(2,1)S(1)}, u32[]{:S(2)}, u32[]{:S(2)}) async-start(bf16[32,16,256]{2,1,0:T(8,128)(2,1)} %broadcast_in_dim.22), calls=%async_computation | async-start | bytes 524288 | tf_op jit(solution)/shard_map/all_to_all | solution.py:21
  11.3 0.6 pad_add_fusion.place
  11.9 7.4 %all-to-all-done.columns = bf16[32,16,256]{2,1,0:T(8,128)(2,1)S(1)} async-done(((bf16[32,16,256]{2,1,0:T(8,128)(2,1)}), bf16[32,16,256]{2,1,0:T(8,128)(2,1)S(1)}, u32[]{:S(2)}, u32[]{:S(2)}) %all-to-all-start) | async-done | bytes 262176 | tf_op jit(solution)/shard_map/all_to_all | solution.py:21
  19.3 0.0 copy-start.1
  19.3 0.7 copy-done.1
  20.0 3.5 %project.1 = (f32[16,8,128]{2,1,0:T(8,128)}, f32[16,8,128]{2,1,0:T(8,128)}) custom-call(s32[3]{0:T(128)} %pad_add_fusion.place, bf16[32,16,256]{2,1,0:T(8,128)(2,1)} %copy-done.1, bf16[64,64,256]{2,1,0:T(8,128)(2,1)} %bitcast.21), custom_call_target="tpu_custom_call" | custom-call | flops 268435456 | bytes 1048576 | tf_op jit(solution)/shard_map/project/pallas_call | solution.py:214
  23.4 2.1 %collective-permute-start = (f32[16,8,128]{2,1,0:T(8,128)}, f32[16,8,128]{2,1,0:T(8,128)S(1)}, u32[]{:S(2)}, u32[]{:S(2)}) collective-permute-start(f32[16,8,128]{2,1,0:T(8,128)} %get-tuple-element.5), channel_id=1, source_target_pairs={{0,1},{1,0},{2,3},{3,2},{4,5},{5,4},{6,7},{7,6},{8,9},{9,8},{10,11... | collective-permute-start | bytes 196616 | tf_op jit(solution)/shard_map/ppermute | solution.py:221
  25.5 1.1 collective-permute-done
  26.6 0.9 add.15
  27.5 16.6 %all_to_all.30.sums = f32[4,16,8,128]{3,2,1,0:T(8,128)} all-to-all(f32[4,16,8,128]{3,2,1,0:T(8,128)S(1)} %broadcast_in_dim.23), channel_id=1, replica_groups=mesh['row_0'=4,'row_1'=2,'row_2'=4,'col_0'=4,'col_1'=2] {'col_0'}, dimensions={0} | all-to-all | bytes 524288 | tf_op jit(solution)/shard_map/all_to_all | solution.py:21
  44.1 0.6 broadcast_in_dim.24
  44.7 5.7 %all-to-all-start.2 = ((bf16[8,16,256]{2,1,0:T(8,128)(2,1)}), bf16[8,16,256]{2,1,0:T(8,128)(2,1)S(1)}, u32[]{:S(2)}, u32[]{:S(2)}) async-start(bf16[8,16,256]{2,1,0:T(8,128)(2,1)} %broadcast_in_dim.24), calls=%async_computation.2 | async-start | bytes 131072 | tf_op jit(solution)/shard_map/all_to_all | solution.py:21
  50.4 1.6 %coeffs.1.mine = bf16[16,8,128]{2,1,0:T(8,128)(2,1)} custom-call(s32[3]{0:T(128)} %pad_add_fusion.place, s32[1,64]{1,0:T(1,128)} %ranks.1, f32[4,16,8,128]{3,2,1,0:T(8,128)} %all_to_all.30.sums), custom_call_target="tpu_custom_call" | custom-call | flops 1 | bytes 1048576 | tf_op jit(solution)/shard_map/coeffs/pallas_call | solution.py:226
  52.0 0.1 collective-permute-start.1
  52.1 5.8 %all-to-all-done.2.noise = bf16[8,16,256]{2,1,0:T(8,128)(2,1)S(1)} async-done(((bf16[8,16,256]{2,1,0:T(8,128)(2,1)}), bf16[8,16,256]{2,1,0:T(8,128)(2,1)S(1)}, u32[]{:S(2)}, u32[]{:S(2)}) %all-to-all-start.2) | async-done | bytes 65568 | tf_op jit(solution)/shard_map/all_to_all | solution.py:21
  57.9 0.0 copy-start.3
  57.9 0.6 copy-done.3
  58.5 2.9 %ondiag.1.on_diag = f32[16,256]{1,0:T(8,128)} custom-call(s32[3]{0:T(128)} %pad_add_fusion.place, bf16[8,16,256]{2,1,0:T(8,128)(2,1)} %copy-done.3, bf16[2,256,2048]{2,1,0:T(8,128)(2,1)} %bitcast.23), custom_call_target="tpu_custom_call" | custom-call | flops 268435456 | bytes 1048576 | tf_op jit(solution)/shard_map/ondiag/pallas_call | solution.py:223
  61.4 0.0 collective-permute-done.1.theirs
  61.4 0.0 copy-start.5
  61.4 0.6 copy-done.5
  62.0 2.7 %samples.1 = f32[8,16,256]{2,1,0:T(8,128)} custom-call(s32[3]{0:T(128)} %pad_add_fusion.place, bf16[16,8,128]{2,1,0:T(8,128)(2,1)} %coeffs.1.mine, bf16[16,8,128]{2,1,0:T(8,128)(2,1)} %copy-done.5, bf16[32,128,256]{2,1,0:T(8,128)(2,1)} %bitcast.22, f32[16,256]{1,0:T(8,128)} %ondiag.1.on_diag), custom_call_target="tpu_custom_call" | custom-call | flops 67108864 | bytes 1048576 | tf_op jit(solution)/shard_map/samples/pallas_call | solution.py:230
  64.7 12.1 %all_to_all.31.table = f32[8,16,256]{2,1,0:T(8,128)S(1)} all-to-all(f32[8,16,256]{2,1,0:T(8,128)} %samples.1), channel_id=1, replica_groups=mesh['row_0'=4,'row_1'=2,'row_2'=4,'col_0'=4,'col_1'=2] {'col_0','col_1'}, dimensions={0} | all-to-all | bytes 262144 | tf_op jit(solution)/shard_map/all_to_all | solution.py:21
  76.9 0.0 copy-start
  76.9 2.4 %collective-permute-start.2 = (bf16[8,16,256]{2,1,0:T(8,128)(2,1)S(1)}, bf16[8,16,256]{2,1,0:T(8,128)(2,1)S(1)}, u32[]{:S(2)}, u32[]{:S(2)}) collective-permute-start(bf16[8,16,256]{2,1,0:T(8,128)(2,1)S(1)} %convert_element_type.3), channel_id=1, source_target_pairs={{0,8},{8,16},{16,24},{24,32},{32,40},{40,48},{48,56},{56,64},{64,7... | collective-permute-start | bytes 196616 | tf_op jit(solution)/shard_map/ppermute | solution.py:240
  79.3 0.0 copy-done
  79.3 6.3 %own.1.base = f32[8,4096]{1,0:T(8,128)} custom-call(f32[8,16,256]{2,1,0:T(8,128)} %copy-done, s32[1,4096]{1,0:T(1,128)} %bitcast.29, s32[1,4096]{1,0:T(1,128)} %bitcast.26), custom_call_target="tpu_custom_call" | custom-call | flops 67108864 | bytes 1048576 | tf_op jit(solution)/shard_map/own/pallas_call | solution.py:245
  85.6 0.0 collective-permute-done.2.prev
  85.6 0.0 copy-start.4
  85.6 0.6 copy-done.4
  86.2 5.9 %bins.1 = f32[16,16,128]{2,1,0:T(8,128)} custom-call(bf16[8,16,256]{2,1,0:T(8,128)(2,1)} %copy-done.4, s32[1,4096]{1,0:T(1,128)} %bitcast.27, f32[8,4096]{1,0:T(8,128)} %own.1.base, s32[1,4096]{1,0:T(1,128)} %bitcast.30), custom_call_target="tpu_custom_call" | custom-call | flops 67108864 | bytes 1048576 | tf_op jit(solution)/shard_map/bins/pallas_call | solution.py:248
  92.1 14.2 %all_to_all.32.parts = f32[16,16,128]{2,1,0:T(8,128)} all-to-all(f32[16,16,128]{2,1,0:T(8,128)} %bins.1), channel_id=1, replica_groups=mesh['row_0'=4,'row_1'=2,'row_2'=4,'col_0'=4,'col_1'=2] {'row_1','col_0'..., dimensions={0} | all-to-all | bytes 262144 | tf_op jit(solution)/shard_map/all_to_all | solution.py:21
  106.3 1.6 %merge.1 = f32[16,16,128]{2,1,0:T(8,128)} custom-call(f32[16,16,128]{2,1,0:T(8,128)} %all_to_all.32.parts), custom_call_target="tpu_custom_call" | custom-call | flops 1 | bytes 1048576 | tf_op jit(solution)/shard_map/merge/pallas_call | solution.py:260
  107.9 5.5 %all-to-all-start.5 = ((f32[16,16,128]{2,1,0:T(8,128)}), f32[16,16,128]{2,1,0:T(8,128)S(1)}, u32[]{:S(2)}, u32[]{:S(2)}) async-start(f32[16,16,128]{2,1,0:T(8,128)} %merge.1), calls=%async_computation.5 | async-start | bytes 262144 | tf_op jit(solution)/shard_map/all_to_all | solution.py:21
  113.4 0.7 slice_bitcast_fusion
  114.1 0.6 broadcast_in_dim.25
  114.7 6.0 %all-to-all-done.5.parts = f32[16,16,128]{2,1,0:T(8,128)S(1)} async-done(((f32[16,16,128]{2,1,0:T(8,128)}), f32[16,16,128]{2,1,0:T(8,128)S(1)}, u32[]{:S(2)}, u32[]{:S(2)}) %all-to-all-start.5) | async-done | bytes 131104 | tf_op jit(solution)/shard_map/all_to_all | solution.py:21
  120.7 0.0 copy-start.2
  120.7 0.7 copy-done.2
  121.4 1.5 %finish.1 = f32[8,128]{1,0:T(8,128)} custom-call(f32[16,16,128]{2,1,0:T(8,128)} %copy-done.2), custom_call_target="tpu_custom_call" | custom-call | flops 1 | bytes 1048576 | tf_op jit(solution)/shard_map/finish/pallas_call | solution.py:263
  (3 shorter events, 0.0 us)
Async XLA Ops:
  2.0 17.2 %all-to-all-start = ((bf16[32,16,256]{2,1,0:T(8,128)(2,1)}), bf16[32,16,256]{2,1,0:T(8,128)(2,1)S(1)}, u32[]{:S(2)}, u32[]{:S(2)}) async-start(bf16[32,16,256]{2,1,0:T(8,128)(2,1)} %broadcast_in_dim.22), calls=%async_computation | async-start | bytes 524288 | tf_op jit(solution)/shard_map/all_to_all | solution.py:21
  19.3 0.7 copy-start.1
  23.4 3.2 %collective-permute-start = (f32[16,8,128]{2,1,0:T(8,128)}, f32[16,8,128]{2,1,0:T(8,128)S(1)}, u32[]{:S(2)}, u32[]{:S(2)}) collective-permute-start(f32[16,8,128]{2,1,0:T(8,128)} %get-tuple-element.5), channel_id=1, source_target_pairs={{0,1},{1,0},{2,3},{3,2},{4,5},{5,4},{6,7},{7,6},{8,9},{9,8},{10,11... | collective-permute-start | bytes 196616 | tf_op jit(solution)/shard_map/ppermute | solution.py:221
  44.7 13.2 %all-to-all-start.2 = ((bf16[8,16,256]{2,1,0:T(8,128)(2,1)}), bf16[8,16,256]{2,1,0:T(8,128)(2,1)S(1)}, u32[]{:S(2)}, u32[]{:S(2)}) async-start(bf16[8,16,256]{2,1,0:T(8,128)(2,1)} %broadcast_in_dim.24), calls=%async_computation.2 | async-start | bytes 131072 | tf_op jit(solution)/shard_map/all_to_all | solution.py:21
  52.0 9.5 %collective-permute-start.1 = (bf16[16,8,128]{2,1,0:T(8,128)(2,1)}, bf16[16,8,128]{2,1,0:T(8,128)(2,1)S(1)}, u32[]{:S(2)}, u32[]{:S(2)}) collective-permute-start(bf16[16,8,128]{2,1,0:T(8,128)(2,1)} %coeffs.1.mine), channel_id=1, source_target_pairs={{0,1},{1,0},{2,3},{3,2},{4,5},{5,4},{6,7},{7,6},{8,9},{9,8},{10,11... | collective-permute-start | bytes 98312 | tf_op jit(solution)/shard_map/ppermute | solution.py:229
  57.9 0.6 copy-start.3
  61.4 0.6 copy-start.5
  76.9 2.4 %copy-start = (f32[8,16,256]{2,1,0:T(8,128)}, f32[8,16,256]{2,1,0:T(8,128)S(1)}, u32[]{:S(2)}) copy-start(f32[8,16,256]{2,1,0:T(8,128)S(1)} %all_to_all.31.table) | copy-start | bytes 393220
  76.9 8.7 %collective-permute-start.2 = (bf16[8,16,256]{2,1,0:T(8,128)(2,1)S(1)}, bf16[8,16,256]{2,1,0:T(8,128)(2,1)S(1)}, u32[]{:S(2)}, u32[]{:S(2)}) collective-permute-start(bf16[8,16,256]{2,1,0:T(8,128)(2,1)S(1)} %convert_element_type.3), channel_id=1, source_target_pairs={{0,8},{8,16},{16,24},{24,32},{32,40},{40,48},{48,56},{56,64},{64,7... | collective-permute-start | bytes 196616 | tf_op jit(solution)/shard_map/ppermute | solution.py:240
  85.6 0.6 copy-start.4
  107.9 12.8 %all-to-all-start.5 = ((f32[16,16,128]{2,1,0:T(8,128)}), f32[16,16,128]{2,1,0:T(8,128)S(1)}, u32[]{:S(2)}, u32[]{:S(2)}) async-start(f32[16,16,128]{2,1,0:T(8,128)} %merge.1), calls=%async_computation.5 | async-start | bytes 262144 | tf_op jit(solution)/shard_map/all_to_all | solution.py:21
  120.7 0.7 copy-start.2

commit v2 on v1

--- a/solution.py
+++ b/solution.py
@@ -1,5 +1,3 @@
-import functools
-
 import jax
 import jax.numpy as jnp
 from jax import lax
@@ -29,18 +27,57 @@
     return lax.dot_general(a, b, (((1,), (1,)), ((), ())), preferred_element_type=F32)
 
 
+HB = pl.BlockSpec(memory_space=pltpu.HBM)
+VM = pl.BlockSpec(memory_space=pltpu.VMEM)
+SM = pl.BlockSpec(memory_space=pltpu.SMEM)
+
+
 def call(kernel, out_shape, in_specs, flops=1, **kw):
-    return pl.pallas_call(
+    run = pl.pallas_call(
         kernel,
         out_shape=out_shape,
         in_specs=in_specs,
         cost_estimate=pl.CostEstimate(flops=flops, bytes_accessed=1 << 20, transcendentals=0),
+        compiler_params=pltpu.CompilerParams(vmem_limit_bytes=16 << 20),
         **kw,
     )
 
-
-VM = pl.BlockSpec(memory_space=pltpu.VMEM)
-SM = pl.BlockSpec(memory_space=pltpu.SMEM)
+    def held(*args):
+        return run(
+            *(
+                a if spec is SM else pltpu.with_memory_space_constraint(a, spec.memory_space)
+                for a, spec in zip(args, in_specs)
+            )
+        )
+
+    return held
+
+
+def stage_kernel(source, out, sem):
+    copy = pltpu.make_async_copy(source, out, sem)
+    copy.start()
+    copy.wait()
+
+
+def spread_kernel(place, keep, received, noise, other, out):
+    blocks = keep.shape[0]
+    first = place[1] == 0
+    own = noise[...].astype(F32)
+    far = other[...].astype(F32)
+    pieces = (jnp.where(first, own, far).astype(BF16), jnp.where(first, far, own).astype(BF16))
+    copies = out.shape[0]
+    for i in range(0, blocks, 2):
+        total = jnp.concatenate([keep[i] + received[i], keep[i + 1] + received[i + 1]], axis=0)
+        top = total.astype(BF16)
+        rest = (total - top.astype(F32)).astype(BF16)
+        for n in range(copies):
+            out[n, 8 * i : 8 * i + 16] = top
+            out[n, 8 * (blocks + i) : 8 * (blocks + i) + 16] = rest
+    for core in range(2):
+        for side in range(2):
+            at = 16 * (blocks + 2 * core + side)
+            for n in range(copies):
+                out[n, at : at + 16] = pieces[core][:, 128 * side : 128 * side + 128]
 
 
 def project_kernel(place, columns, right, keep, send):
@@ -68,36 +105,47 @@
             out[2 * g] = jnp.where(lane < 64, parts[0], parts[1])
             out[2 * g + 1] = jnp.where(lane < 64, parts[2], parts[3])
             return carry
+
         lax.fori_loop(0, groups, step, 0, unroll=4)
 
 
-def coeff_kernel(place, ranks, sums, out):
+def coeff_kernel(place, ranks, parts, out):
     core = place[1]
     lane = lax.broadcasted_iota(jnp.int32, (8, 128), 1)
     left = lane < 64
-    blocks = sums.shape[1]
-    for i in range(blocks):
-        slot = 2 * (core * blocks + i)
-        total = sums[0, i] + sums[1, i] + sums[2, i] + sums[3, i]
-        limit = jnp.where(left, ranks[0, slot], ranks[0, slot + 1] + 64)
-        out[i] = jnp.where(lane < limit, total, 0.0).astype(BF16)
-
-
-def on_diag_kernel(place, noise, diag, out):
+    blocks = out.shape[0]
+    for i in range(0, blocks, 2):
+        total = jnp.zeros((16, 128), F32)
+        for n in range(parts.shape[0]):
+            top = parts[n, 8 * i : 8 * i + 16].astype(F32)
+            total = total + (top + parts[n, 8 * (blocks + i) : 8 * (blocks + i) + 16].astype(F32))
+        for k in range(2):
+            slot = 2 * (core * blocks + i + k)
+            limit = jnp.where(left, ranks[0, slot], ranks[0, slot + 1] + 64)
+            out[i + k] = jnp.where(lane < limit, total[8 * k : 8 * k + 8], 0.0).astype(BF16)
+
+
+def on_diag_kernel(place, parts, diag, out):
     col = place[2]
-    span = noise.shape[2]
+    span = diag.shape[1]
+    pieces = []
+    own = jnp.zeros((16, span), F32)
+    for n in range(parts.shape[0]):
+        for core in range(2):
+            at = 256 + 32 * core
+            piece = jnp.concatenate([parts[n, at : at + 16], parts[n, at + 16 : at + 32]], axis=1)
+            piece = piece.astype(F32)
+            number = 2 * n + core
+            own = jnp.where(col == number, piece, own)
+            pieces.append(jnp.where(number < col, piece, 0.0).astype(BF16))
+    before = jnp.concatenate(pieces, axis=1)
     i_at = lax.broadcasted_iota(jnp.int32, (span, span), 0)
     j_at = lax.broadcasted_iota(jnp.int32, (span, span), 1)
-    gap = j_at - i_at
-    own = noise[col].astype(F32)
-    acc = [own[:8], own[8:]]
-    for piece in range(noise.shape[0]):
-        below = gap < (col - piece) * span
-        for h in range(2):
-            tile = diag[h, :, piece * span : (piece + 1) * span]
-            tile = jnp.where(below, tile.astype(F32), 0.0).astype(BF16)
-            acc[h] = acc[h] + nt_dot(noise[piece], tile)[8 * h : 8 * h + 8]
-    out[...] = jnp.concatenate(acc, axis=0)
+    at = pl.multiple_of(col * span, span)
+    for h in range(2):
+        corner = jnp.where(j_at < i_at, diag[h, :, pl.ds(at, span)].astype(F32), 0.0).astype(BF16)
+        total = nt_dot(before, diag[h]) + nt_dot(own.astype(BF16), corner) + own
+        out[8 * h : 8 * h + 8] = total[8 * h : 8 * h + 8]
 
 
 def sample_kernel(place, mine, theirs, left, on_diag, out):
@@ -147,7 +195,7 @@
         out[:, pl.ds(at, 128)] = lookup(table, a) - other
         return carry
 
-    lax.fori_loop(0, first.shape[1] // 128, step, 0)
+    lax.fori_loop(0, first.shape[1] // 128, step, 0, unroll=4)
 
 
 def bin_kernel(prev, partner, base, bins, out, table, pieces, onehot):
@@ -168,7 +216,7 @@
         onehot[:, pl.ds(at, 128)] = jnp.where(ids == bin_at, 1.0, 0.0).astype(BF16)
         return carry
 
-    lax.fori_loop(0, partner.shape[1] // 128, step, 0)
+    lax.fori_loop(0, partner.shape[1] // 128, step, 0, unroll=4)
     total = nt_dot(pieces[...], onehot[...])
     sums = (total[:8] + total[8:16]) + total[16:24]
     result = jnp.concatenate([sums, total[24:]], axis=0)
@@ -191,8 +239,8 @@
     out[...] = total[:8] / jnp.maximum(total[8:], 1.0)
 
 
-def sds(shape, dtype):
-    return jax.ShapeDtypeStruct(shape, dtype)
+def vmem(shape, dtype):
+    return pltpu.VMEM(shape, dtype)
 
 
 def body(
@@ -209,27 +257,37 @@
 
     local = jnp.transpose(noise[:, :, 0], (1, 0, 2)).reshape(16, span)
     columns = exchange(copies_of(local, ROW), ROW)
-    own_noise = exchange(copies_of(local, COL), COL)
+    other_noise = lax.ppermute(local, "col_1", swap)
+    right = call(
+        stage_kernel,
+        vmem(right_factor.shape[1:], BF16),
+        [HB],
+        scratch_shapes=[pltpu.SemaphoreType.DMA(())],
+        name="stage",
+    )(right_factor[0])
 
     keep, send = call(
         project_kernel,
-        (sds((16, 8, 128), F32), sds((16, 8, 128), F32)),
+        (vmem((16, 8, 128), F32), vmem((16, 8, 128), F32)),
         [SM, VM, VM],
         flops=1 << 28,
         name="project",
-    )(place, columns, right_factor[0])
+    )(place, columns, right)
     received = lax.ppermute(send, "col_1", swap)
-    sums = exchange(copies_of(keep + received, "col_0"), "col_0")
-    on_diag = call(on_diag_kernel, sds((16, span), F32), [SM, VM, VM], flops=1 << 28, name="ondiag")(
-        place, own_noise, diag_factor[:, 0]
-    )
-    mine = call(coeff_kernel, sds((16, 8, 128), BF16), [SM, SM, VM], name="coeffs")(
+    spread = call(
+        spread_kernel, vmem((4, 320, 128), BF16), [SM, VM, VM, VM, VM], name="spread"
+    )(place, keep, received, local, other_noise)
+    sums = exchange(spread, "col_0")
+    mine = call(coeff_kernel, vmem((16, 8, 128), BF16), [SM, SM, VM], name="coeffs")(
         place, tile_ranks, sums
     )
     theirs = lax.ppermute(mine, "col_1", swap)
+    on_diag = call(
+        on_diag_kernel, vmem((16, span), F32), [SM, VM, VM], flops=1 << 28, name="ondiag"
+    )(place, sums, diag_factor[:, 0])
     copies = call(
         sample_kernel,
-        sds((cols, 16, span), F32),
+        vmem((cols, 16, span), F32),
         [SM, VM, VM, VM, VM],
         flops=1 << 26,
         name="samples",
@@ -242,12 +300,12 @@
     )
     first, partner, bins = pair_first[0], pair_partner[0], bin_ids[0]
     pairs = first.shape[1]
-    base = call(own_kernel, sds((8, pairs), F32), [VM, VM, VM], flops=1 << 26, name="own")(
+    base = call(own_kernel, vmem((8, pairs), F32), [VM, VM, VM], flops=1 << 26, name="own")(
         own_tiles, first, partner
     )
     partial = call(
         bin_kernel,
-        sds((lax.axis_size(ZC), 16, NBIN), F32),
+        vmem((lax.axis_size(ZC), 16, NBIN), F32),
         [VM, VM, VM, VM],
         flops=1 << 26,
         scratch_shapes=[
@@ -257,10 +315,10 @@
         ],
         name="bins",
     )(prev_tiles, partner, base, bins)
-    merged = call(merge_kernel, sds((lax.axis_size(XY), 16, NBIN), F32), [VM], name="merge")(
+    merged = call(merge_kernel, vmem((lax.axis_size(XY), 16, NBIN), F32), [VM], name="merge")(
         exchange(partial, ZC)
     )
-    variogram = call(finish_kernel, sds((8, NBIN), F32), [VM], name="finish")(exchange(merged, XY))
+    variogram = call(finish_kernel, jax.ShapeDtypeStruct((8, NBIN), F32), [VM], name="finish")(exchange(merged, XY))
     return (samples, variogram)
 
 

time: 124 us -> 95.1 us (0.77)
  Pallas kernels: 26 us -> 13.2 us
  waiting for transfers between devices: 20.3 us -> 14 us
  starting transfers between devices: 24.9 us -> 19.8 us
  local copies, waits for them, and re-layouts: 6.61 us -> 2.13 us
  blocking collectives: 42.9 us -> 44.6 us
  other arithmetic: 1.46 us -> 0.09 us
    pallas_call x8 -> x10, Pallas kernels: 26 us -> 13.2 us  [held(): run(*(a if spec is SM else pltpu.with_memory_space_constraint(a, spec.mem...]
    all_to_all x3 -> x2, starting transfers between devices: 20.4 us -> 12.9 us  [exchange(): return lax.all_to_all(copies, axis, 0, 0, tiled=True)]
    all_to_all x3 -> x2, waiting for transfers between devices: 19.2 us -> 13 us  [exchange(): return lax.all_to_all(copies, axis, 0, 0, tiled=True)]
    unnamed x13 -> x12, local copies, waits for them, and re-layouts: 3.9 us -> 0.08 us
    ppermute x1, starting transfers between devices: 0.11 us -> 2.16 us  [body(): theirs = lax.ppermute(mine, 'col_1', swap)]
    all_to_all x3, blocking collectives: 42.9 us -> 44.6 us  [exchange(): return lax.all_to_all(copies, axis, 0, 0, tiled=True)]
  transfers between devices with their start and end apart: 6 -> 6, of which waited for: 4 -> 3; matrix products, arithmetic and copies ran while one was open for 2% -> 1% of each run, Pallas kernels for 9% -> 6%
where the time goes in v2:
time: 95.1 us; the launch traced here: 94.7 us
  blocking collectives  44.6 us (47%)
  starting transfers between devices  19.8 us (21%)
  waiting for transfers between devices  14 us (15%)
  Pallas kernels  13.2 us (14%)
  local copies, waits for them, and re-layouts  2.13 us (2%)
    all_to_all x3, blocking collectives, exchange(): return lax.all_to_all(copies, axis, 0, 0, tiled=True)  44.6 us
    pallas_call x10, Pallas kernels, held(): run(*(a if spec is SM else pltpu.with_memory_space_constraint(a, spec.mem...  13.2 us
    all_to_all x2, waiting for transfers between devices, exchange(): return lax.all_to_all(copies, axis, 0, 0, tiled=True)  13 us
    all_to_all x2, starting transfers between devices, exchange(): return lax.all_to_all(copies, axis, 0, 0, tiled=True)  12.9 us
    ppermute x1, starting transfers between devices, body(): lax.ppermute(own_tiles.astype(BF16), ROW, [(source, source + 1) for sourc...  2.46 us
    ppermute x1, starting transfers between devices, body(): received = lax.ppermute(send, 'col_1', swap)  2.17 us
    ppermute x1, starting transfers between devices, body(): theirs = lax.ppermute(mine, 'col_1', swap)  2.16 us
  transfers between devices with their start and end apart: 6, of which 3 were waited for; matrix products, arithmetic and copies ran while one was open for 1% of the time, Pallas kernels for 6%

profile of v2, /device:TPU:1, one launch (start us, length us, event | category | flops | bytes accessed | tf_op | source)
XLA Modules:
  0.0 94.7 jit_solution(9506310224539286907)
XLA Ops:
  0.6 0.7 copy.15
  1.3 0.7 broadcast_in_dim.11
  2.1 9.2 %all-to-all-start = ((bf16[32,16,256]{2,1,0:T(8,128)(2,1)}), bf16[32,16,256]{2,1,0:T(8,128)(2,1)S(1)}, u32[]{:S(2)}, u32[]{:S(2)}) async-start(bf16[32,16,256]{2,1,0:T(8,128)(2,1)} %broadcast_in_dim.11), calls=%async_computation | async-start | bytes 524288 | tf_op jit(solution)/shard_map/all_to_all | solution.py:19
  11.3 1.6 %stage.1.right = bf16[64,64,256]{2,1,0:T(8,128)(2,1)S(1)} custom-call(bf16[64,64,256]{2,1,0:T(8,128)(2,1)} %bitcast.29), custom_call_target="tpu_custom_call" | custom-call | flops 1 | bytes 1048576 | tf_op jit(solution)/shard_map/stage/pallas_call | solution.py:46
  12.9 0.0 copy-start.5
  12.9 0.1 pad_add_fusion.place
  13.0 6.3 %all-to-all-done.columns = bf16[32,16,256]{2,1,0:T(8,128)(2,1)S(1)} async-done(((bf16[32,16,256]{2,1,0:T(8,128)(2,1)}), bf16[32,16,256]{2,1,0:T(8,128)(2,1)S(1)}, u32[]{:S(2)}, u32[]{:S(2)}) %all-to-all-start) | async-done | bytes 262176 | tf_op jit(solution)/shard_map/all_to_all | solution.py:19
  19.3 0.0 copy-start.1
  19.3 1.7 %project.1 = (f32[16,8,128]{2,1,0:T(8,128)S(1)}, f32[16,8,128]{2,1,0:T(8,128)S(1)}) custom-call(s32[3]{0:T(128)S(1)} %pad_add_fusion.place, bf16[32,16,256]{2,1,0:T(8,128)(2,1)S(1)} %all-to-all-done.columns, bf16[64,64,256]{2,1,0:T(8,128)(2,1)S(1)} %stage.1.right), custom_call_target="tpu_custom_call" | custom-call | flops 268435456 | bytes 1048576 | tf_op jit(solution)/shard_map/project/pallas_call | solution.py:46
  21.0 0.0 copy-start
  21.0 2.2 %collective-permute-start = (f32[16,8,128]{2,1,0:T(8,128)S(1)}, f32[16,8,128]{2,1,0:T(8,128)S(1)}, u32[]{:S(2)}, u32[]{:S(2)}) collective-permute-start(f32[16,8,128]{2,1,0:T(8,128)S(1)} %get-tuple-element.5), channel_id=1, source_target_pairs={{0,1},{1,0},{2,3},{3,2},{4,5},{5,4},{6,7},{7,6},{8,9},{9,8},{10,11... | collective-permute-start | bytes 196616 | tf_op jit(solution)/shard_map/ppermute | solution.py:276
  23.2 0.1 collective-permute-start.1
  23.3 1.1 %collective-permute-done.1.other = bf16[16,256]{1,0:T(8,128)(2,1)S(1)} collective-permute-done((bf16[16,256]{1,0:T(8,128)(2,1)S(1)}, bf16[16,256]{1,0:T(8,128)(2,1)S(1)}, u32[]{:S(2)}, u32[]{:S(2)}) %collective-permute-start.1) | collective-permute-done | bytes 8224 | tf_op jit(solution)/shard_map/ppermute | solution.py:260
  24.3 0.0 collective-permute-done.received
  24.3 0.6 spread.1
  24.9 18.3 %all_to_all.25.parts = bf16[4,320,128]{2,1,0:T(8,128)(2,1)S(1)} all-to-all(bf16[4,320,128]{2,1,0:T(8,128)(2,1)S(1)} %spread.1), channel_id=1, replica_groups=mesh['row_0'=4,'row_1'=2,'row_2'=4,'col_0'=4,'col_1'=2] {'col_0'}, dimensions={0} | all-to-all | bytes 655360 | tf_op jit(solution)/shard_map/all_to_all | solution.py:19
  43.2 0.0 copy-done.5
  43.2 0.6 coeffs.1.mine
  43.8 2.2 %collective-permute-start.2 = (bf16[16,8,128]{2,1,0:T(8,128)(2,1)S(1)}, bf16[16,8,128]{2,1,0:T(8,128)(2,1)S(1)}, u32[]{:S(2)}, u32[]{:S(2)}) collective-permute-start(bf16[16,8,128]{2,1,0:T(8,128)(2,1)S(1)} %coeffs.1.mine), channel_id=1, source_target_pairs={{0,1},{1,0},{2,3},{3,2},{4,5},{5,4},{6,7},{7,6},{8,9},{9,8},{10,11... | collective-permute-start | bytes 98312 | tf_op jit(solution)/shard_map/ppermute | solution.py:284
  46.0 0.0 copy-done.1
  46.0 0.0 copy-start.2
  46.0 0.0 copy-start.3
  46.0 1.2 %ondiag.1.on_diag = f32[16,256]{1,0:T(8,128)S(1)} custom-call(s32[3]{0:T(128)S(1)} %pad_add_fusion.place, bf16[4,320,128]{2,1,0:T(8,128)(2,1)S(1)} %all_to_all.25.parts, bf16[2,256,2048]{2,1,0:T(8,128)(2,1)S(1)} %bitcast.21), custom_call_target="tpu_custom_call" | custom-call | flops 268435456 | bytes 1048576 | tf_op jit(solution)/shard_map/ondiag/pallas_call | solution.py:46
  47.2 0.1 copy-start.4
  47.3 0.0 collective-permute-done.2.theirs
  47.3 0.0 copy-done
  47.3 0.9 samples.1
  48.3 10.5 %all_to_all.26.table = f32[8,16,256]{2,1,0:T(8,128)S(1)} all-to-all(f32[8,16,256]{2,1,0:T(8,128)S(1)} %samples.1), channel_id=1, replica_groups=mesh['row_0'=4,'row_1'=2,'row_2'=4,'col_0'=4,'col_1'=2] {'col_0','col_1'}, dimensions={0} | all-to-all | bytes 262144 | tf_op jit(solution)/shard_map/all_to_all | solution.py:19
  58.7 2.5 %collective-permute-start.3 = (bf16[8,16,256]{2,1,0:T(8,128)(2,1)S(1)}, bf16[8,16,256]{2,1,0:T(8,128)(2,1)S(1)}, u32[]{:S(2)}, u32[]{:S(2)}) collective-permute-start(bf16[8,16,256]{2,1,0:T(8,128)(2,1)S(1)} %convert_element_type.3), channel_id=1, source_target_pairs={{0,8},{8,16},{16,24},{24,32},{32,40},{40,48},{48,56},{56,64},{64,7... | collective-permute-start | bytes 196616 | tf_op jit(solution)/shard_map/ppermute | solution.py:298
  61.2 0.0 copy-done.2
  61.2 0.0 copy-done.3
  61.2 3.0 %own.1.base = f32[8,4096]{1,0:T(8,128)S(1)} custom-call(f32[8,16,256]{2,1,0:T(8,128)S(1)} %all_to_all.26.table, s32[1,4096]{1,0:T(1,128)S(1)} %bitcast.27, s32[1,4096]{1,0:T(1,128)S(1)} %bitcast.25), custom_call_target="tpu_custom_call" | custom-call | flops 67108864 | bytes 1048576 | tf_op jit(solution)/shard_map/own/pallas_call | solution.py:46
  64.2 0.0 collective-permute-done.3.prev
  64.2 0.0 copy-done.4
  64.2 2.4 %bins.1 = f32[16,16,128]{2,1,0:T(8,128)S(1)} custom-call(bf16[8,16,256]{2,1,0:T(8,128)(2,1)S(1)} %collective-permute-done.3.prev, s32[1,4096]{1,0:T(1,128)S(1)} %bitcast.26, f32[8,4096]{1,0:T(8,128)S(1)} %own.1.base, s32[1,4096]{1,0:T(1,128)S(1)} %bitcast.28), custom_call_target="tpu_custom_call" | custom-call | flops 67108864 | bytes 1048576 | tf_op jit(solution)/shard_map/bins/pallas_call | solution.py:46
  66.6 15.8 %all_to_all.27.parts = f32[16,16,128]{2,1,0:T(8,128)S(1)} all-to-all(f32[16,16,128]{2,1,0:T(8,128)S(1)} %bins.1), channel_id=1, replica_groups=mesh['row_0'=4,'row_1'=2,'row_2'=4,'col_0'=4,'col_1'=2] {'row_1','col_0'..., dimensions={0} | all-to-all | bytes 262144 | tf_op jit(solution)/shard_map/all_to_all | solution.py:19
  82.4 0.7 merge.1
  83.1 3.7 %all-to-all-start.4 = ((f32[16,16,128]{2,1,0:T(8,128)}), f32[16,16,128]{2,1,0:T(8,128)S(1)}, u32[]{:S(2)}, u32[]{:S(2)}) async-start(f32[16,16,128]{2,1,0:T(8,128)} %merge.1), calls=%async_computation.4 | async-start | bytes 262144 | tf_op jit(solution)/shard_map/all_to_all | solution.py:19
  86.8 0.6 broadcast_in_dim.12
  87.4 6.7 %all-to-all-done.4.parts = f32[16,16,128]{2,1,0:T(8,128)S(1)} async-done(((f32[16,16,128]{2,1,0:T(8,128)}), f32[16,16,128]{2,1,0:T(8,128)S(1)}, u32[]{:S(2)}, u32[]{:S(2)}) %all-to-all-start.4) | async-done | bytes 131104 | tf_op jit(solution)/shard_map/all_to_all | solution.py:19
  94.1 0.6 finish.1
  (3 shorter events, 0.0 us)
Async XLA Ops:
  2.1 17.2 %all-to-all-start = ((bf16[32,16,256]{2,1,0:T(8,128)(2,1)}), bf16[32,16,256]{2,1,0:T(8,128)(2,1)S(1)}, u32[]{:S(2)}, u32[]{:S(2)}) async-start(bf16[32,16,256]{2,1,0:T(8,128)(2,1)} %broadcast_in_dim.11), calls=%async_computation | async-start | bytes 524288 | tf_op jit(solution)/shard_map/all_to_all | solution.py:19
  12.9 30.4 %copy-start.5 = (s32[1,64]{1,0:T(1,128)S(1)}, s32[1,64]{1,0:T(1,128)}, u32[]{:S(2)}) copy-start(s32[1,64]{1,0:T(1,128)} %ranks.1) | copy-start | bytes 772
  19.3 26.7 %copy-start.1 = (bf16[2,1,256,2048]{3,2,1,0:T(8,128)(2,1)S(1)}, bf16[2,1,256,2048]{3,2,1,0:T(8,128)(2,1)}, u32[]{:S(2)}) copy-start(bf16[2,1,256,2048]{3,2,1,0:T(8,128)(2,1)} %param.9) | copy-start | bytes 6291460
  21.0 26.3 %copy-start = (bf16[1,64,64,256]{3,2,1,0:T(8,128)(2,1)S(1)}, bf16[1,64,64,256]{3,2,1,0:T(8,128)(2,1)}, u32[]{:S(2)}) copy-start(bf16[1,64,64,256]{3,2,1,0:T(8,128)(2,1)} %param.10) | copy-start | bytes 6291460
  21.0 3.4 %collective-permute-start = (f32[16,8,128]{2,1,0:T(8,128)S(1)}, f32[16,8,128]{2,1,0:T(8,128)S(1)}, u32[]{:S(2)}, u32[]{:S(2)}) collective-permute-start(f32[16,8,128]{2,1,0:T(8,128)S(1)} %get-tuple-element.5), channel_id=1, source_target_pairs={{0,1},{1,0},{2,3},{3,2},{4,5},{5,4},{6,7},{7,6},{8,9},{9,8},{10,11... | collective-permute-start | bytes 196616 | tf_op jit(solution)/shard_map/ppermute | solution.py:276
  23.2 1.2 %collective-permute-start.1 = (bf16[16,256]{1,0:T(8,128)(2,1)S(1)}, bf16[16,256]{1,0:T(8,128)(2,1)S(1)}, u32[]{:S(2)}, u32[]{:S(2)}) collective-permute-start(bf16[16,256]{1,0:T(8,128)(2,1)S(1)} %bitcast.23), channel_id=1, source_target_pairs={{0,1},{1,0},{2,3},{3,2},{4,5},{5,4},{6,7},{7,6},{8,9},{9,8},{10,11... | collective-permute-start | bytes 24584 | tf_op jit(solution)/shard_map/ppermute | solution.py:260
  43.8 3.5 %collective-permute-start.2 = (bf16[16,8,128]{2,1,0:T(8,128)(2,1)S(1)}, bf16[16,8,128]{2,1,0:T(8,128)(2,1)S(1)}, u32[]{:S(2)}, u32[]{:S(2)}) collective-permute-start(bf16[16,8,128]{2,1,0:T(8,128)(2,1)S(1)} %coeffs.1.mine), channel_id=1, source_target_pairs={{0,1},{1,0},{2,3},{3,2},{4,5},{5,4},{6,7},{7,6},{8,9},{9,8},{10,11... | collective-permute-start | bytes 98312 | tf_op jit(solution)/shard_map/ppermute | solution.py:284
  46.0 15.2 %copy-start.2 = (s32[1,1,4096]{2,1,0:T(1,128)S(1)}, s32[1,1,4096]{2,1,0:T(1,128)}, u32[]{:S(2)}) copy-start(s32[1,1,4096]{2,1,0:T(1,128)} %param.14) | copy-start | bytes 49156
  46.0 15.2 %copy-start.3 = (s32[1,1,4096]{2,1,0:T(1,128)S(1)}, s32[1,1,4096]{2,1,0:T(1,128)}, u32[]{:S(2)}) copy-start(s32[1,1,4096]{2,1,0:T(1,128)} %param.13) | copy-start | bytes 49156
  47.2 17.0 %copy-start.4 = (s32[1,1,4096]{2,1,0:T(1,128)S(1)}, s32[1,1,4096]{2,1,0:T(1,128)}, u32[]{:S(2)}) copy-start(s32[1,1,4096]{2,1,0:T(1,128)} %param.15) | copy-start | bytes 49156
  58.7 5.5 %collective-permute-start.3 = (bf16[8,16,256]{2,1,0:T(8,128)(2,1)S(1)}, bf16[8,16,256]{2,1,0:T(8,128)(2,1)S(1)}, u32[]{:S(2)}, u32[]{:S(2)}) collective-permute-start(bf16[8,16,256]{2,1,0:T(8,128)(2,1)S(1)} %convert_element_type.3), channel_id=1, source_target_pairs={{0,8},{8,16},{16,24},{24,32},{32,40},{40,48},{48,56},{56,64},{64,7... | collective-permute-start | bytes 196616 | tf_op jit(solution)/shard_map/ppermute | solution.py:298
  83.1 11.0 %all-to-all-start.4 = ((f32[16,16,128]{2,1,0:T(8,128)}), f32[16,16,128]{2,1,0:T(8,128)S(1)}, u32[]{:S(2)}, u32[]{:S(2)}) async-start(f32[16,16,128]{2,1,0:T(8,128)} %merge.1), calls=%async_computation.4 | async-start | bytes 262144 | tf_op jit(solution)/shard_map/all_to_all | solution.py:19

commit v3 on v2

--- a/solution.py
+++ b/solution.py
@@ -17,10 +17,6 @@
 
 def exchange(copies, axis):
     return lax.all_to_all(copies, axis, 0, 0, tiled=True)
-
-
-def copies_of(x, axis):
-    return jnp.broadcast_to(x[None], (lax.axis_size(axis), *x.shape))
 
 
 def nt_dot(a, b):
@@ -53,15 +49,41 @@
     return held
 
 
+def copies_kernel(noise, local, out):
+    rows = [noise[s, h].astype(F32) for h in range(2) for s in range(8)]
+    mine = jnp.concatenate(rows, axis=0).astype(BF16)
+    local[...] = mine
+    for n in range(out.shape[0]):
+        out[n] = mine
+
+
+def prepare_kernel(bins, ranks, onehot, keep):
+    core = lax.axis_index("col_1")
+    lane = lax.broadcasted_iota(jnp.int32, (1, 128), 1)
+    for i in range(keep.shape[0]):
+        slot = 2 * (core * keep.shape[0] + i)
+        limit = jnp.where(lane < 64, ranks[0, slot], ranks[0, slot + 1] + 64)
+        keep[i] = jnp.where(lane < limit, 1.0, 0.0)
+    bin_at = lax.broadcasted_iota(jnp.int32, (NBIN, 128), 0)
+
+    def step(n, carry):
+        at = pl.multiple_of(n * 128, 128)
+        ids = jnp.broadcast_to(bins[:, pl.ds(at, 128)], (NBIN, 128))
+        onehot[:, pl.ds(at, 128)] = jnp.where(ids == bin_at, 1.0, 0.0).astype(BF16)
+        return carry
+
+    lax.fori_loop(0, bins.shape[1] // 128, step, 0, unroll=4)
+
+
 def stage_kernel(source, out, sem):
     copy = pltpu.make_async_copy(source, out, sem)
     copy.start()
     copy.wait()
 
 
-def spread_kernel(place, keep, received, noise, other, out):
+def spread_kernel(keep, received, noise, other, out):
     blocks = keep.shape[0]
-    first = place[1] == 0
+    first = lax.axis_index("col_1") == 0
     own = noise[...].astype(F32)
     far = other[...].astype(F32)
     pieces = (jnp.where(first, own, far).astype(BF16), jnp.where(first, far, own).astype(BF16))
@@ -80,8 +102,8 @@
                 out[n, at : at + 16] = pieces[core][:, 128 * side : 128 * side + 128]
 
 
-def project_kernel(place, columns, right, keep, send):
-    row, core = place[0], place[1]
+def project_kernel(columns, right, keep, send):
+    row, core = lax.axis_index(ROW), lax.axis_index("col_1")
     tiles = 2 * columns.shape[0]
     groups = right.shape[0] // 8
     lane = lax.broadcasted_iota(jnp.int32, (8, 128), 1)
@@ -109,10 +131,7 @@
         lax.fori_loop(0, groups, step, 0, unroll=4)
 
 
-def coeff_kernel(place, ranks, parts, out):
-    core = place[1]
-    lane = lax.broadcasted_iota(jnp.int32, (8, 128), 1)
-    left = lane < 64
+def coeff_kernel(allowed, parts, out):
     blocks = out.shape[0]
     for i in range(0, blocks, 2):
         total = jnp.zeros((16, 128), F32)
@@ -120,13 +139,12 @@
             top = parts[n, 8 * i : 8 * i + 16].astype(F32)
             total = total + (top + parts[n, 8 * (blocks + i) : 8 * (blocks + i) + 16].astype(F32))
         for k in range(2):
-            slot = 2 * (core * blocks + i + k)
-            limit = jnp.where(left, ranks[0, slot], ranks[0, slot + 1] + 64)
-            out[i + k] = jnp.where(lane < limit, total[8 * k : 8 * k + 8], 0.0).astype(BF16)
-
-
-def on_diag_kernel(place, parts, diag, out):
-    col = place[2]
+            inside = jnp.broadcast_to(allowed[i + k], (8, 128)) > 0.5
+            out[i + k] = jnp.where(inside, total[8 * k : 8 * k + 8], 0.0).astype(BF16)
+
+
+def on_diag_kernel(parts, diag, out):
+    col = lax.axis_index(COL)
     span = diag.shape[1]
     pieces = []
     own = jnp.zeros((16, span), F32)
@@ -148,8 +166,8 @@
         out[8 * h : 8 * h + 8] = total[8 * h : 8 * h + 8]
 
 
-def sample_kernel(place, mine, theirs, left, on_diag, out):
-    row, core = place[0], place[1]
+def sample_kernel(mine, theirs, left, on_diag, out):
+    row, core = lax.axis_index(ROW), lax.axis_index("col_1")
     blocks = mine.shape[0]
     last = 4 * blocks - 1
     lane = lax.broadcasted_iota(jnp.int32, (8, 128), 1)
@@ -198,9 +216,14 @@
     lax.fori_loop(0, first.shape[1] // 128, step, 0, unroll=4)
 
 
-def bin_kernel(prev, partner, base, bins, out, table, pieces, onehot):
+def put_rows(out, rows):
+    for n in range(out.shape[0]):
+        for i in range(9):
+            out[n, :, 128 * i : 128 * i + 128] = rows[i]
+
+
+def bin_kernel(prev, partner, base, onehot, out, table, pieces):
     table[...] = prev[...].astype(F32)
-    bin_at = lax.broadcasted_iota(jnp.int32, (NBIN, 128), 0)
 
     def step(n, carry):
         at = pl.multiple_of(n * 128, 128)
@@ -212,31 +235,28 @@
         mid = rest.astype(BF16).astype(F32)
         stack = jnp.concatenate([top, mid, rest - mid, jnp.ones_like(value)], axis=0)
         pieces[:, pl.ds(at, 128)] = stack.astype(BF16)
-        ids = jnp.broadcast_to(bins[:, pl.ds(at, 128)], (NBIN, 128))
-        onehot[:, pl.ds(at, 128)] = jnp.where(ids == bin_at, 1.0, 0.0).astype(BF16)
         return carry
 
     lax.fori_loop(0, partner.shape[1] // 128, step, 0, unroll=4)
     total = nt_dot(pieces[...], onehot[...])
     sums = (total[:8] + total[8:16]) + total[16:24]
-    result = jnp.concatenate([sums, total[24:]], axis=0)
-    for n in range(out.shape[0]):
-        out[n] = result
-
-
-def merge_kernel(parts, out):
+    put_rows(out, [sums[i : i + 1] for i in range(8)] + [total[24:25]])
+
+
+def added(parts):
     total = parts[0]
     for n in range(1, parts.shape[0]):
         total = total + parts[n]
-    for n in range(out.shape[0]):
-        out[n] = total
+    return [total[:, 128 * i : 128 * i + 128] for i in range(9)]
+
+
+def merge_kernel(parts, out):
+    put_rows(out, added(parts))
 
 
 def finish_kernel(parts, out):
-    total = parts[0]
-    for n in range(1, parts.shape[0]):
-        total = total + parts[n]
-    out[...] = total[:8] / jnp.maximum(total[8:], 1.0)
+    rows = added(parts)
+    out[...] = jnp.concatenate(rows[:8], axis=0) / jnp.maximum(rows[8], 1.0)
 
 
 def vmem(shape, dtype):
@@ -246,17 +266,27 @@
 def body(
     noise, diag_factor, left_factor, right_factor, tile_ranks, pair_first, pair_partner, bin_ids
 ):
-    row_at = lax.axis_index(ROW)
-    col_at = lax.axis_index(COL)
-    core_at = lax.axis_index("col_1")
     rows = lax.axis_size(ROW)
     cols = lax.axis_size(COL)
-    place = jnp.stack([row_at, core_at, col_at]).astype(jnp.int32)
     span = noise.shape[3]
     swap = [(0, 1), (1, 0)]
-
-    local = jnp.transpose(noise[:, :, 0], (1, 0, 2)).reshape(16, span)
-    columns = exchange(copies_of(local, ROW), ROW)
+    first, partner, bins = pair_first[0], pair_partner[0], bin_ids[0]
+    pairs = first.shape[1]
+
+    local, spread_noise = call(
+        copies_kernel,
+        (vmem((16, span), BF16), vmem((rows, 16, span), BF16)),
+        [VM],
+        name="copies",
+    )(noise)
+    columns = exchange(spread_noise, ROW)
+    onehot, allowed = call(
+        prepare_kernel,
+        (vmem((NBIN, pairs), BF16), vmem((16, 1, 128), F32)),
+        [VM, SM],
+        flops=1 << 20,
+        name="prepare",
+    )(bins, tile_ranks)
     other_noise = lax.ppermute(local, "col_1", swap)
     right = call(
         stage_kernel,
@@ -269,53 +299,50 @@
     keep, send = call(
         project_kernel,
         (vmem((16, 8, 128), F32), vmem((16, 8, 128), F32)),
-        [SM, VM, VM],
+        [VM, VM],
         flops=1 << 28,
         name="project",
-    )(place, columns, right)
+    )(columns, right)
     received = lax.ppermute(send, "col_1", swap)
     spread = call(
-        spread_kernel, vmem((4, 320, 128), BF16), [SM, VM, VM, VM, VM], name="spread"
-    )(place, keep, received, local, other_noise)
+        spread_kernel, vmem((4, 320, 128), BF16), [VM, VM, VM, VM], name="spread"
+    )(keep, received, local, other_noise)
     sums = exchange(spread, "col_0")
-    mine = call(coeff_kernel, vmem((16, 8, 128), BF16), [SM, SM, VM], name="coeffs")(
-        place, tile_ranks, sums
+    mine = call(coeff_kernel, vmem((16, 8, 128), BF16), [VM, VM], name="coeffs")(
+        allowed, sums
     )
     theirs = lax.ppermute(mine, "col_1", swap)
     on_diag = call(
-        on_diag_kernel, vmem((16, span), F32), [SM, VM, VM], flops=1 << 28, name="ondiag"
-    )(place, sums, diag_factor[:, 0])
+        on_diag_kernel, vmem((16, span), F32), [VM, VM], flops=1 << 28, name="ondiag"
+    )(sums, diag_factor[:, 0])
     copies = call(
         sample_kernel,
         vmem((cols, 16, span), F32),
-        [SM, VM, VM, VM, VM],
+        [VM, VM, VM, VM],
         flops=1 << 26,
         name="samples",
-    )(place, mine, theirs, left_factor[0].reshape(32, 128, span), on_diag)
+    )(mine, theirs, left_factor[0].reshape(32, 128, span), on_diag)
     samples = jnp.transpose(copies[0].reshape(2, 8, span), (1, 0, 2))[:, :, None]
 
     own_tiles = exchange(copies, COL)
     prev_tiles = lax.ppermute(
         own_tiles.astype(BF16), ROW, [(source, source + 1) for source in range(rows - 1)]
     )
-    first, partner, bins = pair_first[0], pair_partner[0], bin_ids[0]
-    pairs = first.shape[1]
     base = call(own_kernel, vmem((8, pairs), F32), [VM, VM, VM], flops=1 << 26, name="own")(
         own_tiles, first, partner
     )
     partial = call(
         bin_kernel,
-        vmem((lax.axis_size(ZC), 16, NBIN), F32),
+        vmem((lax.axis_size(ZC), 1, 9 * NBIN), F32),
         [VM, VM, VM, VM],
         flops=1 << 26,
         scratch_shapes=[
             pltpu.VMEM((cols, 16, span), F32),
             pltpu.VMEM((32, pairs), BF16),
-            pltpu.VMEM((NBIN, pairs), BF16),
         ],
         name="bins",
-    )(prev_tiles, partner, base, bins)
-    merged = call(merge_kernel, vmem((lax.axis_size(XY), 16, NBIN), F32), [VM], name="merge")(
+    )(prev_tiles, partner, base, onehot)
+    merged = call(merge_kernel, vmem((lax.axis_size(XY), 1, 9 * NBIN), F32), [VM], name="merge")(
         exchange(partial, ZC)
     )
     variogram = call(finish_kernel, jax.ShapeDtypeStruct((8, NBIN), F32), [VM], name="finish")(exchange(merged, XY))

time: 95.1 us -> 93.4 us (0.982)
  blocking collectives: 44.6 us -> 25.6 us
  waiting for transfers between devices: 14 us -> 23.2 us
  starting transfers between devices: 19.8 us -> 26.6 us
  local copies, waits for them, and re-layouts: 2.13 us -> 3.8 us
    all_to_all x3 -> x2, blocking collectives: 44.6 us -> 25.6 us  [exchange(): return lax.all_to_all(copies, axis, 0, 0, tiled=True)]
    all_to_all x2 -> x3, waiting for transfers between devices: 13 us -> 22.1 us  [exchange(): return lax.all_to_all(copies, axis, 0, 0, tiled=True)]
    all_to_all x2 -> x3, starting transfers between devices: 12.9 us -> 20 us  [exchange(): return lax.all_to_all(copies, axis, 0, 0, tiled=True)]
    unnamed x12 -> x13, local copies, waits for them, and re-layouts: 0.08 us -> 3.16 us
    pallas_call x10 -> x12, Pallas kernels: 13.2 us -> 12.9 us  [held(): run(*(a if spec is SM else pltpu.with_memory_space_constraint(a, spec.mem...]
  transfers between devices with their start and end apart: 6 -> 7, of which waited for: 3 -> 4; matrix products, arithmetic and copies ran while one was open for 1% -> 1% of each run, Pallas kernels for 6% -> 7%
where the time goes in v3:
time: 93.4 us; the launch traced here: 92.9 us
  starting transfers between devices  26.6 us (28%)
  blocking collectives  25.6 us (27%)
  waiting for transfers between devices  23.2 us (25%)
  Pallas kernels  12.9 us (14%)
  local copies, waits for them, and re-layouts  3.8 us (4%)
    all_to_all x2, blocking collectives, exchange(): return lax.all_to_all(copies, axis, 0, 0, tiled=True)  25.6 us
    all_to_all x3, waiting for transfers between devices, exchange(): return lax.all_to_all(copies, axis, 0, 0, tiled=True)  22.1 us
    all_to_all x3, starting transfers between devices, exchange(): return lax.all_to_all(copies, axis, 0, 0, tiled=True)  20 us
    pallas_call x12, Pallas kernels, held(): run(*(a if spec is SM else pltpu.with_memory_space_constraint(a, spec.mem...  12.9 us
    unnamed x13, local copies, waits for them, and re-layouts  3.16 us
    ppermute x1, starting transfers between devices, body(): lax.ppermute(own_tiles.astype(BF16), ROW, [(source, source + 1) for sourc...  2.46 us
    ppermute x1, starting transfers between devices, body(): received = lax.ppermute(send, 'col_1', swap)  2.17 us
  transfers between devices with their start and end apart: 7, of which 4 were waited for; matrix products, arithmetic and copies ran while one was open for 1% of the time, Pallas kernels for 7%

profile of v3, /device:TPU:1, one launch (start us, length us, event | category | flops | bytes accessed | tf_op | source)
XLA Modules:
  0.0 92.9 jit_solution(8331378669011259227)
XLA Ops:
  0.6 0.7 copy.10.noise
  1.3 0.7 copies.1
  2.1 9.2 %all-to-all-start = ((bf16[32,16,256]{2,1,0:T(8,128)(2,1)}), bf16[32,16,256]{2,1,0:T(8,128)(2,1)S(1)}, u32[]{:S(2)}, u32[]{:S(2)}) async-start(bf16[32,16,256]{2,1,0:T(8,128)(2,1)} %get-tuple-element.9), calls=%async_computation | async-start | bytes 524288 | tf_op jit(solution)/shard_map/all_to_all | solution.py:19
  11.3 1.6 %stage.1.right = bf16[64,64,256]{2,1,0:T(8,128)(2,1)S(1)} custom-call(bf16[64,64,256]{2,1,0:T(8,128)(2,1)} %bitcast.17), custom_call_target="tpu_custom_call" | custom-call | flops 1 | bytes 1048576 | tf_op jit(solution)/shard_map/stage/pallas_call | solution.py:42
  12.9 0.0 copy-start.4
  12.9 0.0 copy-start.5
  12.9 6.4 %all-to-all-done.columns = bf16[32,16,256]{2,1,0:T(8,128)(2,1)S(1)} async-done(((bf16[32,16,256]{2,1,0:T(8,128)(2,1)}), bf16[32,16,256]{2,1,0:T(8,128)(2,1)S(1)}, u32[]{:S(2)}, u32[]{:S(2)}) %all-to-all-start) | async-done | bytes 262176 | tf_op jit(solution)/shard_map/all_to_all | solution.py:19
  19.3 1.1 %project.1 = (f32[16,8,128]{2,1,0:T(8,128)S(1)}, f32[16,8,128]{2,1,0:T(8,128)S(1)}) custom-call(bf16[32,16,256]{2,1,0:T(8,128)(2,1)S(1)} %all-to-all-done.columns, bf16[64,64,256]{2,1,0:T(8,128)(2,1)S(1)} %stage.1.right), custom_call_target="tpu_custom_call" | custom-call | flops 268435456 | bytes 1048576 | tf_op jit(solution)/shard_map/project/pallas_call | solution.py:42
  20.4 2.2 %collective-permute-start = (f32[16,8,128]{2,1,0:T(8,128)S(1)}, f32[16,8,128]{2,1,0:T(8,128)S(1)}, u32[]{:S(2)}, u32[]{:S(2)}) collective-permute-start(f32[16,8,128]{2,1,0:T(8,128)S(1)} %get-tuple-element.11), channel_id=1, source_target_pairs={{0,1},{1,0},{2,3},{3,2},{4,5},{5,4},{6,7},{7,6},{8,9},{9,8},{10,11... | collective-permute-start | bytes 196616 | tf_op jit(solution)/shard_map/ppermute | solution.py:306
  22.6 0.1 collective-permute-start.1
  22.7 1.1 %collective-permute-done.1.other = bf16[16,256]{1,0:T(8,128)(2,1)S(1)} collective-permute-done((bf16[16,256]{1,0:T(8,128)(2,1)S(1)}, bf16[16,256]{1,0:T(8,128)(2,1)S(1)}, u32[]{:S(2)}, u32[]{:S(2)}) %collective-permute-start.1) | collective-permute-done | bytes 8224 | tf_op jit(solution)/shard_map/ppermute | solution.py:290
  23.8 0.0 collective-permute-done.received
  23.8 0.8 spread.1
  24.5 7.3 %all-to-all-start.1 = ((bf16[4,320,128]{2,1,0:T(8,128)(2,1)}), bf16[4,320,128]{2,1,0:T(8,128)(2,1)S(1)}, u32[]{:S(2)}, u32[]{:S(2)}) async-start(bf16[4,320,128]{2,1,0:T(8,128)(2,1)} %spread.1), calls=%async_computation.1 | async-start | bytes 655360 | tf_op jit(solution)/shard_map/all_to_all | solution.py:19
  31.8 0.0 copy-done.4
  31.8 0.0 copy-done.5
  31.8 0.9 prepare.1
  32.7 9.9 %all-to-all-done.1.parts = bf16[4,320,128]{2,1,0:T(8,128)(2,1)S(1)} async-done(((bf16[4,320,128]{2,1,0:T(8,128)(2,1)}), bf16[4,320,128]{2,1,0:T(8,128)(2,1)S(1)}, u32[]{:S(2)}, u32[]{:S(2)}) %all-to-all-start.1) | async-done | bytes 327712 | tf_op jit(solution)/shard_map/all_to_all | solution.py:19
  42.7 1.9 %collective-permute-start.2 = (bf16[16,8,128]{2,1,0:T(8,128)(2,1)S(1)}, bf16[16,8,128]{2,1,0:T(8,128)(2,1)S(1)}, u32[]{:S(2)}, u32[]{:S(2)}) collective-permute-start(bf16[16,8,128]{2,1,0:T(8,128)(2,1)S(1)} %coeffs.1.mine), channel_id=1, source_target_pairs={{0,1},{1,0},{2,3},{3,2},{4,5},{5,4},{6,7},{7,6},{8,9},{9,8},{10,11... | collective-permute-start | bytes 98312 | tf_op jit(solution)/shard_map/ppermute | solution.py:314
  44.5 0.0 copy-start
  44.5 1.6 %copy-done = bf16[2,1,256,2048]{3,2,1,0:T(8,128)(2,1)S(1)} copy-done((bf16[2,1,256,2048]{3,2,1,0:T(8,128)(2,1)S(1)}, bf16[2,1,256,2048]{3,2,1,0:T(8,128)(2,1)}, u32[]{:S(2)}) %copy-start) | copy-done | bytes 2097176
  46.1 0.0 copy-start.1
  46.1 0.0 copy-start.2
  46.1 0.0 copy-start.3
  46.1 0.7 ondiag.1.on_diag
  46.8 0.0 collective-permute-done.2.theirs
  46.9 0.8 copy-done.1
  47.7 0.4 samples.1
  48.1 11.4 %all_to_all.25.table = f32[8,16,256]{2,1,0:T(8,128)S(1)} all-to-all(f32[8,16,256]{2,1,0:T(8,128)S(1)} %samples.1), channel_id=1, replica_groups=mesh['row_0'=4,'row_1'=2,'row_2'=4,'col_0'=4,'col_1'=2] {'col_0','col_1'}, dimensions={0} | all-to-all | bytes 262144 | tf_op jit(solution)/shard_map/all_to_all | solution.py:19
  59.5 2.5 %collective-permute-start.3 = (bf16[8,16,256]{2,1,0:T(8,128)(2,1)S(1)}, bf16[8,16,256]{2,1,0:T(8,128)(2,1)S(1)}, u32[]{:S(2)}, u32[]{:S(2)}) collective-permute-start(bf16[8,16,256]{2,1,0:T(8,128)(2,1)S(1)} %convert_element_type.3), channel_id=1, source_target_pairs={{0,8},{8,16},{16,24},{24,32},{32,40},{40,48},{48,56},{56,64},{64,7... | collective-permute-start | bytes 196616 | tf_op jit(solution)/shard_map/ppermute | solution.py:328
  62.0 0.0 copy-done.2
  62.0 0.0 copy-done.3
  62.0 3.0 %own.1.base = f32[8,4096]{1,0:T(8,128)S(1)} custom-call(f32[8,16,256]{2,1,0:T(8,128)S(1)} %all_to_all.25.table, s32[1,4096]{1,0:T(1,128)S(1)} %bitcast.15, s32[1,4096]{1,0:T(1,128)S(1)} %bitcast.13), custom_call_target="tpu_custom_call" | custom-call | flops 67108864 | bytes 1048576 | tf_op jit(solution)/shard_map/own/pallas_call | solution.py:42
  65.0 0.0 collective-permute-done.3.prev
  65.0 2.3 %bins.1 = f32[16,1,1152]{2,1,0:T(1,128)S(1)} custom-call(bf16[8,16,256]{2,1,0:T(8,128)(2,1)S(1)} %collective-permute-done.3.prev, s32[1,4096]{1,0:T(1,128)S(1)} %bitcast.14, f32[8,4096]{1,0:T(8,128)S(1)} %own.1.base, bf16[128,4096]{1,0:T(8,128)(2,1)S(1)} %get-tuple-element.13.onehot), custom_call_target="tpu_custom_call" | custom-call | flops 67108864 | bytes 1048576 | tf_op jit(solution)/shard_map/bins/pallas_call | solution.py:42
  67.4 14.2 %all_to_all.26.parts = f32[16,1,1152]{2,1,0:T(1,128)S(1)} all-to-all(f32[16,1,1152]{2,1,0:T(1,128)S(1)} %bins.1), channel_id=1, replica_groups=mesh['row_0'=4,'row_1'=2,'row_2'=4,'col_0'=4,'col_1'=2] {'row_1','col_0'..., dimensions={0} | all-to-all | bytes 147456 | tf_op jit(solution)/shard_map/all_to_all | solution.py:19
  81.6 0.7 merge.1
  82.3 3.5 %all-to-all-start.4 = ((f32[16,1,1152]{2,1,0:T(1,128)}), f32[16,1,1152]{2,1,0:T(1,128)S(1)}, u32[]{:S(2)}, u32[]{:S(2)}) async-start(f32[16,1,1152]{2,1,0:T(1,128)} %merge.1), calls=%async_computation.4 | async-start | bytes 147456 | tf_op jit(solution)/shard_map/all_to_all | solution.py:19
  85.8 0.6 broadcast_in_dim.3
  86.4 5.8 %all-to-all-done.4.parts = f32[16,1,1152]{2,1,0:T(1,128)S(1)} async-done(((f32[16,1,1152]{2,1,0:T(1,128)}), f32[16,1,1152]{2,1,0:T(1,128)S(1)}, u32[]{:S(2)}, u32[]{:S(2)}) %all-to-all-start.4) | async-done | bytes 73760 | tf_op jit(solution)/shard_map/all_to_all | solution.py:19
  92.3 0.6 finish.1
  (4 shorter events, 0.1 us)
Async XLA Ops:
  2.1 17.2 %all-to-all-start = ((bf16[32,16,256]{2,1,0:T(8,128)(2,1)}), bf16[32,16,256]{2,1,0:T(8,128)(2,1)S(1)}, u32[]{:S(2)}, u32[]{:S(2)}) async-start(bf16[32,16,256]{2,1,0:T(8,128)(2,1)} %get-tuple-element.9), calls=%async_computation | async-start | bytes 524288 | tf_op jit(solution)/shard_map/all_to_all | solution.py:19
  12.9 18.9 %copy-start.4 = (s32[1,1,4096]{2,1,0:T(1,128)S(1)}, s32[1,1,4096]{2,1,0:T(1,128)}, u32[]{:S(2)}) copy-start(s32[1,1,4096]{2,1,0:T(1,128)} %param.15) | copy-start | bytes 49156
  12.9 18.9 %copy-start.5 = (s32[1,64]{1,0:T(1,128)S(1)}, s32[1,64]{1,0:T(1,128)}, u32[]{:S(2)}) copy-start(s32[1,64]{1,0:T(1,128)} %ranks.1) | copy-start | bytes 772
  20.4 3.4 %collective-permute-start = (f32[16,8,128]{2,1,0:T(8,128)S(1)}, f32[16,8,128]{2,1,0:T(8,128)S(1)}, u32[]{:S(2)}, u32[]{:S(2)}) collective-permute-start(f32[16,8,128]{2,1,0:T(8,128)S(1)} %get-tuple-element.11), channel_id=1, source_target_pairs={{0,1},{1,0},{2,3},{3,2},{4,5},{5,4},{6,7},{7,6},{8,9},{9,8},{10,11... | collective-permute-start | bytes 196616 | tf_op jit(solution)/shard_map/ppermute | solution.py:306
  22.6 1.2 %collective-permute-start.1 = (bf16[16,256]{1,0:T(8,128)(2,1)S(1)}, bf16[16,256]{1,0:T(8,128)(2,1)S(1)}, u32[]{:S(2)}, u32[]{:S(2)}) collective-permute-start(bf16[16,256]{1,0:T(8,128)(2,1)S(1)} %get-tuple-element.12.noise), channel_id=1, source_target_pairs={{0,1},{1,0},{2,3},{3,2},{4,5},{5,4},{6,7},{7,6},{8,9},{9,8},{10,11... | collective-permute-start | bytes 24584 | tf_op jit(solution)/shard_map/ppermute | solution.py:290
  24.5 18.1 %all-to-all-start.1 = ((bf16[4,320,128]{2,1,0:T(8,128)(2,1)}), bf16[4,320,128]{2,1,0:T(8,128)(2,1)S(1)}, u32[]{:S(2)}, u32[]{:S(2)}) async-start(bf16[4,320,128]{2,1,0:T(8,128)(2,1)} %spread.1), calls=%async_computation.1 | async-start | bytes 655360 | tf_op jit(solution)/shard_map/all_to_all | solution.py:19
  42.7 4.2 %collective-permute-start.2 = (bf16[16,8,128]{2,1,0:T(8,128)(2,1)S(1)}, bf16[16,8,128]{2,1,0:T(8,128)(2,1)S(1)}, u32[]{:S(2)}, u32[]{:S(2)}) collective-permute-start(bf16[16,8,128]{2,1,0:T(8,128)(2,1)S(1)} %coeffs.1.mine), channel_id=1, source_target_pairs={{0,1},{1,0},{2,3},{3,2},{4,5},{5,4},{6,7},{7,6},{8,9},{9,8},{10,11... | collective-permute-start | bytes 98312 | tf_op jit(solution)/shard_map/ppermute | solution.py:314
  44.5 1.6 %copy-start = (bf16[2,1,256,2048]{3,2,1,0:T(8,128)(2,1)S(1)}, bf16[2,1,256,2048]{3,2,1,0:T(8,128)(2,1)}, u32[]{:S(2)}) copy-start(bf16[2,1,256,2048]{3,2,1,0:T(8,128)(2,1)} %param.9) | copy-start | bytes 6291460
  46.1 1.6 %copy-start.1 = (bf16[1,64,64,256]{3,2,1,0:T(8,128)(2,1)S(1)}, bf16[1,64,64,256]{3,2,1,0:T(8,128)(2,1)}, u32[]{:S(2)}) copy-start(bf16[1,64,64,256]{3,2,1,0:T(8,128)(2,1)} %param.10) | copy-start | bytes 6291460
  46.1 15.9 %copy-start.2 = (s32[1,1,4096]{2,1,0:T(1,128)S(1)}, s32[1,1,4096]{2,1,0:T(1,128)}, u32[]{:S(2)}) copy-start(s32[1,1,4096]{2,1,0:T(1,128)} %param.14) | copy-start | bytes 49156
  46.1 15.9 %copy-start.3 = (s32[1,1,4096]{2,1,0:T(1,128)S(1)}, s32[1,1,4096]{2,1,0:T(1,128)}, u32[]{:S(2)}) copy-start(s32[1,1,4096]{2,1,0:T(1,128)} %param.13) | copy-start | bytes 49156
  59.5 5.5 %collective-permute-start.3 = (bf16[8,16,256]{2,1,0:T(8,128)(2,1)S(1)}, bf16[8,16,256]{2,1,0:T(8,128)(2,1)S(1)}, u32[]{:S(2)}, u32[]{:S(2)}) collective-permute-start(bf16[8,16,256]{2,1,0:T(8,128)(2,1)S(1)} %convert_element_type.3), channel_id=1, source_target_pairs={{0,8},{8,16},{16,24},{24,32},{32,40},{40,48},{48,56},{56,64},{64,7... | collective-permute-start | bytes 196616 | tf_op jit(solution)/shard_map/ppermute | solution.py:328
  82.3 10.0 %all-to-all-start.4 = ((f32[16,1,1152]{2,1,0:T(1,128)}), f32[16,1,1152]{2,1,0:T(1,128)S(1)}, u32[]{:S(2)}, u32[]{:S(2)}) async-start(f32[16,1,1152]{2,1,0:T(1,128)} %merge.1), calls=%async_computation.4 | async-start | bytes 147456 | tf_op jit(solution)/shard_map/all_to_all | solution.py:19

commit v4 on v3

--- a/solution.py
+++ b/solution.py
@@ -1,3 +1,5 @@
+import functools
+
 import jax
 import jax.numpy as jnp
 from jax import lax
@@ -102,33 +104,34 @@
                 out[n, at : at + 16] = pieces[core][:, 128 * side : 128 * side + 128]
 
 
-def project_kernel(columns, right, keep, send):
+def project_kernel(columns, right, out, *, away):
     row, core = lax.axis_index(ROW), lax.axis_index("col_1")
+    half = 1 - core if away else core
     tiles = 2 * columns.shape[0]
     groups = right.shape[0] // 8
     lane = lax.broadcasted_iota(jnp.int32, (8, 128), 1)
-    for half, out in ((core, keep), (1 - core, send)):
-        def step(g, carry, half=half, out=out):
-            base = (half * groups + g) * 4
-            blocks = []
-            low = []
-            for n in range(4):
-                slot = base + n
-                tile = jnp.where(slot < row, slot, slot - row)
-                first = tile < tiles // 2
-                blocks.append(columns[jnp.where(first, tile, tiles - 1 - tile)])
-                low.append(first)
-            factor = right[pl.ds(base, 4)].reshape(256, 256)
-            full = nt_dot(jnp.concatenate(blocks, axis=0), factor)
-            parts = []
-            for n in range(4):
-                cols = full[16 * n : 16 * n + 16, 128 * (n // 2) : 128 * (n // 2) + 128]
-                parts.append(jnp.where(low[n], cols[:8], cols[8:]))
-            out[2 * g] = jnp.where(lane < 64, parts[0], parts[1])
-            out[2 * g + 1] = jnp.where(lane < 64, parts[2], parts[3])
-            return carry
-
-        lax.fori_loop(0, groups, step, 0, unroll=4)
+
+    def step(g, carry):
+        base = (half * groups + g) * 4
+        blocks = []
+        low = []
+        for n in range(4):
+            slot = base + n
+            tile = jnp.where(slot < row, slot, slot - row)
+            first = tile < tiles // 2
+            blocks.append(columns[jnp.where(first, tile, tiles - 1 - tile)])
+            low.append(first)
+        factor = right[pl.ds(base, 4)].reshape(256, 256)
+        full = nt_dot(jnp.concatenate(blocks, axis=0), factor)
+        parts = []
+        for n in range(4):
+            cols = full[16 * n : 16 * n + 16, 128 * (n // 2) : 128 * (n // 2) + 128]
+            parts.append(jnp.where(low[n], cols[:8], cols[8:]))
+        out[2 * g] = jnp.where(lane < 64, parts[0], parts[1])
+        out[2 * g + 1] = jnp.where(lane < 64, parts[2], parts[3])
+        return carry
+
+    lax.fori_loop(0, groups, step, 0, unroll=4)
 
 
 def coeff_kernel(allowed, parts, out):
@@ -166,7 +169,7 @@
         out[8 * h : 8 * h + 8] = total[8 * h : 8 * h + 8]
 
 
-def sample_kernel(mine, theirs, left, on_diag, out):
+def sample_kernel(mine, theirs, left, on_diag, out, samples):
     row, core = lax.axis_index(ROW), lax.axis_index("col_1")
     blocks = mine.shape[0]
     last = 4 * blocks - 1
@@ -184,36 +187,60 @@
         weights = jnp.concatenate(rows, axis=1)
         factor = left[pl.ds(half * blocks, blocks)].reshape(blocks * 128, left.shape[2])
         acc = acc + jnp.dot(weights, factor, preferred_element_type=F32)
+    samples[...] = acc
     for n in range(out.shape[0]):
-        out[n] = acc
-
-
-def lookup(table, idx):
+        out[n] = acc.astype(BF16)
+
+
+def pack(table, words):
+    tiles = [
+        [table[p, 8 * h : 8 * h + 8].astype(F32) for h in range(2)] for p in range(table.shape[0])
+    ]
+    top = jnp.abs(tiles[0][0])
+    for pair in tiles:
+        for tile in pair:
+            top = jnp.maximum(top, jnp.abs(tile))
+    top = jnp.maximum(jnp.max(top, axis=1, keepdims=True), 1e-30)
+    scale = 32700.0 / top
+    for p, pair in enumerate(tiles):
+        upper, lower = (jnp.round(tile * scale).astype(jnp.int32) for tile in pair)
+        words[p] = (upper << 16) | (lower & 0xFFFF)
+    return jnp.broadcast_to(top * (1.0 / 32700.0), (8, 128))
+
+
+def lookup(words, unit, idx):
     low = idx & 127
     bit = [((idx >> (7 + n)) & 1) == 1 for n in range(5)]
 
     def tree(level, number):
         if level < 0:
-            h, piece, half = number >> 4, (number >> 1) & 7, number & 1
-            source = table[piece, 8 * h : 8 * h + 8, 128 * half : 128 * half + 128]
+            piece, half = number >> 1, number & 1
+            source = words[piece, :, 128 * half : 128 * half + 128]
             return jnp.take_along_axis(source, low, axis=1, mode="promise_in_bounds")
-        zero = tree(level - 1, number)
-        one = tree(level - 1, number | (1 << level))
-        return jnp.where(bit[level], one, zero)
-
-    return tree(4, 0)
-
-
-def own_kernel(table, first, partner, out):
+        return jnp.where(bit[level], tree(level - 1, number | (1 << level)), tree(level - 1, number))
+
+    word = tree(3, 0)
+    return (jnp.where(bit[4], word << 16, word) >> 16).astype(F32) * unit
+
+
+def own_kernel(table, first, partner, out, words):
+    unit = pack(table, words)
+
     def step(n, carry):
         at = pl.multiple_of(n * 128, 128)
         a = jnp.broadcast_to(first[:, pl.ds(at, 128)], (8, 128))
         b = jnp.broadcast_to(partner[:, pl.ds(at, 128)], (8, 128))
-        other = jnp.where(b >= 4096, lookup(table, b), 0.0)
-        out[:, pl.ds(at, 128)] = lookup(table, a) - other
+        other = jnp.where(b >= 4096, lookup(words, unit, b), 0.0)
+        out[:, pl.ds(at, 128)] = lookup(words, unit, a) - other
         return carry
 
-    lax.fori_loop(0, first.shape[1] // 128, step, 0, unroll=4)
+    lax.fori_loop(0, first.shape[1] // 128, step, 0, unroll=8)
+
+
+def emit_kernel(samples, out):
+    for h in range(2):
+        for s in range(8):
+            out[s, h] = samples[8 * h + s : 8 * h + s + 1]
 
 
 def put_rows(out, rows):
@@ -222,13 +249,13 @@
             out[n, :, 128 * i : 128 * i + 128] = rows[i]
 
 
-def bin_kernel(prev, partner, base, onehot, out, table, pieces):
-    table[...] = prev[...].astype(F32)
+def bin_kernel(prev, partner, base, onehot, out, words, pieces):
+    unit = pack(prev, words)
 
     def step(n, carry):
         at = pl.multiple_of(n * 128, 128)
         b = jnp.broadcast_to(partner[:, pl.ds(at, 128)], (8, 128))
-        differ = base[:, pl.ds(at, 128)] - jnp.where(b < 4096, lookup(table, b), 0.0)
+        differ = base[:, pl.ds(at, 128)] - jnp.where(b < 4096, lookup(words, unit, b), 0.0)
         value = 0.5 * differ * differ
         top = value.astype(BF16).astype(F32)
         rest = value - top
@@ -237,7 +264,7 @@
         pieces[:, pl.ds(at, 128)] = stack.astype(BF16)
         return carry
 
-    lax.fori_loop(0, partner.shape[1] // 128, step, 0, unroll=4)
+    lax.fori_loop(0, partner.shape[1] // 128, step, 0, unroll=8)
     total = nt_dot(pieces[...], onehot[...])
     sums = (total[:8] + total[8:16]) + total[16:24]
     put_rows(out, [sums[i : i + 1] for i in range(8)] + [total[24:25]])
@@ -296,14 +323,18 @@
         name="stage",
     )(right_factor[0])
 
-    keep, send = call(
-        project_kernel,
-        (vmem((16, 8, 128), F32), vmem((16, 8, 128), F32)),
-        [VM, VM],
-        flops=1 << 28,
-        name="project",
-    )(columns, right)
+    def project(away, name):
+        return call(
+            functools.partial(project_kernel, away=away),
+            vmem((16, 8, 128), F32),
+            [VM, VM],
+            flops=1 << 28,
+            name=name,
+        )(columns, right)
+
+    send = project(True, "send")
     received = lax.ppermute(send, "col_1", swap)
+    keep = project(False, "keep")
     spread = call(
         spread_kernel, vmem((4, 320, 128), BF16), [VM, VM, VM, VM], name="spread"
     )(keep, received, local, other_noise)
@@ -315,29 +346,33 @@
     on_diag = call(
         on_diag_kernel, vmem((16, span), F32), [VM, VM], flops=1 << 28, name="ondiag"
     )(sums, diag_factor[:, 0])
-    copies = call(
+    copies, own_samples = call(
         sample_kernel,
-        vmem((cols, 16, span), F32),
+        (vmem((cols, 16, span), BF16), vmem((16, span), F32)),
         [VM, VM, VM, VM],
         flops=1 << 26,
         name="samples",
     )(mine, theirs, left_factor[0].reshape(32, 128, span), on_diag)
-    samples = jnp.transpose(copies[0].reshape(2, 8, span), (1, 0, 2))[:, :, None]
-
     own_tiles = exchange(copies, COL)
-    prev_tiles = lax.ppermute(
-        own_tiles.astype(BF16), ROW, [(source, source + 1) for source in range(rows - 1)]
-    )
-    base = call(own_kernel, vmem((8, pairs), F32), [VM, VM, VM], flops=1 << 26, name="own")(
-        own_tiles, first, partner
-    )
+    prev_tiles = lax.ppermute(own_tiles, ROW, [(source, source + 1) for source in range(rows - 1)])
+    samples = call(
+        emit_kernel, jax.ShapeDtypeStruct((8, 2, 1, span), F32), [VM], name="emit"
+    )(own_samples)
+    base = call(
+        own_kernel,
+        vmem((8, pairs), F32),
+        [VM, VM, VM],
+        flops=1 << 26,
+        scratch_shapes=[pltpu.VMEM((cols, 8, span), jnp.int32)],
+        name="own",
+    )(own_tiles, first, partner)
     partial = call(
         bin_kernel,
         vmem((lax.axis_size(ZC), 1, 9 * NBIN), F32),
         [VM, VM, VM, VM],
         flops=1 << 26,
         scratch_shapes=[
-            pltpu.VMEM((cols, 16, span), F32),
+            pltpu.VMEM((cols, 8, span), jnp.int32),
             pltpu.VMEM((32, pairs), BF16),
         ],
         name="bins",

time: 93.4 us -> 91.8 us (0.983)
  Pallas kernels: 12.9 us -> 11.4 us
    pallas_call x12 -> x14, Pallas kernels: 12.9 us -> 11.4 us  [held(): run(*(a if spec is SM else pltpu.with_memory_space_constraint(a, spec.mem...]
  transfers between devices with their start and end apart: 7 -> 7, of which waited for: 4 -> 4; matrix products, arithmetic and copies ran while one was open for 1% -> 0% of each run, Pallas kernels for 7% -> 7%
where the time goes in v4:
time: 91.8 us; the launch traced here: 91.3 us
  starting transfers between devices  27.1 us (30%)
  blocking collectives  25.3 us (28%)
  waiting for transfers between devices  22.8 us (25%)
  Pallas kernels  11.4 us (12%)
  local copies, waits for them, and re-layouts  3.91 us (4%)
    all_to_all x2, blocking collectives, exchange(): return lax.all_to_all(copies, axis, 0, 0, tiled=True)  25.3 us
    all_to_all x3, waiting for transfers between devices, exchange(): return lax.all_to_all(copies, axis, 0, 0, tiled=True)  22.2 us
    all_to_all x3, starting transfers between devices, exchange(): return lax.all_to_all(copies, axis, 0, 0, tiled=True)  20.3 us
    pallas_call x14, Pallas kernels, held(): run(*(a if spec is SM else pltpu.with_memory_space_constraint(a, spec.mem...  11.4 us
    unnamed x13, local copies, waits for them, and re-layouts  3.91 us
    ppermute x1, starting transfers between devices, body(): lax.ppermute(own_tiles, ROW, [(source, source + 1) for source in range(ro...  2.65 us
    ppermute x1, starting transfers between devices, body(): received = lax.ppermute(send, 'col_1', swap)  2.17 us
    ppermute x1, starting transfers between devices, body(): theirs = lax.ppermute(mine, 'col_1', swap)  1.87 us
  transfers between devices with their start and end apart: 7, of which 4 were waited for; matrix products, arithmetic and copies ran while one was open for 0% of the time, Pallas kernels for 7%

profile of v4, /device:TPU:1, one launch (start us, length us, event | category | flops | bytes accessed | tf_op | source)
XLA Modules:
  0.0 91.3 jit_solution(10259591019188684201)
XLA Ops:
  0.6 0.7 copy.10.noise
  1.3 0.7 copies.1
  2.1 9.2 %all-to-all-start = ((bf16[32,16,256]{2,1,0:T(8,128)(2,1)}), bf16[32,16,256]{2,1,0:T(8,128)(2,1)S(1)}, u32[]{:S(2)}, u32[]{:S(2)}) async-start(bf16[32,16,256]{2,1,0:T(8,128)(2,1)} %get-tuple-element.9), calls=%async_computation | async-start | bytes 524288 | tf_op jit(solution)/shard_map/all_to_all | solution.py:21
  11.3 1.6 %stage.1.right = bf16[64,64,256]{2,1,0:T(8,128)(2,1)S(1)} custom-call(bf16[64,64,256]{2,1,0:T(8,128)(2,1)} %bitcast.12), custom_call_target="tpu_custom_call" | custom-call | flops 1 | bytes 1048576 | tf_op jit(solution)/shard_map/stage/pallas_call | solution.py:44
  12.9 6.4 %all-to-all-done.columns = bf16[32,16,256]{2,1,0:T(8,128)(2,1)S(1)} async-done(((bf16[32,16,256]{2,1,0:T(8,128)(2,1)}), bf16[32,16,256]{2,1,0:T(8,128)(2,1)S(1)}, u32[]{:S(2)}, u32[]{:S(2)}) %all-to-all-start) | async-done | bytes 262176 | tf_op jit(solution)/shard_map/all_to_all | solution.py:21
  19.3 0.6 send.1
  19.9 0.0 copy-start.2
  19.9 0.0 copy-start.4
  19.9 2.2 %collective-permute-start = (f32[16,8,128]{2,1,0:T(8,128)S(1)}, f32[16,8,128]{2,1,0:T(8,128)S(1)}, u32[]{:S(2)}, u32[]{:S(2)}) collective-permute-start(f32[16,8,128]{2,1,0:T(8,128)S(1)} %send.1), channel_id=1, source_target_pairs={{0,1},{1,0},{2,3},{3,2},{4,5},{5,4},{6,7},{7,6},{8,9},{9,8},{10,11... | collective-permute-start | bytes 196616 | tf_op jit(solution)/shard_map/ppermute | solution.py:336
  22.1 0.1 collective-permute-start.1
  22.2 0.6 keep.1
  22.7 0.5 collective-permute-done.1.other
  23.2 0.0 collective-permute-done.received
  23.2 0.8 spread.1
  24.0 7.3 %all-to-all-start.1 = ((bf16[4,320,128]{2,1,0:T(8,128)(2,1)}), bf16[4,320,128]{2,1,0:T(8,128)(2,1)S(1)}, u32[]{:S(2)}, u32[]{:S(2)}) async-start(bf16[4,320,128]{2,1,0:T(8,128)(2,1)} %spread.1), calls=%async_computation.1 | async-start | bytes 655360 | tf_op jit(solution)/shard_map/all_to_all | solution.py:21
  31.3 0.0 copy-done.2
  31.3 0.0 copy-done.4
  31.3 0.9 prepare.1
  32.2 9.9 %all-to-all-done.1.parts = bf16[4,320,128]{2,1,0:T(8,128)(2,1)S(1)} async-done(((bf16[4,320,128]{2,1,0:T(8,128)(2,1)}), bf16[4,320,128]{2,1,0:T(8,128)(2,1)S(1)}, u32[]{:S(2)}, u32[]{:S(2)}) %all-to-all-start.1) | async-done | bytes 327712 | tf_op jit(solution)/shard_map/all_to_all | solution.py:21
  42.1 1.9 %collective-permute-start.2 = (bf16[16,8,128]{2,1,0:T(8,128)(2,1)S(1)}, bf16[16,8,128]{2,1,0:T(8,128)(2,1)S(1)}, u32[]{:S(2)}, u32[]{:S(2)}) collective-permute-start(bf16[16,8,128]{2,1,0:T(8,128)(2,1)S(1)} %coeffs.1.mine), channel_id=1, source_target_pairs={{0,1},{1,0},{2,3},{3,2},{4,5},{5,4},{6,7},{7,6},{8,9},{9,8},{10,11... | collective-permute-start | bytes 98312 | tf_op jit(solution)/shard_map/ppermute | solution.py:345
  44.0 0.0 copy-start
  44.0 1.6 %copy-done = bf16[2,1,256,2048]{3,2,1,0:T(8,128)(2,1)S(1)} copy-done((bf16[2,1,256,2048]{3,2,1,0:T(8,128)(2,1)S(1)}, bf16[2,1,256,2048]{3,2,1,0:T(8,128)(2,1)}, u32[]{:S(2)}) %copy-start) | copy-done | bytes 2097176
  45.6 0.0 copy-start.3
  45.6 0.0 copy-start.5
  45.6 0.7 ondiag.1.on_diag
  46.3 0.0 collective-permute-done.2.theirs
  46.3 0.0 copy-start.1
  46.3 1.6 %copy-done.1 = bf16[1,64,64,256]{3,2,1,0:T(8,128)(2,1)S(1)} copy-done((bf16[1,64,64,256]{3,2,1,0:T(8,128)(2,1)S(1)}, bf16[1,64,64,256]{3,2,1,0:T(8,128)(2,1)}, u32[]{:S(2)}) %copy-start.1) | copy-done | bytes 2097176
  47.9 0.4 samples.1
  48.3 10.6 %all_to_all.25.table = bf16[8,16,256]{2,1,0:T(8,128)(2,1)S(1)} all-to-all(bf16[8,16,256]{2,1,0:T(8,128)(2,1)S(1)} %get-tuple-element.12), channel_id=1, replica_groups=mesh['row_0'=4,'row_1'=2,'row_2'=4,'col_0'=4,'col_1'=2] {'col_0','col_1'}, dimensions={0} | all-to-all | bytes 131072 | tf_op jit(solution)/shard_map/all_to_all | solution.py:21
  58.9 2.6 %collective-permute-start.3 = (bf16[8,16,256]{2,1,0:T(8,128)(2,1)S(1)}, bf16[8,16,256]{2,1,0:T(8,128)(2,1)S(1)}, u32[]{:S(2)}, u32[]{:S(2)}) collective-permute-start(bf16[8,16,256]{2,1,0:T(8,128)(2,1)S(1)} %all_to_all.25.table), channel_id=1, source_target_pairs={{0,8},{8,16},{16,24},{24,32},{32,40},{40,48},{48,56},{56,64},{64,7... | collective-permute-start | bytes 196616 | tf_op jit(solution)/shard_map/ppermute | solution.py:357
  61.6 0.0 copy-done.3
  61.6 0.0 copy-done.5
  61.6 1.7 %own.1.base = f32[8,4096]{1,0:T(8,128)S(1)} custom-call(bf16[8,16,256]{2,1,0:T(8,128)(2,1)S(1)} %all_to_all.25.table, s32[1,4096]{1,0:T(1,128)S(1)} %bitcast.11, s32[1,4096]{1,0:T(1,128)S(1)} %bitcast.9), custom_call_target="tpu_custom_call" | custom-call | flops 67108864 | bytes 1048576 | tf_op jit(solution)/shard_map/own/pallas_call | solution.py:44
  63.3 0.0 collective-permute-done.3.prev
  63.3 1.5 %bins.1 = f32[16,1,1152]{2,1,0:T(1,128)S(1)} custom-call(bf16[8,16,256]{2,1,0:T(8,128)(2,1)S(1)} %collective-permute-done.3.prev, s32[1,4096]{1,0:T(1,128)S(1)} %bitcast.10, f32[8,4096]{1,0:T(8,128)S(1)} %own.1.base, bf16[128,4096]{1,0:T(8,128)(2,1)S(1)} %get-tuple-element.13.onehot), custom_call_target="tpu_custom_call" | custom-call | flops 67108864 | bytes 1048576 | tf_op jit(solution)/shard_map/bins/pallas_call | solution.py:44
  64.8 14.7 %all_to_all.26.parts = f32[16,1,1152]{2,1,0:T(1,128)S(1)} all-to-all(f32[16,1,1152]{2,1,0:T(1,128)S(1)} %bins.1), channel_id=1, replica_groups=mesh['row_0'=4,'row_1'=2,'row_2'=4,'col_0'=4,'col_1'=2] {'row_1','col_0'..., dimensions={0} | all-to-all | bytes 147456 | tf_op jit(solution)/shard_map/all_to_all | solution.py:21
  79.6 0.7 merge.1
  80.3 3.8 %all-to-all-start.4 = ((f32[16,1,1152]{2,1,0:T(1,128)}), f32[16,1,1152]{2,1,0:T(1,128)S(1)}, u32[]{:S(2)}, u32[]{:S(2)}) async-start(f32[16,1,1152]{2,1,0:T(1,128)} %merge.1), calls=%async_computation.4 | async-start | bytes 147456 | tf_op jit(solution)/shard_map/all_to_all | solution.py:21
  84.1 0.6 emit.1
  84.7 5.9 %all-to-all-done.4.parts = f32[16,1,1152]{2,1,0:T(1,128)S(1)} async-done(((f32[16,1,1152]{2,1,0:T(1,128)}), f32[16,1,1152]{2,1,0:T(1,128)S(1)}, u32[]{:S(2)}, u32[]{:S(2)}) %all-to-all-start.4) | async-done | bytes 73760 | tf_op jit(solution)/shard_map/all_to_all | solution.py:21
  90.6 0.6 finish.1
  (1 shorter events, 0.0 us)
Async XLA Ops:
  2.1 17.2 %all-to-all-start = ((bf16[32,16,256]{2,1,0:T(8,128)(2,1)}), bf16[32,16,256]{2,1,0:T(8,128)(2,1)S(1)}, u32[]{:S(2)}, u32[]{:S(2)}) async-start(bf16[32,16,256]{2,1,0:T(8,128)(2,1)} %get-tuple-element.9), calls=%async_computation | async-start | bytes 524288 | tf_op jit(solution)/shard_map/all_to_all | solution.py:21
  19.9 11.4 %copy-start.2 = (s32[1,1,4096]{2,1,0:T(1,128)S(1)}, s32[1,1,4096]{2,1,0:T(1,128)}, u32[]{:S(2)}) copy-start(s32[1,1,4096]{2,1,0:T(1,128)} %param.15) | copy-start | bytes 49156
  19.9 11.4 %copy-start.4 = (s32[1,64]{1,0:T(1,128)S(1)}, s32[1,64]{1,0:T(1,128)}, u32[]{:S(2)}) copy-start(s32[1,64]{1,0:T(1,128)} %ranks.1) | copy-start | bytes 772
  19.9 3.4 %collective-permute-start = (f32[16,8,128]{2,1,0:T(8,128)S(1)}, f32[16,8,128]{2,1,0:T(8,128)S(1)}, u32[]{:S(2)}, u32[]{:S(2)}) collective-permute-start(f32[16,8,128]{2,1,0:T(8,128)S(1)} %send.1), channel_id=1, source_target_pairs={{0,1},{1,0},{2,3},{3,2},{4,5},{5,4},{6,7},{7,6},{8,9},{9,8},{10,11... | collective-permute-start | bytes 196616 | tf_op jit(solution)/shard_map/ppermute | solution.py:336
  22.1 1.2 %collective-permute-start.1 = (bf16[16,256]{1,0:T(8,128)(2,1)S(1)}, bf16[16,256]{1,0:T(8,128)(2,1)S(1)}, u32[]{:S(2)}, u32[]{:S(2)}) collective-permute-start(bf16[16,256]{1,0:T(8,128)(2,1)S(1)} %get-tuple-element.10.noise), channel_id=1, source_target_pairs={{0,1},{1,0},{2,3},{3,2},{4,5},{5,4},{6,7},{7,6},{8,9},{9,8},{10,11... | collective-permute-start | bytes 24584 | tf_op jit(solution)/shard_map/ppermute | solution.py:317
  24.0 18.1 %all-to-all-start.1 = ((bf16[4,320,128]{2,1,0:T(8,128)(2,1)}), bf16[4,320,128]{2,1,0:T(8,128)(2,1)S(1)}, u32[]{:S(2)}, u32[]{:S(2)}) async-start(bf16[4,320,128]{2,1,0:T(8,128)(2,1)} %spread.1), calls=%async_computation.1 | async-start | bytes 655360 | tf_op jit(solution)/shard_map/all_to_all | solution.py:21
  42.1 4.2 %collective-permute-start.2 = (bf16[16,8,128]{2,1,0:T(8,128)(2,1)S(1)}, bf16[16,8,128]{2,1,0:T(8,128)(2,1)S(1)}, u32[]{:S(2)}, u32[]{:S(2)}) collective-permute-start(bf16[16,8,128]{2,1,0:T(8,128)(2,1)S(1)} %coeffs.1.mine), channel_id=1, source_target_pairs={{0,1},{1,0},{2,3},{3,2},{4,5},{5,4},{6,7},{7,6},{8,9},{9,8},{10,11... | collective-permute-start | bytes 98312 | tf_op jit(solution)/shard_map/ppermute | solution.py:345
  44.0 1.6 %copy-start = (bf16[2,1,256,2048]{3,2,1,0:T(8,128)(2,1)S(1)}, bf16[2,1,256,2048]{3,2,1,0:T(8,128)(2,1)}, u32[]{:S(2)}) copy-start(bf16[2,1,256,2048]{3,2,1,0:T(8,128)(2,1)} %param.9) | copy-start | bytes 6291460
  45.6 16.0 %copy-start.3 = (s32[1,1,4096]{2,1,0:T(1,128)S(1)}, s32[1,1,4096]{2,1,0:T(1,128)}, u32[]{:S(2)}) copy-start(s32[1,1,4096]{2,1,0:T(1,128)} %param.14) | copy-start | bytes 49156
  45.6 16.0 %copy-start.5 = (s32[1,1,4096]{2,1,0:T(1,128)S(1)}, s32[1,1,4096]{2,1,0:T(1,128)}, u32[]{:S(2)}) copy-start(s32[1,1,4096]{2,1,0:T(1,128)} %param.13) | copy-start | bytes 49156
  46.3 1.6 %copy-start.1 = (bf16[1,64,64,256]{3,2,1,0:T(8,128)(2,1)S(1)}, bf16[1,64,64,256]{3,2,1,0:T(8,128)(2,1)}, u32[]{:S(2)}) copy-start(bf16[1,64,64,256]{3,2,1,0:T(8,128)(2,1)} %param.10) | copy-start | bytes 6291460
  58.9 4.4 %collective-permute-start.3 = (bf16[8,16,256]{2,1,0:T(8,128)(2,1)S(1)}, bf16[8,16,256]{2,1,0:T(8,128)(2,1)S(1)}, u32[]{:S(2)}, u32[]{:S(2)}) collective-permute-start(bf16[8,16,256]{2,1,0:T(8,128)(2,1)S(1)} %all_to_all.25.table), channel_id=1, source_target_pairs={{0,8},{8,16},{16,24},{24,32},{32,40},{40,48},{48,56},{56,64},{64,7... | collective-permute-start | bytes 196616 | tf_op jit(solution)/shard_map/ppermute | solution.py:357
  80.3 10.4 %all-to-all-start.4 = ((f32[16,1,1152]{2,1,0:T(1,128)}), f32[16,1,1152]{2,1,0:T(1,128)S(1)}, u32[]{:S(2)}, u32[]{:S(2)}) async-start(f32[16,1,1152]{2,1,0:T(1,128)} %merge.1), calls=%async_computation.4 | async-start | bytes 147456 | tf_op jit(solution)/shard_map/all_to_all | solution.py:21

commit v5 on v4

--- a/solution.py
+++ b/solution.py
@@ -14,6 +14,10 @@
 XY = ("row_0", "row_2")
 ZC = ("row_1", "col_0", "col_1")
 F32 = jnp.float32
+F16 = jnp.float16
+SUM_UNIT = 128.0
+NOISE_UNIT = 1024.0
+TURNS = (1, 3, 2)
 BF16 = jnp.bfloat16
 
 
@@ -27,6 +31,7 @@
 
 HB = pl.BlockSpec(memory_space=pltpu.HBM)
 VM = pl.BlockSpec(memory_space=pltpu.VMEM)
+RAW = pl.BlockSpec(memory_space=pltpu.VMEM)
 SM = pl.BlockSpec(memory_space=pltpu.SMEM)
 
 
@@ -43,7 +48,7 @@
     def held(*args):
         return run(
             *(
-                a if spec is SM else pltpu.with_memory_space_constraint(a, spec.memory_space)
+                a if spec is SM or spec is RAW else pltpu.with_memory_space_constraint(a, spec.memory_space)
                 for a, spec in zip(args, in_specs)
             )
         )
@@ -52,7 +57,7 @@
 
 
 def copies_kernel(noise, local, out):
-    rows = [noise[s, h].astype(F32) for h in range(2) for s in range(8)]
+    rows = [noise[s].astype(F32)[h : h + 1] for h in range(2) for s in range(8)]
     mine = jnp.concatenate(rows, axis=0).astype(BF16)
     local[...] = mine
     for n in range(out.shape[0]):
@@ -61,10 +66,12 @@
 
 def prepare_kernel(bins, ranks, onehot, keep):
     core = lax.axis_index("col_1")
-    lane = lax.broadcasted_iota(jnp.int32, (1, 128), 1)
+    lane = lax.broadcasted_iota(jnp.int32, (1, 256), 1)
     for i in range(keep.shape[0]):
-        slot = 2 * (core * keep.shape[0] + i)
-        limit = jnp.where(lane < 64, ranks[0, slot], ranks[0, slot + 1] + 64)
+        slot = 4 * (core * keep.shape[0] + i)
+        limit = ranks[0, slot + 3] + 192
+        for n in (2, 1, 0):
+            limit = jnp.where(lane < 64 * n + 64, ranks[0, slot + n] + 64 * n, limit)
         keep[i] = jnp.where(lane < limit, 1.0, 0.0)
     bin_at = lax.broadcasted_iota(jnp.int32, (NBIN, 128), 0)
 
@@ -81,27 +88,6 @@
     copy = pltpu.make_async_copy(source, out, sem)
     copy.start()
     copy.wait()
-
-
-def spread_kernel(keep, received, noise, other, out):
-    blocks = keep.shape[0]
-    first = lax.axis_index("col_1") == 0
-    own = noise[...].astype(F32)
-    far = other[...].astype(F32)
-    pieces = (jnp.where(first, own, far).astype(BF16), jnp.where(first, far, own).astype(BF16))
-    copies = out.shape[0]
-    for i in range(0, blocks, 2):
-        total = jnp.concatenate([keep[i] + received[i], keep[i + 1] + received[i + 1]], axis=0)
-        top = total.astype(BF16)
-        rest = (total - top.astype(F32)).astype(BF16)
-        for n in range(copies):
-            out[n, 8 * i : 8 * i + 16] = top
-            out[n, 8 * (blocks + i) : 8 * (blocks + i) + 16] = rest
-    for core in range(2):
-        for side in range(2):
-            at = 16 * (blocks + 2 * core + side)
-            for n in range(copies):
-                out[n, at : at + 16] = pieces[core][:, 128 * side : 128 * side + 128]
 
 
 def project_kernel(columns, right, out, *, away):
@@ -127,65 +113,52 @@
         for n in range(4):
             cols = full[16 * n : 16 * n + 16, 128 * (n // 2) : 128 * (n // 2) + 128]
             parts.append(jnp.where(low[n], cols[:8], cols[8:]))
-        out[2 * g] = jnp.where(lane < 64, parts[0], parts[1])
-        out[2 * g + 1] = jnp.where(lane < 64, parts[2], parts[3])
+        out[g, :, :128] = jnp.where(lane < 64, parts[0], parts[1])
+        out[g, :, 128:] = jnp.where(lane < 64, parts[2], parts[3])
         return carry
 
     lax.fori_loop(0, groups, step, 0, unroll=4)
 
 
-def coeff_kernel(allowed, parts, out):
-    blocks = out.shape[0]
-    for i in range(0, blocks, 2):
-        total = jnp.zeros((16, 128), F32)
-        for n in range(parts.shape[0]):
-            top = parts[n, 8 * i : 8 * i + 16].astype(F32)
-            total = total + (top + parts[n, 8 * (blocks + i) : 8 * (blocks + i) + 16].astype(F32))
-        for k in range(2):
-            inside = jnp.broadcast_to(allowed[i + k], (8, 128)) > 0.5
-            out[i + k] = jnp.where(inside, total[8 * k : 8 * k + 8], 0.0).astype(BF16)
-
-
-def on_diag_kernel(parts, diag, out):
-    col = lax.axis_index(COL)
+def on_diag_kernel(n0, n1, n2, n3, diag, out):
+    col, chip = lax.axis_index(COL), lax.axis_index("col_0")
     span = diag.shape[1]
-    pieces = []
-    own = jnp.zeros((16, span), F32)
-    for n in range(parts.shape[0]):
-        for core in range(2):
-            at = 256 + 32 * core
-            piece = jnp.concatenate([parts[n, at : at + 16], parts[n, at + 16 : at + 32]], axis=1)
-            piece = piece.astype(F32)
-            number = 2 * n + core
-            own = jnp.where(col == number, piece, own)
-            pieces.append(jnp.where(number < col, piece, 0.0).astype(BF16))
-    before = jnp.concatenate(pieces, axis=1)
+    own = jnp.where(lax.axis_index("col_1") == 0, n0[:16].astype(F32), n0[16:].astype(F32))
     i_at = lax.broadcasted_iota(jnp.int32, (span, span), 0)
     j_at = lax.broadcasted_iota(jnp.int32, (span, span), 1)
+    acc = [own, own]
     at = pl.multiple_of(col * span, span)
     for h in range(2):
         corner = jnp.where(j_at < i_at, diag[h, :, pl.ds(at, span)].astype(F32), 0.0).astype(BF16)
-        total = nt_dot(before, diag[h]) + nt_dot(own.astype(BF16), corner) + own
-        out[8 * h : 8 * h + 8] = total[8 * h : 8 * h + 8]
+        acc[h] = acc[h] + nt_dot(own.astype(BF16), corner)
+    for noise, turn in zip((n0, n1, n2, n3), (0, *TURNS)):
+        for core in range(2):
+            number = 2 * lax.rem(chip + 4 - turn, 4) + core
+            piece = noise[16 * core : 16 * core + 16].astype(F32)
+            piece = jnp.where(number < col, piece, 0.0).astype(BF16)
+            from_ = pl.multiple_of(number * span, span)
+            for h in range(2):
+                acc[h] = acc[h] + nt_dot(piece, diag[h, :, pl.ds(from_, span)])
+    for h in range(2):
+        out[8 * h : 8 * h + 8] = acc[h][8 * h : 8 * h + 8]
 
 
 def sample_kernel(mine, theirs, left, on_diag, out, samples):
     row, core = lax.axis_index(ROW), lax.axis_index("col_1")
     blocks = mine.shape[0]
-    last = 4 * blocks - 1
-    lane = lax.broadcasted_iota(jnp.int32, (8, 128), 1)
-    side = jnp.where(lane < 64, 0, 1)
+    last = 8 * blocks - 1
+    side = lax.broadcasted_iota(jnp.int32, (8, 256), 1) >> 6
     acc = on_diag[...]
     for half, coeffs in ((core, mine), (1 - core, theirs)):
         rows = []
         for i in range(blocks):
-            slot = 2 * (half * blocks + i) + side
+            slot = 4 * (half * blocks + i) + side
             c = coeffs[i].astype(F32)
             upper = jnp.where(slot < row, c, 0.0)
             lower = jnp.where((slot >= row) & (slot < last), c, 0.0)
             rows.append(jnp.concatenate([upper, lower], axis=0).astype(BF16))
         weights = jnp.concatenate(rows, axis=1)
-        factor = left[pl.ds(half * blocks, blocks)].reshape(blocks * 128, left.shape[2])
+        factor = left[pl.ds(half * blocks, blocks)].reshape(blocks * 256, left.shape[2])
         acc = acc + jnp.dot(weights, factor, preferred_element_type=F32)
     samples[...] = acc
     for n in range(out.shape[0]):
@@ -303,13 +276,13 @@
     local, spread_noise = call(
         copies_kernel,
         (vmem((16, span), BF16), vmem((rows, 16, span), BF16)),
-        [VM],
+        [RAW],
         name="copies",
-    )(noise)
+    )(jnp.transpose(noise, (0, 2, 1, 3))[:, 0])
     columns = exchange(spread_noise, ROW)
     onehot, allowed = call(
         prepare_kernel,
-        (vmem((NBIN, pairs), BF16), vmem((16, 1, 128), F32)),
+        (vmem((NBIN, pairs), BF16), vmem((8, 1, 256), F32)),
         [VM, SM],
         flops=1 << 20,
         name="prepare",
@@ -326,7 +299,7 @@
     def project(away, name):
         return call(
             functools.partial(project_kernel, away=away),
-            vmem((16, 8, 128), F32),
+            vmem((8, 8, 256), F32),
             [VM, VM],
             flops=1 << 28,
             name=name,
@@ -335,24 +308,34 @@
     send = project(True, "send")
     received = lax.ppermute(send, "col_1", swap)
     keep = project(False, "keep")
-    spread = call(
-        spread_kernel, vmem((4, 320, 128), BF16), [VM, VM, VM, VM], name="spread"
-    )(keep, received, local, other_noise)
-    sums = exchange(spread, "col_0")
-    mine = call(coeff_kernel, vmem((16, 8, 128), BF16), [VM, VM], name="coeffs")(
-        allowed, sums
+    pair = keep + received
+    low_first = lax.axis_index("col_1") == 0
+    noises = jnp.where(
+        low_first,
+        jnp.concatenate([local, other_noise]),
+        jnp.concatenate([other_noise, local]),
     )
+    noises16 = (noises.astype(F32) * NOISE_UNIT).astype(F16)
+    payload = jnp.concatenate([(pair * SUM_UNIT).astype(F16).reshape(64, 256), noises16])
+    arrived = []
+    for turn in TURNS:
+        arrived.append(
+            lax.ppermute(payload, "col_0", [(chip, (chip + turn) % 4) for chip in range(4)])
+        )
+    total = sum(x[:64].astype(F32) for x in arrived).reshape(8, 8, 256) * (1.0 / SUM_UNIT) + pair
+    mine = jnp.where(allowed > 0.5, total, 0.0).astype(BF16)
+    all_noise = [noises] + [(x[64:].astype(F32) * (1.0 / NOISE_UNIT)).astype(BF16) for x in arrived]
     theirs = lax.ppermute(mine, "col_1", swap)
     on_diag = call(
-        on_diag_kernel, vmem((16, span), F32), [VM, VM], flops=1 << 28, name="ondiag"
-    )(sums, diag_factor[:, 0])
+        on_diag_kernel, vmem((16, span), F32), [VM] * 5, flops=1 << 28, name="ondiag"
+    )(*all_noise, diag_factor[:, 0])
     copies, own_samples = call(
         sample_kernel,
         (vmem((cols, 16, span), BF16), vmem((16, span), F32)),
         [VM, VM, VM, VM],
         flops=1 << 26,
         name="samples",
-    )(mine, theirs, left_factor[0].reshape(32, 128, span), on_diag)
+    )(mine, theirs, left_factor[0].reshape(16, 256, span), on_diag)
     own_tiles = exchange(copies, COL)
     prev_tiles = lax.ppermute(own_tiles, ROW, [(source, source + 1) for source in range(rows - 1)])
     samples = call(

time: 91.8 us -> 83.8 us (0.913)
  waiting for transfers between devices: 22.8 us -> 14.1 us
  local copies, waits for them, and re-layouts: 3.91 us -> 0.73 us
  blocking collectives: 25.3 us -> 28.1 us
  starting transfers between devices: 27.1 us -> 28.9 us
    all_to_all x3 -> x2, waiting for transfers between devices: 22.2 us -> 10.3 us  [exchange(): return lax.all_to_all(copies, axis, 0, 0, tiled=True)]
    ppermute x0 -> x3, starting transfers between devices: none -> 8.46 us  [body(): lax.ppermute(payload, 'col_0', [(chip, (chip + turn) % 4) for chip in ran...]
    all_to_all x3 -> x2, starting transfers between devices: 20.3 us -> 13 us  [exchange(): return lax.all_to_all(copies, axis, 0, 0, tiled=True)]
    ppermute x0 -> x3, waiting for transfers between devices: none -> 3.4 us  [body(): lax.ppermute(payload, 'col_0', [(chip, (chip + turn) % 4) for chip in ran...]
    unnamed x13 -> x15, local copies, waits for them, and re-layouts: 3.91 us -> 0.73 us
    all_to_all x2, blocking collectives: 25.3 us -> 28.1 us  [exchange(): return lax.all_to_all(copies, axis, 0, 0, tiled=True)]
    ppermute x1, starting transfers between devices: 0.1 us -> 1.04 us  [body(): other_noise = lax.ppermute(local, 'col_1', swap)]
    pallas_call x14 -> x12, Pallas kernels: 11.4 us -> 10.6 us  [held(): run(*(a if spec is SM or spec is RAW else pltpu.with_memory_space_constra...]
  transfers between devices with their start and end apart: 7 -> 9, of which waited for: 4 -> 5; matrix products, arithmetic and copies ran while one was open for 0% -> 0% of each run, Pallas kernels for 7% -> 7%
where the time goes in v5:
time: 83.8 us; the launch traced here: 83.4 us
  starting transfers between devices  28.9 us (34%)
  blocking collectives  28.1 us (34%)
  waiting for transfers between devices  14.1 us (17%)
  Pallas kernels  10.6 us (13%)
  between operations  0.84 us (1%)
    all_to_all x2, blocking collectives, exchange(): return lax.all_to_all(copies, axis, 0, 0, tiled=True)  28.1 us
    all_to_all x2, starting transfers between devices, exchange(): return lax.all_to_all(copies, axis, 0, 0, tiled=True)  13 us
    pallas_call x12, Pallas kernels, held(): run(*(a if spec is SM or spec is RAW else pltpu.with_memory_space_constra...  10.6 us
    all_to_all x2, waiting for transfers between devices, exchange(): return lax.all_to_all(copies, axis, 0, 0, tiled=True)  10.3 us
    ppermute x3, starting transfers between devices, body(): lax.ppermute(payload, 'col_0', [(chip, (chip + turn) % 4) for chip in ran...  8.46 us
    ppermute x3, waiting for transfers between devices, body(): lax.ppermute(payload, 'col_0', [(chip, (chip + turn) % 4) for chip in ran...  3.4 us
    ppermute x1, starting transfers between devices, body(): lax.ppermute(own_tiles, ROW, [(source, source + 1) for source in range(ro...  2.49 us
    ppermute x1, starting transfers between devices, body(): received = lax.ppermute(send, 'col_1', swap)  2.17 us
  transfers between devices with their start and end apart: 9, of which 5 were waited for; matrix products, arithmetic and copies ran while one was open for 0% of the time, Pallas kernels for 7%

profile of v5, /device:TPU:1, one launch (start us, length us, event | category | flops | bytes accessed | tf_op | source)
XLA Modules:
  0.0 83.4 jit_solution(13486624556652515899)
XLA Ops:
  0.6 0.0 copy-start.4
  0.6 0.7 copy-done.4
  1.3 0.7 copies.1
  2.1 9.2 %all-to-all-start = ((bf16[32,16,256]{2,1,0:T(8,128)(2,1)}), bf16[32,16,256]{2,1,0:T(8,128)(2,1)S(1)}, u32[]{:S(2)}, u32[]{:S(2)}) async-start(bf16[32,16,256]{2,1,0:T(8,128)(2,1)} %get-tuple-element.9), calls=%async_computation | async-start | bytes 524288 | tf_op jit(solution)/shard_map/all_to_all | solution.py:25
  11.3 1.0 %collective-permute-start.1 = (bf16[16,256]{1,0:T(8,128)(2,1)S(1)}, bf16[16,256]{1,0:T(8,128)(2,1)S(1)}, u32[]{:S(2)}, u32[]{:S(2)}) collective-permute-start(bf16[16,256]{1,0:T(8,128)(2,1)S(1)} %get-tuple-element.10), channel_id=1, source_target_pairs={{0,1},{1,0},{2,3},{3,2},{4,5},{5,4},{6,7},{7,6},{8,9},{9,8},{10,11... | collective-permute-start | bytes 24584 | tf_op jit(solution)/shard_map/ppermute | solution.py:290
  12.3 0.0 copy-start.2
  12.3 0.0 copy-start.5
  12.3 1.6 %stage.1.right = bf16[64,64,256]{2,1,0:T(8,128)(2,1)S(1)} custom-call(bf16[64,64,256]{2,1,0:T(8,128)(2,1)} %bitcast.25), custom_call_target="tpu_custom_call" | custom-call | flops 1 | bytes 1048576 | tf_op jit(solution)/shard_map/stage/pallas_call | solution.py:49
  14.0 0.0 copy-done.2
  14.0 0.0 copy-done.5
  14.0 0.9 %prepare.1 = (bf16[128,4096]{1,0:T(8,128)(2,1)S(1)}, f32[8,1,256]{2,1,0:T(1,128)S(1)}) custom-call(s32[1,4096]{1,0:T(1,128)S(1)} %bitcast.20, s32[1,64]{1,0:T(1,128)S(1)} %copy-done.5), custom_call_target="tpu_custom_call" | custom-call | flops 1048576 | bytes 1048576 | tf_op jit(solution)/shard_map/prepare/pallas_call | solution.py:49
  14.9 4.4 %all-to-all-done.columns = bf16[32,16,256]{2,1,0:T(8,128)(2,1)S(1)} async-done(((bf16[32,16,256]{2,1,0:T(8,128)(2,1)}), bf16[32,16,256]{2,1,0:T(8,128)(2,1)S(1)}, u32[]{:S(2)}, u32[]{:S(2)}) %all-to-all-start) | async-done | bytes 262176 | tf_op jit(solution)/shard_map/all_to_all | solution.py:25
  19.3 0.6 send.1
  19.8 0.0 copy-start
  19.9 2.2 %collective-permute-start = (f32[8,8,256]{2,1,0:T(8,128)S(1)}, f32[8,8,256]{2,1,0:T(8,128)S(1)}, u32[]{:S(2)}, u32[]{:S(2)}) collective-permute-start(f32[8,8,256]{2,1,0:T(8,128)S(1)} %send.1), channel_id=1, source_target_pairs={{0,1},{1,0},{2,3},{3,2},{4,5},{5,4},{6,7},{7,6},{8,9},{9,8},{10,11... | collective-permute-start | bytes 196616 | tf_op jit(solution)/shard_map/ppermute | solution.py:309
  22.0 0.0 collective-permute-done.1
  22.1 0.0 copy-start.1
  22.1 0.6 keep.1
  22.7 0.3 collective-permute-done
  23.0 6.1 %collective-permute-start.4 = (f16[96,256]{1,0:T(8,128)(2,1)S(1)}, f16[96,256]{1,0:T(8,128)(2,1)S(1)}, u32[]{:S(2)}, u32[]{:S(2)}) collective-permute-start(f16[96,256]{1,0:T(8,128)(2,1)S(1)} %pad_maximum_fusion), channel_id=1, source_target_pairs={{0,4},{2,6},{4,0},{6,2},{1,5},{3,7},{5,1},{7,3},{8,12},{10,14},{12... | collective-permute-start | bytes 147464 | tf_op jit(solution)/shard_map/ppermute | solution.py:323
  29.1 0.3 collective-permute-start.3
  29.3 2.1 %collective-permute-start.2 = (f16[96,256]{1,0:T(8,128)(2,1)S(1)}, f16[96,256]{1,0:T(8,128)(2,1)S(1)}, u32[]{:S(2)}, u32[]{:S(2)}) collective-permute-start(f16[96,256]{1,0:T(8,128)(2,1)S(1)} %pad_maximum_fusion), channel_id=1, source_target_pairs={{0,2},{2,4},{4,6},{6,0},{1,3},{3,5},{5,7},{7,1},{8,10},{10,12},{12... | collective-permute-start | bytes 147464 | tf_op jit(solution)/shard_map/ppermute | solution.py:323
  31.5 0.0 collective-permute-done.4
  31.5 3.4 %collective-permute-done.3 = f16[96,256]{1,0:T(8,128)(2,1)S(1)} collective-permute-done((f16[96,256]{1,0:T(8,128)(2,1)S(1)}, f16[96,256]{1,0:T(8,128)(2,1)S(1)}, u32[]{:S(2)}, u32[]{:S(2)}) %collective-permute-start.3) | collective-permute-done | bytes 49184 | tf_op jit(solution)/shard_map/ppermute | solution.py:323
  34.9 0.0 collective-permute-done.2
  34.9 1.7 %collective-permute-start.5 = (bf16[8,8,256]{2,1,0:T(8,128)(2,1)S(1)}, bf16[8,8,256]{2,1,0:T(8,128)(2,1)S(1)}, u32[]{:S(2)}, u32[]{:S(2)}) collective-permute-start(bf16[8,8,256]{2,1,0:T(8,128)(2,1)S(1)} %fusion.1.mine), channel_id=1, source_target_pairs={{0,1},{1,0},{2,3},{3,2},{4,5},{5,4},{6,7},{7,6},{8,9},{9,8},{10,11... | collective-permute-start | bytes 98312 | tf_op jit(solution)/shard_map/ppermute | solution.py:328
  36.7 0.0 copy-done
  36.7 0.0 copy-start.3
  36.7 0.0 copy-start.6
  36.7 0.7 ondiag.1.on_diag
  37.4 0.1 collective-permute-done.5.theirs
  37.5 0.0 copy-done.1
  37.5 0.4 samples.1
  37.9 13.4 %all_to_all.20.table = bf16[8,16,256]{2,1,0:T(8,128)(2,1)S(1)} all-to-all(bf16[8,16,256]{2,1,0:T(8,128)(2,1)S(1)} %get-tuple-element.12), channel_id=1, replica_groups=mesh['row_0'=4,'row_1'=2,'row_2'=4,'col_0'=4,'col_1'=2] {'col_0','col_1'}, dimensions={0} | all-to-all | bytes 131072 | tf_op jit(solution)/shard_map/all_to_all | solution.py:25
  51.3 2.5 %collective-permute-start.6 = (bf16[8,16,256]{2,1,0:T(8,128)(2,1)S(1)}, bf16[8,16,256]{2,1,0:T(8,128)(2,1)S(1)}, u32[]{:S(2)}, u32[]{:S(2)}) collective-permute-start(bf16[8,16,256]{2,1,0:T(8,128)(2,1)S(1)} %all_to_all.20.table), channel_id=1, source_target_pairs={{0,8},{8,16},{16,24},{24,32},{32,40},{40,48},{48,56},{56,64},{64,7... | collective-permute-start | bytes 196616 | tf_op jit(solution)/shard_map/ppermute | solution.py:340
  53.8 0.0 copy-done.3
  53.8 0.0 copy-done.6
  53.8 1.7 %own.1.base = f32[8,4096]{1,0:T(8,128)S(1)} custom-call(bf16[8,16,256]{2,1,0:T(8,128)(2,1)S(1)} %all_to_all.20.table, s32[1,4096]{1,0:T(1,128)S(1)} %bitcast.24, s32[1,4096]{1,0:T(1,128)S(1)} %bitcast.21), custom_call_target="tpu_custom_call" | custom-call | flops 67108864 | bytes 1048576 | tf_op jit(solution)/shard_map/own/pallas_call | solution.py:49
  55.5 0.0 collective-permute-done.6.prev
  55.5 1.5 %bins.1 = f32[16,1,1152]{2,1,0:T(1,128)S(1)} custom-call(bf16[8,16,256]{2,1,0:T(8,128)(2,1)S(1)} %collective-permute-done.6.prev, s32[1,4096]{1,0:T(1,128)S(1)} %bitcast.22, f32[8,4096]{1,0:T(8,128)S(1)} %own.1.base, bf16[128,4096]{1,0:T(8,128)(2,1)S(1)} %get-tuple-element.13.onehot), custom_call_target="tpu_custom_call" | custom-call | flops 67108864 | bytes 1048576 | tf_op jit(solution)/shard_map/bins/pallas_call | solution.py:49
  57.0 14.7 %all_to_all.21.parts = f32[16,1,1152]{2,1,0:T(1,128)S(1)} all-to-all(f32[16,1,1152]{2,1,0:T(1,128)S(1)} %bins.1), channel_id=1, replica_groups=mesh['row_0'=4,'row_1'=2,'row_2'=4,'col_0'=4,'col_1'=2] {'row_1','col_0'..., dimensions={0} | all-to-all | bytes 147456 | tf_op jit(solution)/shard_map/all_to_all | solution.py:25
  71.7 0.7 merge.1
  72.4 3.8 %all-to-all-start.3 = ((f32[16,1,1152]{2,1,0:T(1,128)}), f32[16,1,1152]{2,1,0:T(1,128)S(1)}, u32[]{:S(2)}, u32[]{:S(2)}) async-start(f32[16,1,1152]{2,1,0:T(1,128)} %merge.1), calls=%async_computation.3 | async-start | bytes 147456 | tf_op jit(solution)/shard_map/all_to_all | solution.py:25
  76.2 0.6 emit.1
  76.8 5.9 %all-to-all-done.3.parts = f32[16,1,1152]{2,1,0:T(1,128)S(1)} async-done(((f32[16,1,1152]{2,1,0:T(1,128)}), f32[16,1,1152]{2,1,0:T(1,128)S(1)}, u32[]{:S(2)}, u32[]{:S(2)}) %all-to-all-start.3) | async-done | bytes 73760 | tf_op jit(solution)/shard_map/all_to_all | solution.py:25
  82.8 0.6 finish.1
  (9 shorter events, 0.1 us)
Async XLA Ops:
  0.6 0.7 copy-start.4
  2.1 17.2 %all-to-all-start = ((bf16[32,16,256]{2,1,0:T(8,128)(2,1)}), bf16[32,16,256]{2,1,0:T(8,128)(2,1)S(1)}, u32[]{:S(2)}, u32[]{:S(2)}) async-start(bf16[32,16,256]{2,1,0:T(8,128)(2,1)} %get-tuple-element.9), calls=%async_computation | async-start | bytes 524288 | tf_op jit(solution)/shard_map/all_to_all | solution.py:25
  11.3 10.8 %collective-permute-start.1 = (bf16[16,256]{1,0:T(8,128)(2,1)S(1)}, bf16[16,256]{1,0:T(8,128)(2,1)S(1)}, u32[]{:S(2)}, u32[]{:S(2)}) collective-permute-start(bf16[16,256]{1,0:T(8,128)(2,1)S(1)} %get-tuple-element.10), channel_id=1, source_target_pairs={{0,1},{1,0},{2,3},{3,2},{4,5},{5,4},{6,7},{7,6},{8,9},{9,8},{10,11... | collective-permute-start | bytes 24584 | tf_op jit(solution)/shard_map/ppermute | solution.py:290
  12.3 1.6 %copy-start.2 = (s32[1,1,4096]{2,1,0:T(1,128)S(1)}, s32[1,1,4096]{2,1,0:T(1,128)}, u32[]{:S(2)}) copy-start(s32[1,1,4096]{2,1,0:T(1,128)} %param.15) | copy-start | bytes 49156
  12.3 1.7 %copy-start.5 = (s32[1,64]{1,0:T(1,128)S(1)}, s32[1,64]{1,0:T(1,128)}, u32[]{:S(2)}) copy-start(s32[1,64]{1,0:T(1,128)} %ranks.1) | copy-start | bytes 772
  19.8 16.8 %copy-start = (bf16[2,1,256,2048]{3,2,1,0:T(8,128)(2,1)S(1)}, bf16[2,1,256,2048]{3,2,1,0:T(8,128)(2,1)}, u32[]{:S(2)}) copy-start(bf16[2,1,256,2048]{3,2,1,0:T(8,128)(2,1)} %param.9) | copy-start | bytes 6291460
  19.9 3.1 %collective-permute-start = (f32[8,8,256]{2,1,0:T(8,128)S(1)}, f32[8,8,256]{2,1,0:T(8,128)S(1)}, u32[]{:S(2)}, u32[]{:S(2)}) collective-permute-start(f32[8,8,256]{2,1,0:T(8,128)S(1)} %send.1), channel_id=1, source_target_pairs={{0,1},{1,0},{2,3},{3,2},{4,5},{5,4},{6,7},{7,6},{8,9},{9,8},{10,11... | collective-permute-start | bytes 196616 | tf_op jit(solution)/shard_map/ppermute | solution.py:309
  22.1 15.4 %copy-start.1 = (bf16[1,64,64,256]{3,2,1,0:T(8,128)(2,1)S(1)}, bf16[1,64,64,256]{3,2,1,0:T(8,128)(2,1)}, u32[]{:S(2)}) copy-start(bf16[1,64,64,256]{3,2,1,0:T(8,128)(2,1)} %param.10) | copy-start | bytes 6291460
  23.0 8.5 %collective-permute-start.4 = (f16[96,256]{1,0:T(8,128)(2,1)S(1)}, f16[96,256]{1,0:T(8,128)(2,1)S(1)}, u32[]{:S(2)}, u32[]{:S(2)}) collective-permute-start(f16[96,256]{1,0:T(8,128)(2,1)S(1)} %pad_maximum_fusion), channel_id=1, source_target_pairs={{0,4},{2,6},{4,0},{6,2},{1,5},{3,7},{5,1},{7,3},{8,12},{10,14},{12... | collective-permute-start | bytes 147464 | tf_op jit(solution)/shard_map/ppermute | solution.py:323
  29.1 5.8 %collective-permute-start.3 = (f16[96,256]{1,0:T(8,128)(2,1)S(1)}, f16[96,256]{1,0:T(8,128)(2,1)S(1)}, u32[]{:S(2)}, u32[]{:S(2)}) collective-permute-start(f16[96,256]{1,0:T(8,128)(2,1)S(1)} %pad_maximum_fusion), channel_id=1, source_target_pairs={{0,6},{2,0},{4,2},{6,4},{1,7},{3,1},{5,3},{7,5},{8,14},{10,8},{12,... | collective-permute-start | bytes 147464 | tf_op jit(solution)/shard_map/ppermute | solution.py:323
  29.3 5.5 %collective-permute-start.2 = (f16[96,256]{1,0:T(8,128)(2,1)S(1)}, f16[96,256]{1,0:T(8,128)(2,1)S(1)}, u32[]{:S(2)}, u32[]{:S(2)}) collective-permute-start(f16[96,256]{1,0:T(8,128)(2,1)S(1)} %pad_maximum_fusion), channel_id=1, source_target_pairs={{0,2},{2,4},{4,6},{6,0},{1,3},{3,5},{5,7},{7,1},{8,10},{10,12},{12... | collective-permute-start | bytes 147464 | tf_op jit(solution)/shard_map/ppermute | solution.py:323
  34.9 2.6 %collective-permute-start.5 = (bf16[8,8,256]{2,1,0:T(8,128)(2,1)S(1)}, bf16[8,8,256]{2,1,0:T(8,128)(2,1)S(1)}, u32[]{:S(2)}, u32[]{:S(2)}) collective-permute-start(bf16[8,8,256]{2,1,0:T(8,128)(2,1)S(1)} %fusion.1.mine), channel_id=1, source_target_pairs={{0,1},{1,0},{2,3},{3,2},{4,5},{5,4},{6,7},{7,6},{8,9},{9,8},{10,11... | collective-permute-start | bytes 98312 | tf_op jit(solution)/shard_map/ppermute | solution.py:328
  36.7 17.1 %copy-start.3 = (s32[1,1,4096]{2,1,0:T(1,128)S(1)}, s32[1,1,4096]{2,1,0:T(1,128)}, u32[]{:S(2)}) copy-start(s32[1,1,4096]{2,1,0:T(1,128)} %param.14) | copy-start | bytes 49156
  36.7 17.1 %copy-start.6 = (s32[1,1,4096]{2,1,0:T(1,128)S(1)}, s32[1,1,4096]{2,1,0:T(1,128)}, u32[]{:S(2)}) copy-start(s32[1,1,4096]{2,1,0:T(1,128)} %param.13) | copy-start | bytes 49156
  51.3 4.2 %collective-permute-start.6 = (bf16[8,16,256]{2,1,0:T(8,128)(2,1)S(1)}, bf16[8,16,256]{2,1,0:T(8,128)(2,1)S(1)}, u32[]{:S(2)}, u32[]{:S(2)}) collective-permute-start(bf16[8,16,256]{2,1,0:T(8,128)(2,1)S(1)} %all_to_all.20.table), channel_id=1, source_target_pairs={{0,8},{8,16},{16,24},{24,32},{32,40},{40,48},{48,56},{56,64},{64,7... | collective-permute-start | bytes 196616 | tf_op jit(solution)/shard_map/ppermute | solution.py:340
  72.4 10.3 %all-to-all-start.3 = ((f32[16,1,1152]{2,1,0:T(1,128)}), f32[16,1,1152]{2,1,0:T(1,128)S(1)}, u32[]{:S(2)}, u32[]{:S(2)}) async-start(f32[16,1,1152]{2,1,0:T(1,128)} %merge.1), calls=%async_computation.3 | async-start | bytes 147456 | tf_op jit(solution)/shard_map/all_to_all | solution.py:25

commit v6 on v5

--- a/solution.py
+++ b/solution.py
@@ -17,7 +17,7 @@
 F16 = jnp.float16
 SUM_UNIT = 128.0
 NOISE_UNIT = 1024.0
-TURNS = (1, 3, 2)
+TURNS = (2, 1, 3)
 BF16 = jnp.bfloat16
 
 
@@ -31,7 +31,6 @@
 
 HB = pl.BlockSpec(memory_space=pltpu.HBM)
 VM = pl.BlockSpec(memory_space=pltpu.VMEM)
-RAW = pl.BlockSpec(memory_space=pltpu.VMEM)
 SM = pl.BlockSpec(memory_space=pltpu.SMEM)
 
 
@@ -48,7 +47,7 @@
     def held(*args):
         return run(
             *(
-                a if spec is SM or spec is RAW else pltpu.with_memory_space_constraint(a, spec.memory_space)
+                a if spec is SM else pltpu.with_memory_space_constraint(a, spec.memory_space)
                 for a, spec in zip(args, in_specs)
             )
         )
@@ -56,7 +55,10 @@
     return held
 
 
-def copies_kernel(noise, local, out):
+def copies_kernel(source, local, out, noise, sem):
+    copy = pltpu.make_async_copy(source, noise, sem)
+    copy.start()
+    copy.wait()
     rows = [noise[s].astype(F32)[h : h + 1] for h in range(2) for s in range(8)]
     mine = jnp.concatenate(rows, axis=0).astype(BF16)
     local[...] = mine
@@ -276,7 +278,8 @@
     local, spread_noise = call(
         copies_kernel,
         (vmem((16, span), BF16), vmem((rows, 16, span), BF16)),
-        [RAW],
+        [HB],
+        scratch_shapes=[pltpu.VMEM((8, 2, span), BF16), pltpu.SemaphoreType.DMA(())],
         name="copies",
     )(jnp.transpose(noise, (0, 2, 1, 3))[:, 0])
     columns = exchange(spread_noise, ROW)

time: 83.8 us -> 84.1 us (level)
  transfers between devices with their start and end apart: 9 -> 9, of which waited for: 5 -> 6; matrix products, arithmetic and copies ran while one was open for 0% -> 0% of each run, Pallas kernels for 7% -> 7%
where the time goes in v6:
time: 84.1 us; the launch traced here: 83.7 us
  starting transfers between devices  29 us (34%)
  blocking collectives  27.8 us (33%)
  waiting for transfers between devices  14.5 us (17%)
  Pallas kernels  11.4 us (14%)
    all_to_all x2, blocking collectives, exchange(): return lax.all_to_all(copies, axis, 0, 0, tiled=True)  27.8 us
    all_to_all x2, starting transfers between devices, exchange(): return lax.all_to_all(copies, axis, 0, 0, tiled=True)  13.3 us
    pallas_call x12, Pallas kernels, held(): run(*(a if spec is SM else pltpu.with_memory_space_constraint(a, spec.mem...  11.4 us
    all_to_all x2, waiting for transfers between devices, exchange(): return lax.all_to_all(copies, axis, 0, 0, tiled=True)  10.3 us
    ppermute x3, starting transfers between devices, body(): lax.ppermute(payload, 'col_0', [(chip, (chip + turn) % 4) for chip in ran...  8.45 us
    ppermute x3, waiting for transfers between devices, body(): lax.ppermute(payload, 'col_0', [(chip, (chip + turn) % 4) for chip in ran...  3.87 us
    ppermute x1, starting transfers between devices, body(): lax.ppermute(own_tiles, ROW, [(source, source + 1) for source in range(ro...  2.46 us
    ppermute x1, starting transfers between devices, body(): received = lax.ppermute(send, 'col_1', swap)  2.17 us
  transfers between devices with their start and end apart: 9, of which 6 were waited for; matrix products, arithmetic and copies ran while one was open for 0% of the time, Pallas kernels for 7%

profile of v6, /device:TPU:1, one launch (start us, length us, event | category | flops | bytes accessed | tf_op | source)
XLA Modules:
  0.0 83.7 jit_solution(14173481701900431202)
XLA Ops:
  0.6 1.4 %copies.1 = (bf16[16,256]{1,0:T(8,128)(2,1)S(1)}, bf16[32,16,256]{2,1,0:T(8,128)(2,1)}) custom-call(bf16[8,2,256]{2,1,0:T(2,128)(2,1)} %bitcast.26), custom_call_target="tpu_custom_call" | custom-call | flops 1 | bytes 1048576 | tf_op jit(solution)/shard_map/copies/pallas_call | solution.py:48
  2.1 9.2 %all-to-all-start = ((bf16[32,16,256]{2,1,0:T(8,128)(2,1)}), bf16[32,16,256]{2,1,0:T(8,128)(2,1)S(1)}, u32[]{:S(2)}, u32[]{:S(2)}) async-start(bf16[32,16,256]{2,1,0:T(8,128)(2,1)} %get-tuple-element.9), calls=%async_computation | async-start | bytes 524288 | tf_op jit(solution)/shard_map/all_to_all | solution.py:25
  11.3 1.0 %collective-permute-start.1 = (bf16[16,256]{1,0:T(8,128)(2,1)S(1)}, bf16[16,256]{1,0:T(8,128)(2,1)S(1)}, u32[]{:S(2)}, u32[]{:S(2)}) collective-permute-start(bf16[16,256]{1,0:T(8,128)(2,1)S(1)} %get-tuple-element.10), channel_id=1, source_target_pairs={{0,1},{1,0},{2,3},{3,2},{4,5},{5,4},{6,7},{7,6},{8,9},{9,8},{10,11... | collective-permute-start | bytes 24584 | tf_op jit(solution)/shard_map/ppermute | solution.py:293
  12.3 0.0 copy-start.2
  12.3 0.0 copy-start.4
  12.3 1.6 %stage.1.right = bf16[64,64,256]{2,1,0:T(8,128)(2,1)S(1)} custom-call(bf16[64,64,256]{2,1,0:T(8,128)(2,1)} %bitcast.24), custom_call_target="tpu_custom_call" | custom-call | flops 1 | bytes 1048576 | tf_op jit(solution)/shard_map/stage/pallas_call | solution.py:48
  14.0 0.0 copy-done.2
  14.0 0.0 copy-done.4
  14.0 0.9 %prepare.1 = (bf16[128,4096]{1,0:T(8,128)(2,1)S(1)}, f32[8,1,256]{2,1,0:T(1,128)S(1)}) custom-call(s32[1,4096]{1,0:T(1,128)S(1)} %bitcast.20, s32[1,64]{1,0:T(1,128)S(1)} %copy-done.4), custom_call_target="tpu_custom_call" | custom-call | flops 1048576 | bytes 1048576 | tf_op jit(solution)/shard_map/prepare/pallas_call | solution.py:48
  14.9 4.4 %all-to-all-done.columns = bf16[32,16,256]{2,1,0:T(8,128)(2,1)S(1)} async-done(((bf16[32,16,256]{2,1,0:T(8,128)(2,1)}), bf16[32,16,256]{2,1,0:T(8,128)(2,1)S(1)}, u32[]{:S(2)}, u32[]{:S(2)}) %all-to-all-start) | async-done | bytes 262176 | tf_op jit(solution)/shard_map/all_to_all | solution.py:25
  19.3 0.6 send.1
  19.9 0.0 copy-start
  19.9 2.2 %collective-permute-start = (f32[8,8,256]{2,1,0:T(8,128)S(1)}, f32[8,8,256]{2,1,0:T(8,128)S(1)}, u32[]{:S(2)}, u32[]{:S(2)}) collective-permute-start(f32[8,8,256]{2,1,0:T(8,128)S(1)} %send.1), channel_id=1, source_target_pairs={{0,1},{1,0},{2,3},{3,2},{4,5},{5,4},{6,7},{7,6},{8,9},{9,8},{10,11... | collective-permute-start | bytes 196616 | tf_op jit(solution)/shard_map/ppermute | solution.py:312
  22.1 0.0 collective-permute-done.1
  22.1 0.0 copy-start.1
  22.1 0.6 keep.1
  22.7 0.3 collective-permute-done
  23.0 5.2 %collective-permute-start.4 = (f16[96,256]{1,0:T(8,128)(2,1)S(1)}, f16[96,256]{1,0:T(8,128)(2,1)S(1)}, u32[]{:S(2)}, u32[]{:S(2)}) collective-permute-start(f16[96,256]{1,0:T(8,128)(2,1)S(1)} %pad_maximum_fusion), channel_id=1, source_target_pairs={{0,6},{2,0},{4,2},{6,4},{1,7},{3,1},{5,3},{7,5},{8,14},{10,8},{12,... | collective-permute-start | bytes 147464 | tf_op jit(solution)/shard_map/ppermute | solution.py:326
  28.2 0.0 collective-permute-start.3
  28.2 3.3 %collective-permute-start.2 = (f16[96,256]{1,0:T(8,128)(2,1)S(1)}, f16[96,256]{1,0:T(8,128)(2,1)S(1)}, u32[]{:S(2)}, u32[]{:S(2)}) collective-permute-start(f16[96,256]{1,0:T(8,128)(2,1)S(1)} %pad_maximum_fusion), channel_id=1, source_target_pairs={{0,4},{2,6},{4,0},{6,2},{1,5},{3,7},{5,1},{7,3},{8,12},{10,14},{12... | collective-permute-start | bytes 147464 | tf_op jit(solution)/shard_map/ppermute | solution.py:326
  31.5 0.0 collective-permute-done.4
  31.5 2.3 %collective-permute-done.3 = f16[96,256]{1,0:T(8,128)(2,1)S(1)} collective-permute-done((f16[96,256]{1,0:T(8,128)(2,1)S(1)}, f16[96,256]{1,0:T(8,128)(2,1)S(1)}, u32[]{:S(2)}, u32[]{:S(2)}) %collective-permute-start.3) | collective-permute-done | bytes 49184 | tf_op jit(solution)/shard_map/ppermute | solution.py:326
  33.8 1.5 %collective-permute-done.2 = f16[96,256]{1,0:T(8,128)(2,1)S(1)} collective-permute-done((f16[96,256]{1,0:T(8,128)(2,1)S(1)}, f16[96,256]{1,0:T(8,128)(2,1)S(1)}, u32[]{:S(2)}, u32[]{:S(2)}) %collective-permute-start.2) | collective-permute-done | bytes 49184 | tf_op jit(solution)/shard_map/ppermute | solution.py:326
  35.4 1.6 %collective-permute-start.5 = (bf16[8,8,256]{2,1,0:T(8,128)(2,1)S(1)}, bf16[8,8,256]{2,1,0:T(8,128)(2,1)S(1)}, u32[]{:S(2)}, u32[]{:S(2)}) collective-permute-start(bf16[8,8,256]{2,1,0:T(8,128)(2,1)S(1)} %fusion.1.mine), channel_id=1, source_target_pairs={{0,1},{1,0},{2,3},{3,2},{4,5},{5,4},{6,7},{7,6},{8,9},{9,8},{10,11... | collective-permute-start | bytes 98312 | tf_op jit(solution)/shard_map/ppermute | solution.py:331
  37.0 0.0 copy-done
  37.0 0.0 copy-start.3
  37.0 0.0 copy-start.5
  37.0 0.7 ondiag.1.on_diag
  37.8 0.1 collective-permute-done.5.theirs
  37.8 0.0 copy-done.1
  37.8 0.4 samples.1
  38.2 13.3 %all_to_all.20.table = bf16[8,16,256]{2,1,0:T(8,128)(2,1)S(1)} all-to-all(bf16[8,16,256]{2,1,0:T(8,128)(2,1)S(1)} %get-tuple-element.12), channel_id=1, replica_groups=mesh['row_0'=4,'row_1'=2,'row_2'=4,'col_0'=4,'col_1'=2] {'col_0','col_1'}, dimensions={0} | all-to-all | bytes 131072 | tf_op jit(solution)/shard_map/all_to_all | solution.py:25
  51.5 2.5 %collective-permute-start.6 = (bf16[8,16,256]{2,1,0:T(8,128)(2,1)S(1)}, bf16[8,16,256]{2,1,0:T(8,128)(2,1)S(1)}, u32[]{:S(2)}, u32[]{:S(2)}) collective-permute-start(bf16[8,16,256]{2,1,0:T(8,128)(2,1)S(1)} %all_to_all.20.table), channel_id=1, source_target_pairs={{0,8},{8,16},{16,24},{24,32},{32,40},{40,48},{48,56},{56,64},{64,7... | collective-permute-start | bytes 196616 | tf_op jit(solution)/shard_map/ppermute | solution.py:343
  54.0 0.0 copy-done.3
  54.0 0.0 copy-done.5
  54.0 1.7 %own.1.base = f32[8,4096]{1,0:T(8,128)S(1)} custom-call(bf16[8,16,256]{2,1,0:T(8,128)(2,1)S(1)} %all_to_all.20.table, s32[1,4096]{1,0:T(1,128)S(1)} %bitcast.23, s32[1,4096]{1,0:T(1,128)S(1)} %bitcast.21), custom_call_target="tpu_custom_call" | custom-call | flops 67108864 | bytes 1048576 | tf_op jit(solution)/shard_map/own/pallas_call | solution.py:48
  55.7 0.0 collective-permute-done.6.prev
  55.7 1.5 %bins.1 = f32[16,1,1152]{2,1,0:T(1,128)S(1)} custom-call(bf16[8,16,256]{2,1,0:T(8,128)(2,1)S(1)} %collective-permute-done.6.prev, s32[1,4096]{1,0:T(1,128)S(1)} %bitcast.22, f32[8,4096]{1,0:T(8,128)S(1)} %own.1.base, bf16[128,4096]{1,0:T(8,128)(2,1)S(1)} %get-tuple-element.13.onehot), custom_call_target="tpu_custom_call" | custom-call | flops 67108864 | bytes 1048576 | tf_op jit(solution)/shard_map/bins/pallas_call | solution.py:48
  57.3 14.5 %all_to_all.21.parts = f32[16,1,1152]{2,1,0:T(1,128)S(1)} all-to-all(f32[16,1,1152]{2,1,0:T(1,128)S(1)} %bins.1), channel_id=1, replica_groups=mesh['row_0'=4,'row_1'=2,'row_2'=4,'col_0'=4,'col_1'=2] {'row_1','col_0'..., dimensions={0} | all-to-all | bytes 147456 | tf_op jit(solution)/shard_map/all_to_all | solution.py:25
  71.8 0.7 merge.1
  72.5 4.0 %all-to-all-start.3 = ((f32[16,1,1152]{2,1,0:T(1,128)}), f32[16,1,1152]{2,1,0:T(1,128)S(1)}, u32[]{:S(2)}, u32[]{:S(2)}) async-start(f32[16,1,1152]{2,1,0:T(1,128)} %merge.1), calls=%async_computation.3 | async-start | bytes 147456 | tf_op jit(solution)/shard_map/all_to_all | solution.py:25
  76.5 0.6 emit.1
  77.1 5.9 %all-to-all-done.3.parts = f32[16,1,1152]{2,1,0:T(1,128)S(1)} async-done(((f32[16,1,1152]{2,1,0:T(1,128)}), f32[16,1,1152]{2,1,0:T(1,128)S(1)}, u32[]{:S(2)}, u32[]{:S(2)}) %all-to-all-start.3) | async-done | bytes 73760 | tf_op jit(solution)/shard_map/all_to_all | solution.py:25
  83.1 0.6 finish.1
  (9 shorter events, 0.1 us)
Async XLA Ops:
  2.1 17.2 %all-to-all-start = ((bf16[32,16,256]{2,1,0:T(8,128)(2,1)}), bf16[32,16,256]{2,1,0:T(8,128)(2,1)S(1)}, u32[]{:S(2)}, u32[]{:S(2)}) async-start(bf16[32,16,256]{2,1,0:T(8,128)(2,1)} %get-tuple-element.9), calls=%async_computation | async-start | bytes 524288 | tf_op jit(solution)/shard_map/all_to_all | solution.py:25
  11.3 10.8 %collective-permute-start.1 = (bf16[16,256]{1,0:T(8,128)(2,1)S(1)}, bf16[16,256]{1,0:T(8,128)(2,1)S(1)}, u32[]{:S(2)}, u32[]{:S(2)}) collective-permute-start(bf16[16,256]{1,0:T(8,128)(2,1)S(1)} %get-tuple-element.10), channel_id=1, source_target_pairs={{0,1},{1,0},{2,3},{3,2},{4,5},{5,4},{6,7},{7,6},{8,9},{9,8},{10,11... | collective-permute-start | bytes 24584 | tf_op jit(solution)/shard_map/ppermute | solution.py:293
  12.3 1.6 %copy-start.2 = (s32[1,1,4096]{2,1,0:T(1,128)S(1)}, s32[1,1,4096]{2,1,0:T(1,128)}, u32[]{:S(2)}) copy-start(s32[1,1,4096]{2,1,0:T(1,128)} %param.15) | copy-start | bytes 49156
  12.3 1.7 %copy-start.4 = (s32[1,64]{1,0:T(1,128)S(1)}, s32[1,64]{1,0:T(1,128)}, u32[]{:S(2)}) copy-start(s32[1,64]{1,0:T(1,128)} %ranks.1) | copy-start | bytes 772
  19.9 17.1 %copy-start = (bf16[2,1,256,2048]{3,2,1,0:T(8,128)(2,1)S(1)}, bf16[2,1,256,2048]{3,2,1,0:T(8,128)(2,1)}, u32[]{:S(2)}) copy-start(bf16[2,1,256,2048]{3,2,1,0:T(8,128)(2,1)} %param.9) | copy-start | bytes 6291460
  19.9 3.1 %collective-permute-start = (f32[8,8,256]{2,1,0:T(8,128)S(1)}, f32[8,8,256]{2,1,0:T(8,128)S(1)}, u32[]{:S(2)}, u32[]{:S(2)}) collective-permute-start(f32[8,8,256]{2,1,0:T(8,128)S(1)} %send.1), channel_id=1, source_target_pairs={{0,1},{1,0},{2,3},{3,2},{4,5},{5,4},{6,7},{7,6},{8,9},{9,8},{10,11... | collective-permute-start | bytes 196616 | tf_op jit(solution)/shard_map/ppermute | solution.py:312
  22.1 15.8 %copy-start.1 = (bf16[1,64,64,256]{3,2,1,0:T(8,128)(2,1)S(1)}, bf16[1,64,64,256]{3,2,1,0:T(8,128)(2,1)}, u32[]{:S(2)}) copy-start(bf16[1,64,64,256]{3,2,1,0:T(8,128)(2,1)} %param.10) | copy-start | bytes 6291460
  23.0 8.5 %collective-permute-start.4 = (f16[96,256]{1,0:T(8,128)(2,1)S(1)}, f16[96,256]{1,0:T(8,128)(2,1)S(1)}, u32[]{:S(2)}, u32[]{:S(2)}) collective-permute-start(f16[96,256]{1,0:T(8,128)(2,1)S(1)} %pad_maximum_fusion), channel_id=1, source_target_pairs={{0,6},{2,0},{4,2},{6,4},{1,7},{3,1},{5,3},{7,5},{8,14},{10,8},{12,... | collective-permute-start | bytes 147464 | tf_op jit(solution)/shard_map/ppermute | solution.py:326
  28.2 5.6 %collective-permute-start.3 = (f16[96,256]{1,0:T(8,128)(2,1)S(1)}, f16[96,256]{1,0:T(8,128)(2,1)S(1)}, u32[]{:S(2)}, u32[]{:S(2)}) collective-permute-start(f16[96,256]{1,0:T(8,128)(2,1)S(1)} %pad_maximum_fusion), channel_id=1, source_target_pairs={{0,2},{2,4},{4,6},{6,0},{1,3},{3,5},{5,7},{7,1},{8,10},{10,12},{12... | collective-permute-start | bytes 147464 | tf_op jit(solution)/shard_map/ppermute | solution.py:326
  28.2 7.2 %collective-permute-start.2 = (f16[96,256]{1,0:T(8,128)(2,1)S(1)}, f16[96,256]{1,0:T(8,128)(2,1)S(1)}, u32[]{:S(2)}, u32[]{:S(2)}) collective-permute-start(f16[96,256]{1,0:T(8,128)(2,1)S(1)} %pad_maximum_fusion), channel_id=1, source_target_pairs={{0,4},{2,6},{4,0},{6,2},{1,5},{3,7},{5,1},{7,3},{8,12},{10,14},{12... | collective-permute-start | bytes 147464 | tf_op jit(solution)/shard_map/ppermute | solution.py:326
  35.4 2.4 %collective-permute-start.5 = (bf16[8,8,256]{2,1,0:T(8,128)(2,1)S(1)}, bf16[8,8,256]{2,1,0:T(8,128)(2,1)S(1)}, u32[]{:S(2)}, u32[]{:S(2)}) collective-permute-start(bf16[8,8,256]{2,1,0:T(8,128)(2,1)S(1)} %fusion.1.mine), channel_id=1, source_target_pairs={{0,1},{1,0},{2,3},{3,2},{4,5},{5,4},{6,7},{7,6},{8,9},{9,8},{10,11... | collective-permute-start | bytes 98312 | tf_op jit(solution)/shard_map/ppermute | solution.py:331
  37.0 17.0 %copy-start.3 = (s32[1,1,4096]{2,1,0:T(1,128)S(1)}, s32[1,1,4096]{2,1,0:T(1,128)}, u32[]{:S(2)}) copy-start(s32[1,1,4096]{2,1,0:T(1,128)} %param.14) | copy-start | bytes 49156
  37.0 17.0 %copy-start.5 = (s32[1,1,4096]{2,1,0:T(1,128)S(1)}, s32[1,1,4096]{2,1,0:T(1,128)}, u32[]{:S(2)}) copy-start(s32[1,1,4096]{2,1,0:T(1,128)} %param.13) | copy-start | bytes 49156
  51.5 4.2 %collective-permute-start.6 = (bf16[8,16,256]{2,1,0:T(8,128)(2,1)S(1)}, bf16[8,16,256]{2,1,0:T(8,128)(2,1)S(1)}, u32[]{:S(2)}, u32[]{:S(2)}) collective-permute-start(bf16[8,16,256]{2,1,0:T(8,128)(2,1)S(1)} %all_to_all.20.table), channel_id=1, source_target_pairs={{0,8},{8,16},{16,24},{24,32},{32,40},{40,48},{48,56},{56,64},{64,7... | collective-permute-start | bytes 196616 | tf_op jit(solution)/shard_map/ppermute | solution.py:343
  72.5 10.6 %all-to-all-start.3 = ((f32[16,1,1152]{2,1,0:T(1,128)}), f32[16,1,1152]{2,1,0:T(1,128)S(1)}, u32[]{:S(2)}, u32[]{:S(2)}) async-start(f32[16,1,1152]{2,1,0:T(1,128)} %merge.1), calls=%async_computation.3 | async-start | bytes 147456 | tf_op jit(solution)/shard_map/all_to_all | solution.py:25

commit v7 on v6

--- a/solution.py
+++ b/solution.py
@@ -66,7 +66,7 @@
         out[n] = mine
 
 
-def prepare_kernel(bins, ranks, onehot, keep):
+def prepare_kernel(bins, ranks, onehot, keep, counts):
     core = lax.axis_index("col_1")
     lane = lax.broadcasted_iota(jnp.int32, (1, 256), 1)
     for i in range(keep.shape[0]):
@@ -84,42 +84,47 @@
         return carry
 
     lax.fori_loop(0, bins.shape[1] // 128, step, 0, unroll=4)
-
-
-def stage_kernel(source, out, sem):
-    copy = pltpu.make_async_copy(source, out, sem)
-    copy.start()
-    copy.wait()
-
-
-def project_kernel(columns, right, out, *, away):
+    counts[...] = nt_dot(jnp.ones((8, onehot.shape[1]), BF16), onehot[...])
+
+
+def order_kernel(local, other, out):
+    first = lax.axis_index("col_1") == 0
+    own = local[...].astype(F32)
+    far = other[...].astype(F32)
+    out[:16] = jnp.where(first, own, far).astype(BF16)
+    out[16:] = jnp.where(first, far, own).astype(BF16)
+
+
+def project_kernel(columns, right, out, factors, sems, *, away):
     row, core = lax.axis_index(ROW), lax.axis_index("col_1")
     half = 1 - core if away else core
     tiles = 2 * columns.shape[0]
-    groups = right.shape[0] // 8
+    groups = out.shape[0]
     lane = lax.broadcasted_iota(jnp.int32, (8, 128), 1)
-
-    def step(g, carry):
-        base = (half * groups + g) * 4
+    base = half * groups * 4
+    loads = [
+        pltpu.make_async_copy(right.at[pl.ds(base + 4 * g, 4)], factors.at[g], sems.at[g])
+        for g in range(groups)
+    ]
+    for load in loads:
+        load.start()
+    for g in range(groups):
         blocks = []
         low = []
         for n in range(4):
-            slot = base + n
+            slot = base + 4 * g + n
             tile = jnp.where(slot < row, slot, slot - row)
             first = tile < tiles // 2
             blocks.append(columns[jnp.where(first, tile, tiles - 1 - tile)])
             low.append(first)
-        factor = right[pl.ds(base, 4)].reshape(256, 256)
-        full = nt_dot(jnp.concatenate(blocks, axis=0), factor)
+        loads[g].wait()
+        full = nt_dot(jnp.concatenate(blocks, axis=0), factors[g].reshape(256, 256))
         parts = []
         for n in range(4):
             cols = full[16 * n : 16 * n + 16, 128 * (n // 2) : 128 * (n // 2) + 128]
             parts.append(jnp.where(low[n], cols[:8], cols[8:]))
         out[g, :, :128] = jnp.where(lane < 64, parts[0], parts[1])
         out[g, :, 128:] = jnp.where(lane < 64, parts[2], parts[3])
-        return carry
-
-    lax.fori_loop(0, groups, step, 0, unroll=4)
 
 
 def on_diag_kernel(n0, n1, n2, n3, diag, out):
@@ -224,7 +229,7 @@
             out[n, :, 128 * i : 128 * i + 128] = rows[i]
 
 
-def bin_kernel(prev, partner, base, onehot, out, words, pieces):
+def bin_kernel(prev, partner, base, onehot, counts, out, words, pieces):
     unit = pack(prev, words)
 
     def step(n, carry):
@@ -233,16 +238,13 @@
         differ = base[:, pl.ds(at, 128)] - jnp.where(b < 4096, lookup(words, unit, b), 0.0)
         value = 0.5 * differ * differ
         top = value.astype(BF16).astype(F32)
-        rest = value - top
-        mid = rest.astype(BF16).astype(F32)
-        stack = jnp.concatenate([top, mid, rest - mid, jnp.ones_like(value)], axis=0)
-        pieces[:, pl.ds(at, 128)] = stack.astype(BF16)
+        pieces[:, pl.ds(at, 128)] = jnp.concatenate([top, value - top], axis=0).astype(BF16)
         return carry
 
     lax.fori_loop(0, partner.shape[1] // 128, step, 0, unroll=8)
     total = nt_dot(pieces[...], onehot[...])
-    sums = (total[:8] + total[8:16]) + total[16:24]
-    put_rows(out, [sums[i : i + 1] for i in range(8)] + [total[24:25]])
+    sums = total[:8] + total[8:]
+    put_rows(out, [sums[i : i + 1] for i in range(8)] + [counts[:1]])
 
 
 def added(parts):
@@ -283,28 +285,23 @@
         name="copies",
     )(jnp.transpose(noise, (0, 2, 1, 3))[:, 0])
     columns = exchange(spread_noise, ROW)
-    onehot, allowed = call(
+    onehot, allowed, counts = call(
         prepare_kernel,
-        (vmem((NBIN, pairs), BF16), vmem((8, 1, 256), F32)),
+        (vmem((NBIN, pairs), BF16), vmem((8, 1, 256), F32), vmem((8, NBIN), F32)),
         [VM, SM],
         flops=1 << 20,
         name="prepare",
     )(bins, tile_ranks)
     other_noise = lax.ppermute(local, "col_1", swap)
-    right = call(
-        stage_kernel,
-        vmem(right_factor.shape[1:], BF16),
-        [HB],
-        scratch_shapes=[pltpu.SemaphoreType.DMA(())],
-        name="stage",
-    )(right_factor[0])
+    right = right_factor[0]
 
     def project(away, name):
         return call(
             functools.partial(project_kernel, away=away),
             vmem((8, 8, 256), F32),
-            [VM, VM],
+            [VM, HB],
             flops=1 << 28,
+            scratch_shapes=[pltpu.VMEM((8, 4, 64, span), BF16), pltpu.SemaphoreType.DMA((8,))],
             name=name,
         )(columns, right)
 
@@ -312,12 +309,7 @@
     received = lax.ppermute(send, "col_1", swap)
     keep = project(False, "keep")
     pair = keep + received
-    low_first = lax.axis_index("col_1") == 0
-    noises = jnp.where(
-        low_first,
-        jnp.concatenate([local, other_noise]),
-        jnp.concatenate([other_noise, local]),
-    )
+    noises = call(order_kernel, vmem((32, span), BF16), [VM, VM], name="order")(local, other_noise)
     noises16 = (noises.astype(F32) * NOISE_UNIT).astype(F16)
     payload = jnp.concatenate([(pair * SUM_UNIT).astype(F16).reshape(64, 256), noises16])
     arrived = []
@@ -355,14 +347,14 @@
     partial = call(
         bin_kernel,
         vmem((lax.axis_size(ZC), 1, 9 * NBIN), F32),
-        [VM, VM, VM, VM],
+        [VM, VM, VM, VM, VM],
         flops=1 << 26,
         scratch_shapes=[
             pltpu.VMEM((cols, 8, span), jnp.int32),
-            pltpu.VMEM((32, pairs), BF16),
+            pltpu.VMEM((16, pairs), BF16),
         ],
         name="bins",
-    )(prev_tiles, partner, base, onehot)
+    )(prev_tiles, partner, base, onehot, counts)
     merged = call(merge_kernel, vmem((lax.axis_size(XY), 1, 9 * NBIN), F32), [VM], name="merge")(
         exchange(partial, ZC)
     )

time: 84.1 us -> 87.6 us (1.042)
  Pallas kernels: 11.4 us -> 14.2 us
  local copies, waits for them, and re-layouts: 0.04 us -> 1.4 us
    pallas_call x12, Pallas kernels: 11.4 us -> 14.2 us  [held(): run(*(a if spec is SM else pltpu.with_memory_space_constraint(a, spec.mem...]
    unnamed x13, local copies, waits for them, and re-layouts: 0.04 us -> 1.4 us
  transfers between devices with their start and end apart: 9 -> 9, of which waited for: 6 -> 5; matrix products, arithmetic and copies ran while one was open for 0% -> 0% of each run, Pallas kernels for 7% -> 8%
where the time goes in v7:
time: 87.6 us; the launch traced here: 87.1 us
  starting transfers between devices  28.6 us (33%)
  blocking collectives  28 us (32%)
  Pallas kernels  14.2 us (16%)
  waiting for transfers between devices  13.9 us (16%)
  local copies, waits for them, and re-layouts  1.4 us (2%)
    all_to_all x2, blocking collectives, exchange(): return lax.all_to_all(copies, axis, 0, 0, tiled=True)  28 us
    pallas_call x12, Pallas kernels, held(): run(*(a if spec is SM else pltpu.with_memory_space_constraint(a, spec.mem...  14.2 us
    all_to_all x2, starting transfers between devices, exchange(): return lax.all_to_all(copies, axis, 0, 0, tiled=True)  13 us
    all_to_all x2, waiting for transfers between devices, exchange(): return lax.all_to_all(copies, axis, 0, 0, tiled=True)  10.2 us
    ppermute x3, starting transfers between devices, body(): lax.ppermute(payload, 'col_0', [(chip, (chip + turn) % 4) for chip in ran...  8.45 us
    ppermute x3, waiting for transfers between devices, body(): lax.ppermute(payload, 'col_0', [(chip, (chip + turn) % 4) for chip in ran...  3.66 us
    ppermute x1, starting transfers between devices, body(): lax.ppermute(own_tiles, ROW, [(source, source + 1) for source in range(ro...  2.46 us
    ppermute x1, starting transfers between devices, body(): received = lax.ppermute(send, 'col_1', swap)  2.18 us
  transfers between devices with their start and end apart: 9, of which 5 were waited for; matrix products, arithmetic and copies ran while one was open for 0% of the time, Pallas kernels for 8%

profile of v7, /device:TPU:1, one launch (start us, length us, event | category | flops | bytes accessed | tf_op | source)
XLA Modules:
  0.0 87.1 jit_solution(16493952466884236474)
XLA Ops:
  0.6 1.4 %copies.1 = (bf16[16,256]{1,0:T(8,128)(2,1)S(1)}, bf16[32,16,256]{2,1,0:T(8,128)(2,1)}) custom-call(bf16[8,2,256]{2,1,0:T(2,128)(2,1)} %bitcast.27), custom_call_target="tpu_custom_call" | custom-call | flops 1 | bytes 1048576 | tf_op jit(solution)/shard_map/copies/pallas_call | solution.py:48
  2.1 9.2 %all-to-all-start = ((bf16[32,16,256]{2,1,0:T(8,128)(2,1)}), bf16[32,16,256]{2,1,0:T(8,128)(2,1)S(1)}, u32[]{:S(2)}, u32[]{:S(2)}) async-start(bf16[32,16,256]{2,1,0:T(8,128)(2,1)} %get-tuple-element.10), calls=%async_computation | async-start | bytes 524288 | tf_op jit(solution)/shard_map/all_to_all | solution.py:25
  11.3 1.0 %collective-permute-start.1 = (bf16[16,256]{1,0:T(8,128)(2,1)S(1)}, bf16[16,256]{1,0:T(8,128)(2,1)S(1)}, u32[]{:S(2)}, u32[]{:S(2)}) collective-permute-start(bf16[16,256]{1,0:T(8,128)(2,1)S(1)} %get-tuple-element.11.local), channel_id=1, source_target_pairs={{0,1},{1,0},{2,3},{3,2},{4,5},{5,4},{6,7},{7,6},{8,9},{9,8},{10,11... | collective-permute-start | bytes 24584 | tf_op jit(solution)/shard_map/ppermute | solution.py:295
  12.3 0.0 copy-start.2
  12.3 0.7 copy-done.2
  13.1 0.0 copy-start.4
  13.1 0.7 copy-done.4
  13.7 1.3 %prepare.1 = (bf16[128,4096]{1,0:T(8,128)(2,1)S(1)}, f32[8,1,256]{2,1,0:T(1,128)S(1)}, f32[8,128]{1,0:T(8,128)S(1)}) custom-call(s32[1,4096]{1,0:T(1,128)S(1)} %bitcast.20, s32[1,64]{1,0:T(1,128)S(1)} %copy-done.4), custom_call_target="tpu_custom_call" | custom-call | flops 1048576 | bytes 1048576 | tf_op jit(solution)/shard_map/prepare/pallas_call | solution.py:48
  15.0 0.0 collective-permute-done.1.other
  15.0 4.3 %all-to-all-done.columns = bf16[32,16,256]{2,1,0:T(8,128)(2,1)S(1)} async-done(((bf16[32,16,256]{2,1,0:T(8,128)(2,1)}), bf16[32,16,256]{2,1,0:T(8,128)(2,1)S(1)}, u32[]{:S(2)}, u32[]{:S(2)}) %all-to-all-start) | async-done | bytes 262176 | tf_op jit(solution)/shard_map/all_to_all | solution.py:25
  19.3 2.6 %send.1 = f32[8,8,256]{2,1,0:T(8,128)S(1)} custom-call(bf16[32,16,256]{2,1,0:T(8,128)(2,1)S(1)} %all-to-all-done.columns, bf16[64,64,256]{2,1,0:T(8,128)(2,1)} %bitcast.24), custom_call_target="tpu_custom_call" | custom-call | flops 268435456 | bytes 1048576 | tf_op jit(solution)/shard_map/send/pallas_call | solution.py:48
  21.9 0.0 copy-start
  21.9 2.2 %collective-permute-start = (f32[8,8,256]{2,1,0:T(8,128)S(1)}, f32[8,8,256]{2,1,0:T(8,128)S(1)}, u32[]{:S(2)}, u32[]{:S(2)}) collective-permute-start(f32[8,8,256]{2,1,0:T(8,128)S(1)} %send.1), channel_id=1, source_target_pairs={{0,1},{1,0},{2,3},{3,2},{4,5},{5,4},{6,7},{7,6},{8,9},{9,8},{10,11... | collective-permute-start | bytes 196616 | tf_op jit(solution)/shard_map/ppermute | solution.py:309
  24.1 0.0 copy-start.1
  24.1 2.7 %keep.1 = f32[8,8,256]{2,1,0:T(8,128)S(1)} custom-call(bf16[32,16,256]{2,1,0:T(8,128)(2,1)S(1)} %all-to-all-done.columns, bf16[64,64,256]{2,1,0:T(8,128)(2,1)} %bitcast.25), custom_call_target="tpu_custom_call" | custom-call | flops 268435456 | bytes 1048576 | tf_op jit(solution)/shard_map/keep/pallas_call | solution.py:48
  26.8 0.0 collective-permute-done
  26.9 5.2 %collective-permute-start.4 = (f16[96,256]{1,0:T(8,128)(2,1)S(1)}, f16[96,256]{1,0:T(8,128)(2,1)S(1)}, u32[]{:S(2)}, u32[]{:S(2)}) collective-permute-start(f16[96,256]{1,0:T(8,128)(2,1)S(1)} %pad_maximum_fusion), channel_id=1, source_target_pairs={{0,6},{2,0},{4,2},{6,4},{1,7},{3,1},{5,3},{7,5},{8,14},{10,8},{12,... | collective-permute-start | bytes 147464 | tf_op jit(solution)/shard_map/ppermute | solution.py:318
  32.1 0.0 collective-permute-start.3
  32.1 3.3 %collective-permute-start.2 = (f16[96,256]{1,0:T(8,128)(2,1)S(1)}, f16[96,256]{1,0:T(8,128)(2,1)S(1)}, u32[]{:S(2)}, u32[]{:S(2)}) collective-permute-start(f16[96,256]{1,0:T(8,128)(2,1)S(1)} %pad_maximum_fusion), channel_id=1, source_target_pairs={{0,4},{2,6},{4,0},{6,2},{1,5},{3,7},{5,1},{7,3},{8,12},{10,14},{12... | collective-permute-start | bytes 147464 | tf_op jit(solution)/shard_map/ppermute | solution.py:318
  35.3 0.0 collective-permute-done.4
  35.4 2.7 %collective-permute-done.3 = f16[96,256]{1,0:T(8,128)(2,1)S(1)} collective-permute-done((f16[96,256]{1,0:T(8,128)(2,1)S(1)}, f16[96,256]{1,0:T(8,128)(2,1)S(1)}, u32[]{:S(2)}, u32[]{:S(2)}) %collective-permute-start.3) | collective-permute-done | bytes 49184 | tf_op jit(solution)/shard_map/ppermute | solution.py:318
  38.1 0.9 %collective-permute-done.2 = f16[96,256]{1,0:T(8,128)(2,1)S(1)} collective-permute-done((f16[96,256]{1,0:T(8,128)(2,1)S(1)}, f16[96,256]{1,0:T(8,128)(2,1)S(1)}, u32[]{:S(2)}, u32[]{:S(2)}) %collective-permute-start.2) | collective-permute-done | bytes 49184 | tf_op jit(solution)/shard_map/ppermute | solution.py:318
  39.0 1.4 %collective-permute-start.5 = (bf16[8,8,256]{2,1,0:T(8,128)(2,1)S(1)}, bf16[8,8,256]{2,1,0:T(8,128)(2,1)S(1)}, u32[]{:S(2)}, u32[]{:S(2)}) collective-permute-start(bf16[8,8,256]{2,1,0:T(8,128)(2,1)S(1)} %fusion.1.mine), channel_id=1, source_target_pairs={{0,1},{1,0},{2,3},{3,2},{4,5},{5,4},{6,7},{7,6},{8,9},{9,8},{10,11... | collective-permute-start | bytes 98312 | tf_op jit(solution)/shard_map/ppermute | solution.py:323
  40.5 0.0 copy-done
  40.5 0.0 copy-start.3
  40.5 0.0 copy-start.5
  40.6 0.7 ondiag.1.on_diag
  41.3 0.1 collective-permute-done.5.theirs
  41.4 0.0 copy-done.1
  41.4 0.4 samples.1
  41.7 13.3 %all_to_all.20.table = bf16[8,16,256]{2,1,0:T(8,128)(2,1)S(1)} all-to-all(bf16[8,16,256]{2,1,0:T(8,128)(2,1)S(1)} %get-tuple-element.13), channel_id=1, replica_groups=mesh['row_0'=4,'row_1'=2,'row_2'=4,'col_0'=4,'col_1'=2] {'col_0','col_1'}, dimensions={0} | all-to-all | bytes 131072 | tf_op jit(solution)/shard_map/all_to_all | solution.py:25
  55.1 2.5 %collective-permute-start.6 = (bf16[8,16,256]{2,1,0:T(8,128)(2,1)S(1)}, bf16[8,16,256]{2,1,0:T(8,128)(2,1)S(1)}, u32[]{:S(2)}, u32[]{:S(2)}) collective-permute-start(bf16[8,16,256]{2,1,0:T(8,128)(2,1)S(1)} %all_to_all.20.table), channel_id=1, source_target_pairs={{0,8},{8,16},{16,24},{24,32},{32,40},{40,48},{48,56},{56,64},{64,7... | collective-permute-start | bytes 196616 | tf_op jit(solution)/shard_map/ppermute | solution.py:335
  57.5 0.0 copy-done.3
  57.5 0.0 copy-done.5
  57.5 1.7 %own.1.base = f32[8,4096]{1,0:T(8,128)S(1)} custom-call(bf16[8,16,256]{2,1,0:T(8,128)(2,1)S(1)} %all_to_all.20.table, s32[1,4096]{1,0:T(1,128)S(1)} %bitcast.23, s32[1,4096]{1,0:T(1,128)S(1)} %bitcast.21), custom_call_target="tpu_custom_call" | custom-call | flops 67108864 | bytes 1048576 | tf_op jit(solution)/shard_map/own/pallas_call | solution.py:48
  59.2 0.0 collective-permute-done.6.prev
  59.3 1.5 %bins.1 = f32[16,1,1152]{2,1,0:T(1,128)S(1)} custom-call(bf16[8,16,256]{2,1,0:T(8,128)(2,1)S(1)} %collective-permute-done.6.prev, s32[1,4096]{1,0:T(1,128)S(1)} %bitcast.22, f32[8,4096]{1,0:T(8,128)S(1)} %own.1.base, bf16[128,4096]{1,0:T(8,128)(2,1)S(1)} %get-tuple-element.14.onehot, f32[8,128]{1,0:T(8,128)S(1)} %get-tuple-element.15.counts), custom_call_target="tpu_custom_call" | custom-call | flops 67108864 | bytes 1048576 | tf_op jit(solution)/shard_map/bins/pallas_call | solution.py:48
  60.7 14.7 %all_to_all.21.parts = f32[16,1,1152]{2,1,0:T(1,128)S(1)} all-to-all(f32[16,1,1152]{2,1,0:T(1,128)S(1)} %bins.1), channel_id=1, replica_groups=mesh['row_0'=4,'row_1'=2,'row_2'=4,'col_0'=4,'col_1'=2] {'row_1','col_0'..., dimensions={0} | all-to-all | bytes 147456 | tf_op jit(solution)/shard_map/all_to_all | solution.py:25
  75.5 0.7 merge.1
  76.1 3.8 %all-to-all-start.3 = ((f32[16,1,1152]{2,1,0:T(1,128)}), f32[16,1,1152]{2,1,0:T(1,128)S(1)}, u32[]{:S(2)}, u32[]{:S(2)}) async-start(f32[16,1,1152]{2,1,0:T(1,128)} %merge.1), calls=%async_computation.3 | async-start | bytes 147456 | tf_op jit(solution)/shard_map/all_to_all | solution.py:25
  79.9 0.6 emit.1
  80.6 5.9 %all-to-all-done.3.parts = f32[16,1,1152]{2,1,0:T(1,128)S(1)} async-done(((f32[16,1,1152]{2,1,0:T(1,128)}), f32[16,1,1152]{2,1,0:T(1,128)S(1)}, u32[]{:S(2)}, u32[]{:S(2)}) %all-to-all-start.3) | async-done | bytes 73760 | tf_op jit(solution)/shard_map/all_to_all | solution.py:25
  86.5 0.6 finish.1
  (10 shorter events, 0.1 us)
Async XLA Ops:
  2.1 17.2 %all-to-all-start = ((bf16[32,16,256]{2,1,0:T(8,128)(2,1)}), bf16[32,16,256]{2,1,0:T(8,128)(2,1)S(1)}, u32[]{:S(2)}, u32[]{:S(2)}) async-start(bf16[32,16,256]{2,1,0:T(8,128)(2,1)} %get-tuple-element.10), calls=%async_computation | async-start | bytes 524288 | tf_op jit(solution)/shard_map/all_to_all | solution.py:25
  11.3 3.7 %collective-permute-start.1 = (bf16[16,256]{1,0:T(8,128)(2,1)S(1)}, bf16[16,256]{1,0:T(8,128)(2,1)S(1)}, u32[]{:S(2)}, u32[]{:S(2)}) collective-permute-start(bf16[16,256]{1,0:T(8,128)(2,1)S(1)} %get-tuple-element.11.local), channel_id=1, source_target_pairs={{0,1},{1,0},{2,3},{3,2},{4,5},{5,4},{6,7},{7,6},{8,9},{9,8},{10,11... | collective-permute-start | bytes 24584 | tf_op jit(solution)/shard_map/ppermute | solution.py:295
  12.3 0.7 copy-start.2
  13.1 0.7 copy-start.4
  21.9 18.7 %copy-start = (bf16[2,1,256,2048]{3,2,1,0:T(8,128)(2,1)S(1)}, bf16[2,1,256,2048]{3,2,1,0:T(8,128)(2,1)}, u32[]{:S(2)}) copy-start(bf16[2,1,256,2048]{3,2,1,0:T(8,128)(2,1)} %param.9) | copy-start | bytes 6291460
  21.9 4.9 %collective-permute-start = (f32[8,8,256]{2,1,0:T(8,128)S(1)}, f32[8,8,256]{2,1,0:T(8,128)S(1)}, u32[]{:S(2)}, u32[]{:S(2)}) collective-permute-start(f32[8,8,256]{2,1,0:T(8,128)S(1)} %send.1), channel_id=1, source_target_pairs={{0,1},{1,0},{2,3},{3,2},{4,5},{5,4},{6,7},{7,6},{8,9},{9,8},{10,11... | collective-permute-start | bytes 196616 | tf_op jit(solution)/shard_map/ppermute | solution.py:309
  24.1 17.3 %copy-start.1 = (bf16[1,64,64,256]{3,2,1,0:T(8,128)(2,1)S(1)}, bf16[1,64,64,256]{3,2,1,0:T(8,128)(2,1)}, u32[]{:S(2)}) copy-start(bf16[1,64,64,256]{3,2,1,0:T(8,128)(2,1)} %param.10) | copy-start | bytes 6291460
  26.9 8.5 %collective-permute-start.4 = (f16[96,256]{1,0:T(8,128)(2,1)S(1)}, f16[96,256]{1,0:T(8,128)(2,1)S(1)}, u32[]{:S(2)}, u32[]{:S(2)}) collective-permute-start(f16[96,256]{1,0:T(8,128)(2,1)S(1)} %pad_maximum_fusion), channel_id=1, source_target_pairs={{0,6},{2,0},{4,2},{6,4},{1,7},{3,1},{5,3},{7,5},{8,14},{10,8},{12,... | collective-permute-start | bytes 147464 | tf_op jit(solution)/shard_map/ppermute | solution.py:318
  32.1 6.0 %collective-permute-start.3 = (f16[96,256]{1,0:T(8,128)(2,1)S(1)}, f16[96,256]{1,0:T(8,128)(2,1)S(1)}, u32[]{:S(2)}, u32[]{:S(2)}) collective-permute-start(f16[96,256]{1,0:T(8,128)(2,1)S(1)} %pad_maximum_fusion), channel_id=1, source_target_pairs={{0,2},{2,4},{4,6},{6,0},{1,3},{3,5},{5,7},{7,1},{8,10},{10,12},{12... | collective-permute-start | bytes 147464 | tf_op jit(solution)/shard_map/ppermute | solution.py:318
  32.1 7.0 %collective-permute-start.2 = (f16[96,256]{1,0:T(8,128)(2,1)S(1)}, f16[96,256]{1,0:T(8,128)(2,1)S(1)}, u32[]{:S(2)}, u32[]{:S(2)}) collective-permute-start(f16[96,256]{1,0:T(8,128)(2,1)S(1)} %pad_maximum_fusion), channel_id=1, source_target_pairs={{0,4},{2,6},{4,0},{6,2},{1,5},{3,7},{5,1},{7,3},{8,12},{10,14},{12... | collective-permute-start | bytes 147464 | tf_op jit(solution)/shard_map/ppermute | solution.py:318
  39.0 2.3 %collective-permute-start.5 = (bf16[8,8,256]{2,1,0:T(8,128)(2,1)S(1)}, bf16[8,8,256]{2,1,0:T(8,128)(2,1)S(1)}, u32[]{:S(2)}, u32[]{:S(2)}) collective-permute-start(bf16[8,8,256]{2,1,0:T(8,128)(2,1)S(1)} %fusion.1.mine), channel_id=1, source_target_pairs={{0,1},{1,0},{2,3},{3,2},{4,5},{5,4},{6,7},{7,6},{8,9},{9,8},{10,11... | collective-permute-start | bytes 98312 | tf_op jit(solution)/shard_map/ppermute | solution.py:323
  40.5 17.0 %copy-start.3 = (s32[1,1,4096]{2,1,0:T(1,128)S(1)}, s32[1,1,4096]{2,1,0:T(1,128)}, u32[]{:S(2)}) copy-start(s32[1,1,4096]{2,1,0:T(1,128)} %param.14) | copy-start | bytes 49156
  40.5 17.0 %copy-start.5 = (s32[1,1,4096]{2,1,0:T(1,128)S(1)}, s32[1,1,4096]{2,1,0:T(1,128)}, u32[]{:S(2)}) copy-start(s32[1,1,4096]{2,1,0:T(1,128)} %param.13) | copy-start | bytes 49156
  55.1 4.2 %collective-permute-start.6 = (bf16[8,16,256]{2,1,0:T(8,128)(2,1)S(1)}, bf16[8,16,256]{2,1,0:T(8,128)(2,1)S(1)}, u32[]{:S(2)}, u32[]{:S(2)}) collective-permute-start(bf16[8,16,256]{2,1,0:T(8,128)(2,1)S(1)} %all_to_all.20.table), channel_id=1, source_target_pairs={{0,8},{8,16},{16,24},{24,32},{32,40},{40,48},{48,56},{56,64},{64,7... | collective-permute-start | bytes 196616 | tf_op jit(solution)/shard_map/ppermute | solution.py:335
  76.1 10.4 %all-to-all-start.3 = ((f32[16,1,1152]{2,1,0:T(1,128)}), f32[16,1,1152]{2,1,0:T(1,128)S(1)}, u32[]{:S(2)}, u32[]{:S(2)}) async-start(f32[16,1,1152]{2,1,0:T(1,128)} %merge.1), calls=%async_computation.3 | async-start | bytes 147456 | tf_op jit(solution)/shard_map/all_to_all | solution.py:25

commit v8 on v7

--- a/solution.py
+++ b/solution.py
@@ -55,15 +55,18 @@
     return held
 
 
-def copies_kernel(source, local, out, noise, sem):
-    copy = pltpu.make_async_copy(source, noise, sem)
+def copies_kernel(source, factor, local, out, right, noise, sems):
+    copy = pltpu.make_async_copy(source, noise, sems.at[0])
+    fetch = pltpu.make_async_copy(factor, right, sems.at[1])
     copy.start()
+    fetch.start()
     copy.wait()
     rows = [noise[s].astype(F32)[h : h + 1] for h in range(2) for s in range(8)]
     mine = jnp.concatenate(rows, axis=0).astype(BF16)
     local[...] = mine
     for n in range(out.shape[0]):
         out[n] = mine
+    fetch.wait()
 
 
 def prepare_kernel(bins, ranks, onehot, keep, counts):
@@ -95,36 +98,34 @@
     out[16:] = jnp.where(first, far, own).astype(BF16)
 
 
-def project_kernel(columns, right, out, factors, sems, *, away):
+def project_kernel(columns, right, out, *, away):
     row, core = lax.axis_index(ROW), lax.axis_index("col_1")
     half = 1 - core if away else core
     tiles = 2 * columns.shape[0]
-    groups = out.shape[0]
+    groups = right.shape[0] // 8
     lane = lax.broadcasted_iota(jnp.int32, (8, 128), 1)
-    base = half * groups * 4
-    loads = [
-        pltpu.make_async_copy(right.at[pl.ds(base + 4 * g, 4)], factors.at[g], sems.at[g])
-        for g in range(groups)
-    ]
-    for load in loads:
-        load.start()
-    for g in range(groups):
+
+    def step(g, carry):
+        base = (half * groups + g) * 4
         blocks = []
         low = []
         for n in range(4):
-            slot = base + 4 * g + n
+            slot = base + n
             tile = jnp.where(slot < row, slot, slot - row)
             first = tile < tiles // 2
             blocks.append(columns[jnp.where(first, tile, tiles - 1 - tile)])
             low.append(first)
-        loads[g].wait()
-        full = nt_dot(jnp.concatenate(blocks, axis=0), factors[g].reshape(256, 256))
+        factor = right[pl.ds(base, 4)].reshape(256, 256)
+        full = nt_dot(jnp.concatenate(blocks, axis=0), factor)
         parts = []
         for n in range(4):
             cols = full[16 * n : 16 * n + 16, 128 * (n // 2) : 128 * (n // 2) + 128]
             parts.append(jnp.where(low[n], cols[:8], cols[8:]))
         out[g, :, :128] = jnp.where(lane < 64, parts[0], parts[1])
         out[g, :, 128:] = jnp.where(lane < 64, parts[2], parts[3])
+        return carry
+
+    lax.fori_loop(0, groups, step, 0, unroll=4)
 
 
 def on_diag_kernel(n0, n1, n2, n3, diag, out):
@@ -277,13 +278,17 @@
     first, partner, bins = pair_first[0], pair_partner[0], bin_ids[0]
     pairs = first.shape[1]
 
-    local, spread_noise = call(
+    local, spread_noise, right = call(
         copies_kernel,
-        (vmem((16, span), BF16), vmem((rows, 16, span), BF16)),
-        [HB],
-        scratch_shapes=[pltpu.VMEM((8, 2, span), BF16), pltpu.SemaphoreType.DMA(())],
+        (
+            vmem((16, span), BF16),
+            vmem((rows, 16, span), BF16),
+            vmem(right_factor.shape[1:], BF16),
+        ),
+        [HB, HB],
+        scratch_shapes=[pltpu.VMEM((8, 2, span), BF16), pltpu.SemaphoreType.DMA((2,))],
         name="copies",
-    )(jnp.transpose(noise, (0, 2, 1, 3))[:, 0])
+    )(jnp.transpose(noise, (0, 2, 1, 3))[:, 0], right_factor[0])
     columns = exchange(spread_noise, ROW)
     onehot, allowed, counts = call(
         prepare_kernel,
@@ -293,15 +298,13 @@
         name="prepare",
     )(bins, tile_ranks)
     other_noise = lax.ppermute(local, "col_1", swap)
-    right = right_factor[0]
 
     def project(away, name):
         return call(
             functools.partial(project_kernel, away=away),
             vmem((8, 8, 256), F32),
-            [VM, HB],
+            [VM, VM],
             flops=1 << 28,
-            scratch_shapes=[pltpu.VMEM((8, 4, 64, span), BF16), pltpu.SemaphoreType.DMA((8,))],
             name=name,
         )(columns, right)
 

time: 87.6 us -> 84.9 us (0.969)
  Pallas kernels: 14.2 us -> 11 us
  waiting for transfers between devices: 13.9 us -> 15.8 us
  local copies, waits for them, and re-layouts: 1.4 us -> 0.04 us
    pallas_call x12, Pallas kernels: 14.2 us -> 11 us  [held(): run(*(a if spec is SM else pltpu.with_memory_space_constraint(a, spec.mem...]
    all_to_all x2, waiting for transfers between devices: 10.2 us -> 11.6 us  [exchange(): return lax.all_to_all(copies, axis, 0, 0, tiled=True)]
    unnamed x13, local copies, waits for them, and re-layouts: 1.4 us -> 0.04 us
  transfers between devices with their start and end apart: 9 -> 9, of which waited for: 5 -> 6; matrix products, arithmetic and copies ran while one was open for 0% -> 0% of each run, Pallas kernels for 8% -> 6%
where the time goes in v8:
time: 84.9 us; the launch traced here: 84.5 us
  starting transfers between devices  29 us (34%)
  blocking collectives  27.8 us (33%)
  waiting for transfers between devices  15.8 us (19%)
  Pallas kernels  11 us (13%)
    all_to_all x2, blocking collectives, exchange(): return lax.all_to_all(copies, axis, 0, 0, tiled=True)  27.8 us
    all_to_all x2, starting transfers between devices, exchange(): return lax.all_to_all(copies, axis, 0, 0, tiled=True)  13.3 us
    all_to_all x2, waiting for transfers between devices, exchange(): return lax.all_to_all(copies, axis, 0, 0, tiled=True)  11.6 us
    pallas_call x12, Pallas kernels, held(): run(*(a if spec is SM else pltpu.with_memory_space_constraint(a, spec.mem...  11 us
    ppermute x3, starting transfers between devices, body(): lax.ppermute(payload, 'col_0', [(chip, (chip + turn) % 4) for chip in ran...  8.46 us
    ppermute x3, waiting for transfers between devices, body(): lax.ppermute(payload, 'col_0', [(chip, (chip + turn) % 4) for chip in ran...  3.86 us
    ppermute x1, starting transfers between devices, body(): lax.ppermute(own_tiles, ROW, [(source, source + 1) for source in range(ro...  2.45 us
    ppermute x1, starting transfers between devices, body(): received = lax.ppermute(send, 'col_1', swap)  2.17 us
  transfers between devices with their start and end apart: 9, of which 6 were waited for; matrix products, arithmetic and copies ran while one was open for 0% of the time, Pallas kernels for 6%

profile of v8, /device:TPU:1, one launch (start us, length us, event | category | flops | bytes accessed | tf_op | source)
XLA Modules:
  0.0 84.5 jit_solution(4058171691425255841)
XLA Ops:
  0.6 0.0 copy-start.2
  0.6 0.0 copy-start.4
  0.7 2.3 %copies.1 = (bf16[16,256]{1,0:T(8,128)(2,1)S(1)}, bf16[32,16,256]{2,1,0:T(8,128)(2,1)}, bf16[64,64,256]{2,1,0:T(8,128)(2,1)S(1)}) custom-call(bf16[8,2,256]{2,1,0:T(2,128)(2,1)} %bitcast.25, bf16[64,64,256]{2,1,0:T(8,128)(2,1)} %bitcast.24), custom_call_target="tpu_custom_call" | custom-call | flops 1 | bytes 1048576 | tf_op jit(solution)/shard_map/copies/pallas_call | solution.py:48
  3.0 9.2 %all-to-all-start = ((bf16[32,16,256]{2,1,0:T(8,128)(2,1)}), bf16[32,16,256]{2,1,0:T(8,128)(2,1)S(1)}, u32[]{:S(2)}, u32[]{:S(2)}) async-start(bf16[32,16,256]{2,1,0:T(8,128)(2,1)} %get-tuple-element.11), calls=%async_computation | async-start | bytes 524288 | tf_op jit(solution)/shard_map/all_to_all | solution.py:25
  12.2 1.0 %collective-permute-start.1 = (bf16[16,256]{1,0:T(8,128)(2,1)S(1)}, bf16[16,256]{1,0:T(8,128)(2,1)S(1)}, u32[]{:S(2)}, u32[]{:S(2)}) collective-permute-start(bf16[16,256]{1,0:T(8,128)(2,1)S(1)} %get-tuple-element.13.local), channel_id=1, source_target_pairs={{0,1},{1,0},{2,3},{3,2},{4,5},{5,4},{6,7},{7,6},{8,9},{9,8},{10,11... | collective-permute-start | bytes 24584 | tf_op jit(solution)/shard_map/ppermute | solution.py:300
  13.3 0.0 copy-done.2
  13.3 0.0 copy-done.4
  13.3 1.3 %prepare.1 = (bf16[128,4096]{1,0:T(8,128)(2,1)S(1)}, f32[8,1,256]{2,1,0:T(1,128)S(1)}, f32[8,128]{1,0:T(8,128)S(1)}) custom-call(s32[1,4096]{1,0:T(1,128)S(1)} %bitcast.20, s32[1,64]{1,0:T(1,128)S(1)} %copy-done.4), custom_call_target="tpu_custom_call" | custom-call | flops 1048576 | bytes 1048576 | tf_op jit(solution)/shard_map/prepare/pallas_call | solution.py:48
  14.5 0.0 collective-permute-done.1.other
  14.6 5.7 %all-to-all-done.columns = bf16[32,16,256]{2,1,0:T(8,128)(2,1)S(1)} async-done(((bf16[32,16,256]{2,1,0:T(8,128)(2,1)}), bf16[32,16,256]{2,1,0:T(8,128)(2,1)S(1)}, u32[]{:S(2)}, u32[]{:S(2)}) %all-to-all-start) | async-done | bytes 262176 | tf_op jit(solution)/shard_map/all_to_all | solution.py:25
  20.2 0.6 send.1
  20.8 0.0 copy-start
  20.8 2.2 %collective-permute-start = (f32[8,8,256]{2,1,0:T(8,128)S(1)}, f32[8,8,256]{2,1,0:T(8,128)S(1)}, u32[]{:S(2)}, u32[]{:S(2)}) collective-permute-start(f32[8,8,256]{2,1,0:T(8,128)S(1)} %send.1), channel_id=1, source_target_pairs={{0,1},{1,0},{2,3},{3,2},{4,5},{5,4},{6,7},{7,6},{8,9},{9,8},{10,11... | collective-permute-start | bytes 196616 | tf_op jit(solution)/shard_map/ppermute | solution.py:312
  23.0 0.0 copy-start.1
  23.0 0.6 keep.1
  23.6 0.3 collective-permute-done
  23.9 5.2 %collective-permute-start.4 = (f16[96,256]{1,0:T(8,128)(2,1)S(1)}, f16[96,256]{1,0:T(8,128)(2,1)S(1)}, u32[]{:S(2)}, u32[]{:S(2)}) collective-permute-start(f16[96,256]{1,0:T(8,128)(2,1)S(1)} %pad_maximum_fusion), channel_id=1, source_target_pairs={{0,6},{2,0},{4,2},{6,4},{1,7},{3,1},{5,3},{7,5},{8,14},{10,8},{12,... | collective-permute-start | bytes 147464 | tf_op jit(solution)/shard_map/ppermute | solution.py:321
  29.1 0.0 collective-permute-start.3
  29.1 3.3 %collective-permute-start.2 = (f16[96,256]{1,0:T(8,128)(2,1)S(1)}, f16[96,256]{1,0:T(8,128)(2,1)S(1)}, u32[]{:S(2)}, u32[]{:S(2)}) collective-permute-start(f16[96,256]{1,0:T(8,128)(2,1)S(1)} %pad_maximum_fusion), channel_id=1, source_target_pairs={{0,4},{2,6},{4,0},{6,2},{1,5},{3,7},{5,1},{7,3},{8,12},{10,14},{12... | collective-permute-start | bytes 147464 | tf_op jit(solution)/shard_map/ppermute | solution.py:321
  32.4 0.0 collective-permute-done.4
  32.4 2.3 %collective-permute-done.3 = f16[96,256]{1,0:T(8,128)(2,1)S(1)} collective-permute-done((f16[96,256]{1,0:T(8,128)(2,1)S(1)}, f16[96,256]{1,0:T(8,128)(2,1)S(1)}, u32[]{:S(2)}, u32[]{:S(2)}) %collective-permute-start.3) | collective-permute-done | bytes 49184 | tf_op jit(solution)/shard_map/ppermute | solution.py:321
  34.8 1.5 %collective-permute-done.2 = f16[96,256]{1,0:T(8,128)(2,1)S(1)} collective-permute-done((f16[96,256]{1,0:T(8,128)(2,1)S(1)}, f16[96,256]{1,0:T(8,128)(2,1)S(1)}, u32[]{:S(2)}, u32[]{:S(2)}) %collective-permute-start.2) | collective-permute-done | bytes 49184 | tf_op jit(solution)/shard_map/ppermute | solution.py:321
  36.3 1.6 %collective-permute-start.5 = (bf16[8,8,256]{2,1,0:T(8,128)(2,1)S(1)}, bf16[8,8,256]{2,1,0:T(8,128)(2,1)S(1)}, u32[]{:S(2)}, u32[]{:S(2)}) collective-permute-start(bf16[8,8,256]{2,1,0:T(8,128)(2,1)S(1)} %fusion.1.mine), channel_id=1, source_target_pairs={{0,1},{1,0},{2,3},{3,2},{4,5},{5,4},{6,7},{7,6},{8,9},{9,8},{10,11... | collective-permute-start | bytes 98312 | tf_op jit(solution)/shard_map/ppermute | solution.py:326
  37.9 0.0 copy-done
  37.9 0.0 copy-start.3
  38.0 0.0 copy-start.5
  38.0 0.7 ondiag.1.on_diag
  38.7 0.1 collective-permute-done.5.theirs
  38.8 0.0 copy-done.1
  38.8 0.4 samples.1
  39.2 13.3 %all_to_all.20.table = bf16[8,16,256]{2,1,0:T(8,128)(2,1)S(1)} all-to-all(bf16[8,16,256]{2,1,0:T(8,128)(2,1)S(1)} %get-tuple-element.15), channel_id=1, replica_groups=mesh['row_0'=4,'row_1'=2,'row_2'=4,'col_0'=4,'col_1'=2] {'col_0','col_1'}, dimensions={0} | all-to-all | bytes 131072 | tf_op jit(solution)/shard_map/all_to_all | solution.py:25
  52.5 2.4 %collective-permute-start.6 = (bf16[8,16,256]{2,1,0:T(8,128)(2,1)S(1)}, bf16[8,16,256]{2,1,0:T(8,128)(2,1)S(1)}, u32[]{:S(2)}, u32[]{:S(2)}) collective-permute-start(bf16[8,16,256]{2,1,0:T(8,128)(2,1)S(1)} %all_to_all.20.table), channel_id=1, source_target_pairs={{0,8},{8,16},{16,24},{24,32},{32,40},{40,48},{48,56},{56,64},{64,7... | collective-permute-start | bytes 196616 | tf_op jit(solution)/shard_map/ppermute | solution.py:338
  54.9 0.0 copy-done.3
  54.9 0.0 copy-done.5
  55.0 1.7 %own.1.base = f32[8,4096]{1,0:T(8,128)S(1)} custom-call(bf16[8,16,256]{2,1,0:T(8,128)(2,1)S(1)} %all_to_all.20.table, s32[1,4096]{1,0:T(1,128)S(1)} %bitcast.23, s32[1,4096]{1,0:T(1,128)S(1)} %bitcast.21), custom_call_target="tpu_custom_call" | custom-call | flops 67108864 | bytes 1048576 | tf_op jit(solution)/shard_map/own/pallas_call | solution.py:48
  56.7 0.0 collective-permute-done.6.prev
  56.7 1.5 %bins.1 = f32[16,1,1152]{2,1,0:T(1,128)S(1)} custom-call(bf16[8,16,256]{2,1,0:T(8,128)(2,1)S(1)} %collective-permute-done.6.prev, s32[1,4096]{1,0:T(1,128)S(1)} %bitcast.22, f32[8,4096]{1,0:T(8,128)S(1)} %own.1.base, bf16[128,4096]{1,0:T(8,128)(2,1)S(1)} %get-tuple-element.16.onehot, f32[8,128]{1,0:T(8,128)S(1)} %get-tuple-element.17.counts), custom_call_target="tpu_custom_call" | custom-call | flops 67108864 | bytes 1048576 | tf_op jit(solution)/shard_map/bins/pallas_call | solution.py:48
  58.2 14.5 %all_to_all.21.parts = f32[16,1,1152]{2,1,0:T(1,128)S(1)} all-to-all(f32[16,1,1152]{2,1,0:T(1,128)S(1)} %bins.1), channel_id=1, replica_groups=mesh['row_0'=4,'row_1'=2,'row_2'=4,'col_0'=4,'col_1'=2] {'row_1','col_0'..., dimensions={0} | all-to-all | bytes 147456 | tf_op jit(solution)/shard_map/all_to_all | solution.py:25
  72.7 0.7 merge.1
  73.3 4.0 %all-to-all-start.3 = ((f32[16,1,1152]{2,1,0:T(1,128)}), f32[16,1,1152]{2,1,0:T(1,128)S(1)}, u32[]{:S(2)}, u32[]{:S(2)}) async-start(f32[16,1,1152]{2,1,0:T(1,128)} %merge.1), calls=%async_computation.3 | async-start | bytes 147456 | tf_op jit(solution)/shard_map/all_to_all | solution.py:25
  77.4 0.6 emit.1
  78.0 5.9 %all-to-all-done.3.parts = f32[16,1,1152]{2,1,0:T(1,128)S(1)} async-done(((f32[16,1,1152]{2,1,0:T(1,128)}), f32[16,1,1152]{2,1,0:T(1,128)S(1)}, u32[]{:S(2)}, u32[]{:S(2)}) %all-to-all-start.3) | async-done | bytes 73760 | tf_op jit(solution)/shard_map/all_to_all | solution.py:25
  83.9 0.6 finish.1
  (10 shorter events, 0.1 us)
Async XLA Ops:
  0.6 12.6 %copy-start.2 = (s32[1,1,4096]{2,1,0:T(1,128)S(1)}, s32[1,1,4096]{2,1,0:T(1,128)}, u32[]{:S(2)}) copy-start(s32[1,1,4096]{2,1,0:T(1,128)} %param.15) | copy-start | bytes 49156
  0.6 12.6 %copy-start.4 = (s32[1,64]{1,0:T(1,128)S(1)}, s32[1,64]{1,0:T(1,128)}, u32[]{:S(2)}) copy-start(s32[1,64]{1,0:T(1,128)} %ranks.1) | copy-start | bytes 772
  3.0 17.2 %all-to-all-start = ((bf16[32,16,256]{2,1,0:T(8,128)(2,1)}), bf16[32,16,256]{2,1,0:T(8,128)(2,1)S(1)}, u32[]{:S(2)}, u32[]{:S(2)}) async-start(bf16[32,16,256]{2,1,0:T(8,128)(2,1)} %get-tuple-element.11), calls=%async_computation | async-start | bytes 524288 | tf_op jit(solution)/shard_map/all_to_all | solution.py:25
  12.2 2.3 %collective-permute-start.1 = (bf16[16,256]{1,0:T(8,128)(2,1)S(1)}, bf16[16,256]{1,0:T(8,128)(2,1)S(1)}, u32[]{:S(2)}, u32[]{:S(2)}) collective-permute-start(bf16[16,256]{1,0:T(8,128)(2,1)S(1)} %get-tuple-element.13.local), channel_id=1, source_target_pairs={{0,1},{1,0},{2,3},{3,2},{4,5},{5,4},{6,7},{7,6},{8,9},{9,8},{10,11... | collective-permute-start | bytes 24584 | tf_op jit(solution)/shard_map/ppermute | solution.py:300
  20.8 17.1 %copy-start = (bf16[2,1,256,2048]{3,2,1,0:T(8,128)(2,1)S(1)}, bf16[2,1,256,2048]{3,2,1,0:T(8,128)(2,1)}, u32[]{:S(2)}) copy-start(bf16[2,1,256,2048]{3,2,1,0:T(8,128)(2,1)} %param.9) | copy-start | bytes 6291460
  20.8 3.1 %collective-permute-start = (f32[8,8,256]{2,1,0:T(8,128)S(1)}, f32[8,8,256]{2,1,0:T(8,128)S(1)}, u32[]{:S(2)}, u32[]{:S(2)}) collective-permute-start(f32[8,8,256]{2,1,0:T(8,128)S(1)} %send.1), channel_id=1, source_target_pairs={{0,1},{1,0},{2,3},{3,2},{4,5},{5,4},{6,7},{7,6},{8,9},{9,8},{10,11... | collective-permute-start | bytes 196616 | tf_op jit(solution)/shard_map/ppermute | solution.py:312
  23.0 15.8 %copy-start.1 = (bf16[1,64,64,256]{3,2,1,0:T(8,128)(2,1)S(1)}, bf16[1,64,64,256]{3,2,1,0:T(8,128)(2,1)}, u32[]{:S(2)}) copy-start(bf16[1,64,64,256]{3,2,1,0:T(8,128)(2,1)} %param.10) | copy-start | bytes 6291460
  23.9 8.5 %collective-permute-start.4 = (f16[96,256]{1,0:T(8,128)(2,1)S(1)}, f16[96,256]{1,0:T(8,128)(2,1)S(1)}, u32[]{:S(2)}, u32[]{:S(2)}) collective-permute-start(f16[96,256]{1,0:T(8,128)(2,1)S(1)} %pad_maximum_fusion), channel_id=1, source_target_pairs={{0,6},{2,0},{4,2},{6,4},{1,7},{3,1},{5,3},{7,5},{8,14},{10,8},{12,... | collective-permute-start | bytes 147464 | tf_op jit(solution)/shard_map/ppermute | solution.py:321
  29.1 5.6 %collective-permute-start.3 = (f16[96,256]{1,0:T(8,128)(2,1)S(1)}, f16[96,256]{1,0:T(8,128)(2,1)S(1)}, u32[]{:S(2)}, u32[]{:S(2)}) collective-permute-start(f16[96,256]{1,0:T(8,128)(2,1)S(1)} %pad_maximum_fusion), channel_id=1, source_target_pairs={{0,2},{2,4},{4,6},{6,0},{1,3},{3,5},{5,7},{7,1},{8,10},{10,12},{12... | collective-permute-start | bytes 147464 | tf_op jit(solution)/shard_map/ppermute | solution.py:321
  29.1 7.2 %collective-permute-start.2 = (f16[96,256]{1,0:T(8,128)(2,1)S(1)}, f16[96,256]{1,0:T(8,128)(2,1)S(1)}, u32[]{:S(2)}, u32[]{:S(2)}) collective-permute-start(f16[96,256]{1,0:T(8,128)(2,1)S(1)} %pad_maximum_fusion), channel_id=1, source_target_pairs={{0,4},{2,6},{4,0},{6,2},{1,5},{3,7},{5,1},{7,3},{8,12},{10,14},{12... | collective-permute-start | bytes 147464 | tf_op jit(solution)/shard_map/ppermute | solution.py:321
  36.3 2.4 %collective-permute-start.5 = (bf16[8,8,256]{2,1,0:T(8,128)(2,1)S(1)}, bf16[8,8,256]{2,1,0:T(8,128)(2,1)S(1)}, u32[]{:S(2)}, u32[]{:S(2)}) collective-permute-start(bf16[8,8,256]{2,1,0:T(8,128)(2,1)S(1)} %fusion.1.mine), channel_id=1, source_target_pairs={{0,1},{1,0},{2,3},{3,2},{4,5},{5,4},{6,7},{7,6},{8,9},{9,8},{10,11... | collective-permute-start | bytes 98312 | tf_op jit(solution)/shard_map/ppermute | solution.py:326
  37.9 17.0 %copy-start.3 = (s32[1,1,4096]{2,1,0:T(1,128)S(1)}, s32[1,1,4096]{2,1,0:T(1,128)}, u32[]{:S(2)}) copy-start(s32[1,1,4096]{2,1,0:T(1,128)} %param.14) | copy-start | bytes 49156
  38.0 17.0 %copy-start.5 = (s32[1,1,4096]{2,1,0:T(1,128)S(1)}, s32[1,1,4096]{2,1,0:T(1,128)}, u32[]{:S(2)}) copy-start(s32[1,1,4096]{2,1,0:T(1,128)} %param.13) | copy-start | bytes 49156
  52.5 4.2 %collective-permute-start.6 = (bf16[8,16,256]{2,1,0:T(8,128)(2,1)S(1)}, bf16[8,16,256]{2,1,0:T(8,128)(2,1)S(1)}, u32[]{:S(2)}, u32[]{:S(2)}) collective-permute-start(bf16[8,16,256]{2,1,0:T(8,128)(2,1)S(1)} %all_to_all.20.table), channel_id=1, source_target_pairs={{0,8},{8,16},{16,24},{24,32},{32,40},{40,48},{48,56},{56,64},{64,7... | collective-permute-start | bytes 196616 | tf_op jit(solution)/shard_map/ppermute | solution.py:338
  73.3 10.6 %all-to-all-start.3 = ((f32[16,1,1152]{2,1,0:T(1,128)}), f32[16,1,1152]{2,1,0:T(1,128)S(1)}, u32[]{:S(2)}, u32[]{:S(2)}) async-start(f32[16,1,1152]{2,1,0:T(1,128)} %merge.1), calls=%async_computation.3 | async-start | bytes 147456 | tf_op jit(solution)/shard_map/all_to_all | solution.py:25

commit v9 on v8

--- a/solution.py
+++ b/solution.py
@@ -57,7 +57,9 @@
 
 def copies_kernel(source, factor, local, out, right, noise, sems):
     copy = pltpu.make_async_copy(source, noise, sems.at[0])
-    fetch = pltpu.make_async_copy(factor, right, sems.at[1])
+    half = right.shape[0]
+    away = (1 - lax.axis_index("col_1")) * half
+    fetch = pltpu.make_async_copy(factor.at[pl.ds(away, half)], right, sems.at[1])
     copy.start()
     fetch.start()
     copy.wait()
@@ -90,23 +92,23 @@
     counts[...] = nt_dot(jnp.ones((8, onehot.shape[1]), BF16), onehot[...])
 
 
-def order_kernel(local, other, out):
-    first = lax.axis_index("col_1") == 0
-    own = local[...].astype(F32)
-    far = other[...].astype(F32)
-    out[:16] = jnp.where(first, own, far).astype(BF16)
-    out[16:] = jnp.where(first, far, own).astype(BF16)
+def payload_kernel(keep, received, local, other, out):
+    for g in range(keep.shape[0]):
+        out[8 * g : 8 * g + 8] = (keep[g] + received[g]) * SUM_UNIT
+    out[64:80] = local[...].astype(F32) * NOISE_UNIT
+    out[80:] = other[...].astype(F32) * NOISE_UNIT
 
 
 def project_kernel(columns, right, out, *, away):
     row, core = lax.axis_index(ROW), lax.axis_index("col_1")
     half = 1 - core if away else core
     tiles = 2 * columns.shape[0]
-    groups = right.shape[0] // 8
+    groups = out.shape[0]
     lane = lax.broadcasted_iota(jnp.int32, (8, 128), 1)
 
     def step(g, carry):
         base = (half * groups + g) * 4
+        at = 4 * g if away else base
         blocks = []
         low = []
         for n in range(4):
@@ -115,7 +117,7 @@
             first = tile < tiles // 2
             blocks.append(columns[jnp.where(first, tile, tiles - 1 - tile)])
             low.append(first)
-        factor = right[pl.ds(base, 4)].reshape(256, 256)
+        factor = right[pl.ds(at, 4)].reshape(256, 256)
         full = nt_dot(jnp.concatenate(blocks, axis=0), factor)
         parts = []
         for n in range(4):
@@ -128,10 +130,10 @@
     lax.fori_loop(0, groups, step, 0, unroll=4)
 
 
-def on_diag_kernel(n0, n1, n2, n3, diag, out):
-    col, chip = lax.axis_index(COL), lax.axis_index("col_0")
+def on_diag_kernel(local, other, n1, n2, n3, diag, out):
+    col, chip, mine = lax.axis_index(COL), lax.axis_index("col_0"), lax.axis_index("col_1")
     span = diag.shape[1]
-    own = jnp.where(lax.axis_index("col_1") == 0, n0[:16].astype(F32), n0[16:].astype(F32))
+    own = local[...].astype(F32)
     i_at = lax.broadcasted_iota(jnp.int32, (span, span), 0)
     j_at = lax.broadcasted_iota(jnp.int32, (span, span), 1)
     acc = [own, own]
@@ -139,10 +141,13 @@
     for h in range(2):
         corner = jnp.where(j_at < i_at, diag[h, :, pl.ds(at, span)].astype(F32), 0.0).astype(BF16)
         acc[h] = acc[h] + nt_dot(own.astype(BF16), corner)
-    for noise, turn in zip((n0, n1, n2, n3), (0, *TURNS)):
-        for core in range(2):
+    near = ((local, 0), (other, 0))
+    for turn, places in zip(
+        (0, *TURNS), (near, ((n1, 0), (n1, 16)), ((n2, 0), (n2, 16)), ((n3, 0), (n3, 16)))
+    ):
+        for core, (noise, row) in zip((mine, 1 - mine), places):
             number = 2 * lax.rem(chip + 4 - turn, 4) + core
-            piece = noise[16 * core : 16 * core + 16].astype(F32)
+            piece = noise[row : row + 16].astype(F32)
             piece = jnp.where(number < col, piece, 0.0).astype(BF16)
             from_ = pl.multiple_of(number * span, span)
             for h in range(2):
@@ -215,7 +220,7 @@
         out[:, pl.ds(at, 128)] = lookup(words, unit, a) - other
         return carry
 
-    lax.fori_loop(0, first.shape[1] // 128, step, 0, unroll=8)
+    lax.fori_loop(0, first.shape[1] // 128, step, 0, unroll=16)
 
 
 def emit_kernel(samples, out):
@@ -242,7 +247,7 @@
         pieces[:, pl.ds(at, 128)] = jnp.concatenate([top, value - top], axis=0).astype(BF16)
         return carry
 
-    lax.fori_loop(0, partner.shape[1] // 128, step, 0, unroll=8)
+    lax.fori_loop(0, partner.shape[1] // 128, step, 0, unroll=16)
     total = nt_dot(pieces[...], onehot[...])
     sums = total[:8] + total[8:]
     put_rows(out, [sums[i : i + 1] for i in range(8)] + [counts[:1]])
@@ -278,12 +283,12 @@
     first, partner, bins = pair_first[0], pair_partner[0], bin_ids[0]
     pairs = first.shape[1]
 
-    local, spread_noise, right = call(
+    local, spread_noise, right_away = call(
         copies_kernel,
         (
             vmem((16, span), BF16),
             vmem((rows, 16, span), BF16),
-            vmem(right_factor.shape[1:], BF16),
+            vmem((32, 64, span), BF16),
         ),
         [HB, HB],
         scratch_shapes=[pltpu.VMEM((8, 2, span), BF16), pltpu.SemaphoreType.DMA((2,))],
@@ -306,27 +311,29 @@
             [VM, VM],
             flops=1 << 28,
             name=name,
-        )(columns, right)
+        )(columns, right_away if away else right_factor[0])
 
     send = project(True, "send")
     received = lax.ppermute(send, "col_1", swap)
     keep = project(False, "keep")
-    pair = keep + received
-    noises = call(order_kernel, vmem((32, span), BF16), [VM, VM], name="order")(local, other_noise)
-    noises16 = (noises.astype(F32) * NOISE_UNIT).astype(F16)
-    payload = jnp.concatenate([(pair * SUM_UNIT).astype(F16).reshape(64, 256), noises16])
+    payload = call(payload_kernel, vmem((96, span), F32), [VM] * 4, name="payload")(
+        keep, received, local, other_noise
+    ).astype(F16)
     arrived = []
     for turn in TURNS:
         arrived.append(
             lax.ppermute(payload, "col_0", [(chip, (chip + turn) % 4) for chip in range(4)])
         )
-    total = sum(x[:64].astype(F32) for x in arrived).reshape(8, 8, 256) * (1.0 / SUM_UNIT) + pair
+    total = sum(x[:64].astype(F32) for x in arrived).reshape(8, 8, span) * (1.0 / SUM_UNIT)
+    total = (total + keep) + received
     mine = jnp.where(allowed > 0.5, total, 0.0).astype(BF16)
-    all_noise = [noises] + [(x[64:].astype(F32) * (1.0 / NOISE_UNIT)).astype(BF16) for x in arrived]
+    all_noise = [
+        (x[64:].astype(F32) * (1.0 / NOISE_UNIT)).astype(BF16) for x in arrived
+    ]
     theirs = lax.ppermute(mine, "col_1", swap)
     on_diag = call(
-        on_diag_kernel, vmem((16, span), F32), [VM] * 5, flops=1 << 28, name="ondiag"
-    )(*all_noise, diag_factor[:, 0])
+        on_diag_kernel, vmem((16, span), F32), [VM] * 6, flops=1 << 28, name="ondiag"
+    )(local, other_noise, *all_noise, diag_factor[:, 0])
     copies, own_samples = call(
         sample_kernel,
         (vmem((cols, 16, span), BF16), vmem((16, span), F32)),

time: 84.9 us -> 84.7 us (level)
  blocking collectives: 27.8 us -> 45 us
  starting transfers between devices: 29 us -> 18.8 us
  waiting for transfers between devices: 15.8 us -> 9.93 us
  Pallas kernels: 11 us -> 9.76 us
    all_to_all x2 -> x3, blocking collectives: 27.8 us -> 45 us  [exchange(): return lax.all_to_all(copies, axis, 0, 0, tiled=True)]
    all_to_all x2 -> x1, starting transfers between devices: 13.3 us -> 4.03 us  [exchange(): return lax.all_to_all(copies, axis, 0, 0, tiled=True)]
    all_to_all x2 -> x1, waiting for transfers between devices: 11.6 us -> 5.92 us  [exchange(): return lax.all_to_all(copies, axis, 0, 0, tiled=True)]
    pallas_call x12, Pallas kernels: 11 us -> 9.76 us  [held(): run(*(a if spec is SM else pltpu.with_memory_space_constraint(a, spec.mem...]
    ppermute x1, starting transfers between devices: 1.04 us -> 0.1 us  [body(): other_noise = lax.ppermute(local, 'col_1', swap)]
  transfers between devices with their start and end apart: 9 -> 8, of which waited for: 6 -> 4; matrix products, arithmetic and copies ran while one was open for 0% -> 0% of each run, Pallas kernels for 6% -> 6%
where the time goes in v9:
time: 84.7 us; the launch traced here: 84.4 us
  blocking collectives  45 us (53%)
  starting transfers between devices  18.8 us (22%)
  waiting for transfers between devices  9.93 us (12%)
  Pallas kernels  9.76 us (12%)
    all_to_all x3, blocking collectives, exchange(): return lax.all_to_all(copies, axis, 0, 0, tiled=True)  45 us
    pallas_call x12, Pallas kernels, held(): run(*(a if spec is SM else pltpu.with_memory_space_constraint(a, spec.mem...  9.76 us
    ppermute x3, starting transfers between devices, body(): lax.ppermute(payload, 'col_0', [(chip, (chip + turn) % 4) for chip in ran...  8.46 us
    all_to_all x1, waiting for transfers between devices, exchange(): return lax.all_to_all(copies, axis, 0, 0, tiled=True)  5.92 us
    all_to_all x1, starting transfers between devices, exchange(): return lax.all_to_all(copies, axis, 0, 0, tiled=True)  4.03 us
    ppermute x3, waiting for transfers between devices, body(): lax.ppermute(payload, 'col_0', [(chip, (chip + turn) % 4) for chip in ran...  3.94 us
    ppermute x1, starting transfers between devices, body(): lax.ppermute(own_tiles, ROW, [(source, source + 1) for source in range(ro...  2.45 us
    ppermute x1, starting transfers between devices, body(): received = lax.ppermute(send, 'col_1', swap)  2.18 us
  transfers between devices with their start and end apart: 8, of which 4 were waited for; matrix products, arithmetic and copies ran while one was open for 0% of the time, Pallas kernels for 6%

profile of v9, /device:TPU:1, one launch (start us, length us, event | category | flops | bytes accessed | tf_op | source)
XLA Modules:
  0.0 84.4 jit_solution(11010019183107910089)
XLA Ops:
  0.6 0.0 copy-start
  0.6 0.0 copy-start.3
  0.7 0.0 copy-start.5
  0.7 1.4 %copies.1 = (bf16[16,256]{1,0:T(8,128)(2,1)S(1)}, bf16[32,16,256]{2,1,0:T(8,128)(2,1)S(1)}, bf16[32,64,256]{2,1,0:T(8,128)(2,1)S(1)}) custom-call(bf16[8,2,256]{2,1,0:T(2,128)(2,1)} %bitcast.26, bf16[64,64,256]{2,1,0:T(8,128)(2,1)} %bitcast.18), custom_call_target="tpu_custom_call" | custom-call | flops 1 | bytes 1048576 | tf_op jit(solution)/shard_map/copies/pallas_call | solution.py:48
  2.1 17.0 %all_to_all.20.columns = bf16[32,16,256]{2,1,0:T(8,128)(2,1)S(1)} all-to-all(bf16[32,16,256]{2,1,0:T(8,128)(2,1)S(1)} %get-tuple-element.11), channel_id=1, replica_groups=mesh['row_0'=4,'row_1'=2,'row_2'=4,'col_0'=4,'col_1'=2] {'row_0','row_1'..., dimensions={0} | all-to-all | bytes 524288 | tf_op jit(solution)/shard_map/all_to_all | solution.py:25
  19.1 0.0 copy-start.1
  19.1 0.6 send.1
  19.7 2.2 %collective-permute-start = (f32[8,8,256]{2,1,0:T(8,128)S(1)}, f32[8,8,256]{2,1,0:T(8,128)S(1)}, u32[]{:S(2)}, u32[]{:S(2)}) collective-permute-start(f32[8,8,256]{2,1,0:T(8,128)S(1)} %send.1), channel_id=1, source_target_pairs={{0,1},{1,0},{2,3},{3,2},{4,5},{5,4},{6,7},{7,6},{8,9},{9,8},{10,11... | collective-permute-start | bytes 196616 | tf_op jit(solution)/shard_map/ppermute | solution.py:317
  21.8 0.1 collective-permute-start.1
  21.9 0.0 copy-done.3
  21.9 0.0 copy-done.5
  21.9 1.3 %prepare.1 = (bf16[128,4096]{1,0:T(8,128)(2,1)S(1)}, f32[8,1,256]{2,1,0:T(1,128)S(1)}, f32[8,128]{1,0:T(8,128)S(1)}) custom-call(s32[1,4096]{1,0:T(1,128)S(1)} %bitcast.22, s32[1,64]{1,0:T(1,128)S(1)} %copy-done.5), custom_call_target="tpu_custom_call" | custom-call | flops 1048576 | bytes 1048576 | tf_op jit(solution)/shard_map/prepare/pallas_call | solution.py:48
  23.2 0.0 copy-done
  23.2 0.0 copy-start.2
  23.2 0.6 keep.1
  23.8 0.0 collective-permute-done.1.other
  23.8 0.0 collective-permute-done.received
  23.9 5.2 %collective-permute-start.4 = (f16[96,256]{1,0:T(8,128)(2,1)S(1)}, f16[96,256]{1,0:T(8,128)(2,1)S(1)}, u32[]{:S(2)}, u32[]{:S(2)}) collective-permute-start(f16[96,256]{1,0:T(8,128)(2,1)S(1)} %convert_element_type.33), channel_id=1, source_target_pairs={{0,6},{2,0},{4,2},{6,4},{1,7},{3,1},{5,3},{7,5},{8,14},{10,8},{12,... | collective-permute-start | bytes 147464 | tf_op jit(solution)/shard_map/ppermute | solution.py:325
  29.1 0.0 collective-permute-start.3
  29.1 3.3 %collective-permute-start.2 = (f16[96,256]{1,0:T(8,128)(2,1)S(1)}, f16[96,256]{1,0:T(8,128)(2,1)S(1)}, u32[]{:S(2)}, u32[]{:S(2)}) collective-permute-start(f16[96,256]{1,0:T(8,128)(2,1)S(1)} %convert_element_type.33), channel_id=1, source_target_pairs={{0,4},{2,6},{4,0},{6,2},{1,5},{3,7},{5,1},{7,3},{8,12},{10,14},{12... | collective-permute-start | bytes 147464 | tf_op jit(solution)/shard_map/ppermute | solution.py:325
  32.4 0.0 collective-permute-done.4
  32.4 2.4 %collective-permute-done.3 = f16[96,256]{1,0:T(8,128)(2,1)S(1)} collective-permute-done((f16[96,256]{1,0:T(8,128)(2,1)S(1)}, f16[96,256]{1,0:T(8,128)(2,1)S(1)}, u32[]{:S(2)}, u32[]{:S(2)}) %collective-permute-start.3) | collective-permute-done | bytes 49184 | tf_op jit(solution)/shard_map/ppermute | solution.py:325
  34.8 1.6 %collective-permute-done.2 = f16[96,256]{1,0:T(8,128)(2,1)S(1)} collective-permute-done((f16[96,256]{1,0:T(8,128)(2,1)S(1)}, f16[96,256]{1,0:T(8,128)(2,1)S(1)}, u32[]{:S(2)}, u32[]{:S(2)}) %collective-permute-start.2) | collective-permute-done | bytes 49184 | tf_op jit(solution)/shard_map/ppermute | solution.py:325
  36.3 1.6 %collective-permute-start.5 = (bf16[8,8,256]{2,1,0:T(8,128)(2,1)S(1)}, bf16[8,8,256]{2,1,0:T(8,128)(2,1)S(1)}, u32[]{:S(2)}, u32[]{:S(2)}) collective-permute-start(bf16[8,8,256]{2,1,0:T(8,128)(2,1)S(1)} %fusion.2.mine), channel_id=1, source_target_pairs={{0,1},{1,0},{2,3},{3,2},{4,5},{5,4},{6,7},{7,6},{8,9},{9,8},{10,11... | collective-permute-start | bytes 98312 | tf_op jit(solution)/shard_map/ppermute | solution.py:333
  37.9 0.0 copy-done.1
  37.9 0.0 copy-start.4
  38.0 0.0 copy-start.6
  38.0 0.7 ondiag.1.on_diag
  38.7 0.1 collective-permute-done.5.theirs
  38.8 0.0 copy-done.2
  38.8 0.4 samples.1
  39.2 13.3 %all_to_all.21.table = bf16[8,16,256]{2,1,0:T(8,128)(2,1)S(1)} all-to-all(bf16[8,16,256]{2,1,0:T(8,128)(2,1)S(1)} %get-tuple-element.15), channel_id=1, replica_groups=mesh['row_0'=4,'row_1'=2,'row_2'=4,'col_0'=4,'col_1'=2] {'col_0','col_1'}, dimensions={0} | all-to-all | bytes 131072 | tf_op jit(solution)/shard_map/all_to_all | solution.py:25
  52.5 2.4 %collective-permute-start.6 = (bf16[8,16,256]{2,1,0:T(8,128)(2,1)S(1)}, bf16[8,16,256]{2,1,0:T(8,128)(2,1)S(1)}, u32[]{:S(2)}, u32[]{:S(2)}) collective-permute-start(bf16[8,16,256]{2,1,0:T(8,128)(2,1)S(1)} %all_to_all.21.table), channel_id=1, source_target_pairs={{0,8},{8,16},{16,24},{24,32},{32,40},{40,48},{48,56},{56,64},{64,7... | collective-permute-start | bytes 196616 | tf_op jit(solution)/shard_map/ppermute | solution.py:345
  54.9 0.0 copy-done.4
  54.9 0.0 copy-done.6
  55.0 1.5 %own.1.base = f32[8,4096]{1,0:T(8,128)S(1)} custom-call(bf16[8,16,256]{2,1,0:T(8,128)(2,1)S(1)} %all_to_all.21.table, s32[1,4096]{1,0:T(1,128)S(1)} %bitcast.25, s32[1,4096]{1,0:T(1,128)S(1)} %bitcast.23), custom_call_target="tpu_custom_call" | custom-call | flops 67108864 | bytes 1048576 | tf_op jit(solution)/shard_map/own/pallas_call | solution.py:48
  56.5 0.0 collective-permute-done.6.prev
  56.5 1.3 %bins.1 = f32[16,1,1152]{2,1,0:T(1,128)S(1)} custom-call(bf16[8,16,256]{2,1,0:T(8,128)(2,1)S(1)} %collective-permute-done.6.prev, s32[1,4096]{1,0:T(1,128)S(1)} %bitcast.24, f32[8,4096]{1,0:T(8,128)S(1)} %own.1.base, bf16[128,4096]{1,0:T(8,128)(2,1)S(1)} %get-tuple-element.16.onehot, f32[8,128]{1,0:T(8,128)S(1)} %get-tuple-element.17.counts), custom_call_target="tpu_custom_call" | custom-call | flops 67108864 | bytes 1048576 | tf_op jit(solution)/shard_map/bins/pallas_call | solution.py:48
  57.8 14.7 %all_to_all.22.parts = f32[16,1,1152]{2,1,0:T(1,128)S(1)} all-to-all(f32[16,1,1152]{2,1,0:T(1,128)S(1)} %bins.1), channel_id=1, replica_groups=mesh['row_0'=4,'row_1'=2,'row_2'=4,'col_0'=4,'col_1'=2] {'row_1','col_0'..., dimensions={0} | all-to-all | bytes 147456 | tf_op jit(solution)/shard_map/all_to_all | solution.py:25
  72.5 0.7 merge.1
  73.2 4.0 %all-to-all-start.3 = ((f32[16,1,1152]{2,1,0:T(1,128)}), f32[16,1,1152]{2,1,0:T(1,128)S(1)}, u32[]{:S(2)}, u32[]{:S(2)}) async-start(f32[16,1,1152]{2,1,0:T(1,128)} %merge.1), calls=%async_computation.3 | async-start | bytes 147456 | tf_op jit(solution)/shard_map/all_to_all | solution.py:25
  77.3 0.6 emit.1
  77.9 5.9 %all-to-all-done.3.parts = f32[16,1,1152]{2,1,0:T(1,128)S(1)} async-done(((f32[16,1,1152]{2,1,0:T(1,128)}), f32[16,1,1152]{2,1,0:T(1,128)S(1)}, u32[]{:S(2)}, u32[]{:S(2)}) %all-to-all-start.3) | async-done | bytes 73760 | tf_op jit(solution)/shard_map/all_to_all | solution.py:25
  83.8 0.6 finish.1
  (8 shorter events, 0.1 us)
Async XLA Ops:
  0.6 22.6 %copy-start = (bf16[1,64,64,256]{3,2,1,0:T(8,128)(2,1)S(1)}, bf16[1,64,64,256]{3,2,1,0:T(8,128)(2,1)}, u32[]{:S(2)}) copy-start(bf16[1,64,64,256]{3,2,1,0:T(8,128)(2,1)} %param.11) | copy-start | bytes 6291460
  0.6 21.3 %copy-start.3 = (s32[1,1,4096]{2,1,0:T(1,128)S(1)}, s32[1,1,4096]{2,1,0:T(1,128)}, u32[]{:S(2)}) copy-start(s32[1,1,4096]{2,1,0:T(1,128)} %param.15) | copy-start | bytes 49156
  0.7 21.3 %copy-start.5 = (s32[1,64]{1,0:T(1,128)S(1)}, s32[1,64]{1,0:T(1,128)}, u32[]{:S(2)}) copy-start(s32[1,64]{1,0:T(1,128)} %ranks.1) | copy-start | bytes 772
  19.1 18.8 %copy-start.1 = (bf16[2,1,256,2048]{3,2,1,0:T(8,128)(2,1)S(1)}, bf16[2,1,256,2048]{3,2,1,0:T(8,128)(2,1)}, u32[]{:S(2)}) copy-start(bf16[2,1,256,2048]{3,2,1,0:T(8,128)(2,1)} %param.9) | copy-start | bytes 6291460
  19.7 4.2 %collective-permute-start = (f32[8,8,256]{2,1,0:T(8,128)S(1)}, f32[8,8,256]{2,1,0:T(8,128)S(1)}, u32[]{:S(2)}, u32[]{:S(2)}) collective-permute-start(f32[8,8,256]{2,1,0:T(8,128)S(1)} %send.1), channel_id=1, source_target_pairs={{0,1},{1,0},{2,3},{3,2},{4,5},{5,4},{6,7},{7,6},{8,9},{9,8},{10,11... | collective-permute-start | bytes 196616 | tf_op jit(solution)/shard_map/ppermute | solution.py:317
  21.8 2.0 %collective-permute-start.1 = (bf16[16,256]{1,0:T(8,128)(2,1)S(1)}, bf16[16,256]{1,0:T(8,128)(2,1)S(1)}, u32[]{:S(2)}, u32[]{:S(2)}) collective-permute-start(bf16[16,256]{1,0:T(8,128)(2,1)S(1)} %get-tuple-element.13.local), channel_id=1, source_target_pairs={{0,1},{1,0},{2,3},{3,2},{4,5},{5,4},{6,7},{7,6},{8,9},{9,8},{10,11... | collective-permute-start | bytes 24584 | tf_op jit(solution)/shard_map/ppermute | solution.py:305
  23.2 15.5 %copy-start.2 = (bf16[1,64,64,256]{3,2,1,0:T(8,128)(2,1)S(1)}, bf16[1,64,64,256]{3,2,1,0:T(8,128)(2,1)}, u32[]{:S(2)}) copy-start(bf16[1,64,64,256]{3,2,1,0:T(8,128)(2,1)} %param.10) | copy-start | bytes 6291460
  23.9 8.5 %collective-permute-start.4 = (f16[96,256]{1,0:T(8,128)(2,1)S(1)}, f16[96,256]{1,0:T(8,128)(2,1)S(1)}, u32[]{:S(2)}, u32[]{:S(2)}) collective-permute-start(f16[96,256]{1,0:T(8,128)(2,1)S(1)} %convert_element_type.33), channel_id=1, source_target_pairs={{0,6},{2,0},{4,2},{6,4},{1,7},{3,1},{5,3},{7,5},{8,14},{10,8},{12,... | collective-permute-start | bytes 147464 | tf_op jit(solution)/shard_map/ppermute | solution.py:325
  29.1 5.7 %collective-permute-start.3 = (f16[96,256]{1,0:T(8,128)(2,1)S(1)}, f16[96,256]{1,0:T(8,128)(2,1)S(1)}, u32[]{:S(2)}, u32[]{:S(2)}) collective-permute-start(f16[96,256]{1,0:T(8,128)(2,1)S(1)} %convert_element_type.33), channel_id=1, source_target_pairs={{0,2},{2,4},{4,6},{6,0},{1,3},{3,5},{5,7},{7,1},{8,10},{10,12},{12... | collective-permute-start | bytes 147464 | tf_op jit(solution)/shard_map/ppermute | solution.py:325
  29.1 7.2 %collective-permute-start.2 = (f16[96,256]{1,0:T(8,128)(2,1)S(1)}, f16[96,256]{1,0:T(8,128)(2,1)S(1)}, u32[]{:S(2)}, u32[]{:S(2)}) collective-permute-start(f16[96,256]{1,0:T(8,128)(2,1)S(1)} %convert_element_type.33), channel_id=1, source_target_pairs={{0,4},{2,6},{4,0},{6,2},{1,5},{3,7},{5,1},{7,3},{8,12},{10,14},{12... | collective-permute-start | bytes 147464 | tf_op jit(solution)/shard_map/ppermute | solution.py:325
  36.3 2.4 %collective-permute-start.5 = (bf16[8,8,256]{2,1,0:T(8,128)(2,1)S(1)}, bf16[8,8,256]{2,1,0:T(8,128)(2,1)S(1)}, u32[]{:S(2)}, u32[]{:S(2)}) collective-permute-start(bf16[8,8,256]{2,1,0:T(8,128)(2,1)S(1)} %fusion.2.mine), channel_id=1, source_target_pairs={{0,1},{1,0},{2,3},{3,2},{4,5},{5,4},{6,7},{7,6},{8,9},{9,8},{10,11... | collective-permute-start | bytes 98312 | tf_op jit(solution)/shard_map/ppermute | solution.py:333
  37.9 17.0 %copy-start.4 = (s32[1,1,4096]{2,1,0:T(1,128)S(1)}, s32[1,1,4096]{2,1,0:T(1,128)}, u32[]{:S(2)}) copy-start(s32[1,1,4096]{2,1,0:T(1,128)} %param.14) | copy-start | bytes 49156
  38.0 17.0 %copy-start.6 = (s32[1,1,4096]{2,1,0:T(1,128)S(1)}, s32[1,1,4096]{2,1,0:T(1,128)}, u32[]{:S(2)}) copy-start(s32[1,1,4096]{2,1,0:T(1,128)} %param.13) | copy-start | bytes 49156
  52.5 4.0 %collective-permute-start.6 = (bf16[8,16,256]{2,1,0:T(8,128)(2,1)S(1)}, bf16[8,16,256]{2,1,0:T(8,128)(2,1)S(1)}, u32[]{:S(2)}, u32[]{:S(2)}) collective-permute-start(bf16[8,16,256]{2,1,0:T(8,128)(2,1)S(1)} %all_to_all.21.table), channel_id=1, source_target_pairs={{0,8},{8,16},{16,24},{24,32},{32,40},{40,48},{48,56},{56,64},{64,7... | collective-permute-start | bytes 196616 | tf_op jit(solution)/shard_map/ppermute | solution.py:345
  73.2 10.6 %all-to-all-start.3 = ((f32[16,1,1152]{2,1,0:T(1,128)}), f32[16,1,1152]{2,1,0:T(1,128)S(1)}, u32[]{:S(2)}, u32[]{:S(2)}) async-start(f32[16,1,1152]{2,1,0:T(1,128)} %merge.1), calls=%async_computation.3 | async-start | bytes 147456 | tf_op jit(solution)/shard_map/all_to_all | solution.py:25

commit v10 on v9

--- a/solution.py
+++ b/solution.py
@@ -55,20 +55,15 @@
     return held
 
 
-def copies_kernel(source, factor, local, out, right, noise, sems):
-    copy = pltpu.make_async_copy(source, noise, sems.at[0])
-    half = right.shape[0]
-    away = (1 - lax.axis_index("col_1")) * half
-    fetch = pltpu.make_async_copy(factor.at[pl.ds(away, half)], right, sems.at[1])
+def copies_kernel(source, local, out, noise, sem):
+    copy = pltpu.make_async_copy(source, noise, sem)
     copy.start()
-    fetch.start()
     copy.wait()
     rows = [noise[s].astype(F32)[h : h + 1] for h in range(2) for s in range(8)]
     mine = jnp.concatenate(rows, axis=0).astype(BF16)
     local[...] = mine
     for n in range(out.shape[0]):
         out[n] = mine
-    fetch.wait()
 
 
 def prepare_kernel(bins, ranks, onehot, keep, counts):
@@ -108,7 +103,6 @@
 
     def step(g, carry):
         base = (half * groups + g) * 4
-        at = 4 * g if away else base
         blocks = []
         low = []
         for n in range(4):
@@ -117,7 +111,7 @@
             first = tile < tiles // 2
             blocks.append(columns[jnp.where(first, tile, tiles - 1 - tile)])
             low.append(first)
-        factor = right[pl.ds(at, 4)].reshape(256, 256)
+        factor = right[pl.ds(base, 4)].reshape(256, 256)
         full = nt_dot(jnp.concatenate(blocks, axis=0), factor)
         parts = []
         for n in range(4):
@@ -283,17 +277,17 @@
     first, partner, bins = pair_first[0], pair_partner[0], bin_ids[0]
     pairs = first.shape[1]
 
-    local, spread_noise, right_away = call(
+    local, spread_noise = call(
         copies_kernel,
         (
             vmem((16, span), BF16),
             vmem((rows, 16, span), BF16),
-            vmem((32, 64, span), BF16),
         ),
-        [HB, HB],
-        scratch_shapes=[pltpu.VMEM((8, 2, span), BF16), pltpu.SemaphoreType.DMA((2,))],
+        [HB],
+        flops=1 << 30,
+        scratch_shapes=[pltpu.VMEM((8, 2, span), BF16), pltpu.SemaphoreType.DMA(())],
         name="copies",
-    )(jnp.transpose(noise, (0, 2, 1, 3))[:, 0], right_factor[0])
+    )(jnp.transpose(noise, (0, 2, 1, 3))[:, 0])
     columns = exchange(spread_noise, ROW)
     onehot, allowed, counts = call(
         prepare_kernel,
@@ -311,7 +305,7 @@
             [VM, VM],
             flops=1 << 28,
             name=name,
-        )(columns, right_away if away else right_factor[0])
+        )(columns, right_factor[0])
 
     send = project(True, "send")
     received = lax.ppermute(send, "col_1", swap)

time: 84.7 us -> 84.2 us (level)
  no operation moved by 1% of the time
where the time goes in v10:
time: 84.2 us; the launch traced here: 83.9 us
  blocking collectives  45 us (53%)
  starting transfers between devices  18.8 us (22%)
  waiting for transfers between devices  9.93 us (12%)
  Pallas kernels  9.22 us (11%)
    all_to_all x3, blocking collectives, exchange(): return lax.all_to_all(copies, axis, 0, 0, tiled=True)  45 us
    pallas_call x12, Pallas kernels, held(): run(*(a if spec is SM else pltpu.with_memory_space_constraint(a, spec.mem...  9.22 us
    ppermute x3, starting transfers between devices, body(): lax.ppermute(payload, 'col_0', [(chip, (chip + turn) % 4) for chip in ran...  8.46 us
    all_to_all x1, waiting for transfers between devices, exchange(): return lax.all_to_all(copies, axis, 0, 0, tiled=True)  5.92 us
    all_to_all x1, starting transfers between devices, exchange(): return lax.all_to_all(copies, axis, 0, 0, tiled=True)  4.03 us
    ppermute x3, waiting for transfers between devices, body(): lax.ppermute(payload, 'col_0', [(chip, (chip + turn) % 4) for chip in ran...  3.94 us
    ppermute x1, starting transfers between devices, body(): lax.ppermute(own_tiles, ROW, [(source, source + 1) for source in range(ro...  2.45 us
    ppermute x1, starting transfers between devices, body(): received = lax.ppermute(send, 'col_1', swap)  2.17 us
  transfers between devices with their start and end apart: 8, of which 4 were waited for; matrix products, arithmetic and copies ran while one was open for 0% of the time, Pallas kernels for 6%

profile of v10, /device:TPU:1, one launch (start us, length us, event | category | flops | bytes accessed | tf_op | source)
XLA Modules:
  0.0 83.9 jit_solution(7609498681062121301)
XLA Ops:
  0.6 0.0 copy-start
  0.6 0.9 %copies.1 = (bf16[16,256]{1,0:T(8,128)(2,1)S(1)}, bf16[32,16,256]{2,1,0:T(8,128)(2,1)S(1)}) custom-call(bf16[8,2,256]{2,1,0:T(2,128)(2,1)} %bitcast.27), custom_call_target="tpu_custom_call" | custom-call | flops 1073741824 | bytes 1048576 | tf_op jit(solution)/shard_map/copies/pallas_call | solution.py:48
  1.5 0.0 copy-start.3
  1.5 0.0 copy-start.5
  1.6 17.0 %all_to_all.20.columns = bf16[32,16,256]{2,1,0:T(8,128)(2,1)S(1)} all-to-all(bf16[32,16,256]{2,1,0:T(8,128)(2,1)S(1)} %get-tuple-element.10), channel_id=1, replica_groups=mesh['row_0'=4,'row_1'=2,'row_2'=4,'col_0'=4,'col_1'=2] {'row_0','row_1'..., dimensions={0} | all-to-all | bytes 524288 | tf_op jit(solution)/shard_map/all_to_all | solution.py:25
  18.6 0.0 copy-done
  18.6 0.6 send.1
  19.1 0.0 copy-start.1
  19.2 2.2 %collective-permute-start = (f32[8,8,256]{2,1,0:T(8,128)S(1)}, f32[8,8,256]{2,1,0:T(8,128)S(1)}, u32[]{:S(2)}, u32[]{:S(2)}) collective-permute-start(f32[8,8,256]{2,1,0:T(8,128)S(1)} %send.1), channel_id=1, source_target_pairs={{0,1},{1,0},{2,3},{3,2},{4,5},{5,4},{6,7},{7,6},{8,9},{9,8},{10,11... | collective-permute-start | bytes 196616 | tf_op jit(solution)/shard_map/ppermute | solution.py:311
  21.3 0.1 collective-permute-start.1
  21.4 0.0 copy-done.3
  21.4 0.0 copy-done.5
  21.4 1.3 %prepare.1 = (bf16[128,4096]{1,0:T(8,128)(2,1)S(1)}, f32[8,1,256]{2,1,0:T(1,128)S(1)}, f32[8,128]{1,0:T(8,128)S(1)}) custom-call(s32[1,4096]{1,0:T(1,128)S(1)} %bitcast.22, s32[1,64]{1,0:T(1,128)S(1)} %copy-done.5), custom_call_target="tpu_custom_call" | custom-call | flops 1048576 | bytes 1048576 | tf_op jit(solution)/shard_map/prepare/pallas_call | solution.py:48
  22.7 0.0 copy-start.2
  22.7 0.6 keep.1
  23.3 0.0 collective-permute-done.1.other
  23.3 0.0 collective-permute-done.received
  23.4 5.2 %collective-permute-start.4 = (f16[96,256]{1,0:T(8,128)(2,1)S(1)}, f16[96,256]{1,0:T(8,128)(2,1)S(1)}, u32[]{:S(2)}, u32[]{:S(2)}) collective-permute-start(f16[96,256]{1,0:T(8,128)(2,1)S(1)} %convert_element_type.33), channel_id=1, source_target_pairs={{0,6},{2,0},{4,2},{6,4},{1,7},{3,1},{5,3},{7,5},{8,14},{10,8},{12,... | collective-permute-start | bytes 147464 | tf_op jit(solution)/shard_map/ppermute | solution.py:319
  28.6 0.0 collective-permute-start.3
  28.6 3.3 %collective-permute-start.2 = (f16[96,256]{1,0:T(8,128)(2,1)S(1)}, f16[96,256]{1,0:T(8,128)(2,1)S(1)}, u32[]{:S(2)}, u32[]{:S(2)}) collective-permute-start(f16[96,256]{1,0:T(8,128)(2,1)S(1)} %convert_element_type.33), channel_id=1, source_target_pairs={{0,4},{2,6},{4,0},{6,2},{1,5},{3,7},{5,1},{7,3},{8,12},{10,14},{12... | collective-permute-start | bytes 147464 | tf_op jit(solution)/shard_map/ppermute | solution.py:319
  31.8 0.0 collective-permute-done.4
  31.8 2.4 %collective-permute-done.3 = f16[96,256]{1,0:T(8,128)(2,1)S(1)} collective-permute-done((f16[96,256]{1,0:T(8,128)(2,1)S(1)}, f16[96,256]{1,0:T(8,128)(2,1)S(1)}, u32[]{:S(2)}, u32[]{:S(2)}) %collective-permute-start.3) | collective-permute-done | bytes 49184 | tf_op jit(solution)/shard_map/ppermute | solution.py:319
  34.2 1.6 %collective-permute-done.2 = f16[96,256]{1,0:T(8,128)(2,1)S(1)} collective-permute-done((f16[96,256]{1,0:T(8,128)(2,1)S(1)}, f16[96,256]{1,0:T(8,128)(2,1)S(1)}, u32[]{:S(2)}, u32[]{:S(2)}) %collective-permute-start.2) | collective-permute-done | bytes 49184 | tf_op jit(solution)/shard_map/ppermute | solution.py:319
  35.8 1.6 %collective-permute-start.5 = (bf16[8,8,256]{2,1,0:T(8,128)(2,1)S(1)}, bf16[8,8,256]{2,1,0:T(8,128)(2,1)S(1)}, u32[]{:S(2)}, u32[]{:S(2)}) collective-permute-start(bf16[8,8,256]{2,1,0:T(8,128)(2,1)S(1)} %fusion.2.mine), channel_id=1, source_target_pairs={{0,1},{1,0},{2,3},{3,2},{4,5},{5,4},{6,7},{7,6},{8,9},{9,8},{10,11... | collective-permute-start | bytes 98312 | tf_op jit(solution)/shard_map/ppermute | solution.py:327
  37.4 0.0 copy-done.1
  37.4 0.0 copy-start.4
  37.4 0.0 copy-start.6
  37.4 0.7 ondiag.1.on_diag
  38.2 0.1 collective-permute-done.5.theirs
  38.2 0.0 copy-done.2
  38.2 0.4 samples.1
  38.6 13.3 %all_to_all.21.table = bf16[8,16,256]{2,1,0:T(8,128)(2,1)S(1)} all-to-all(bf16[8,16,256]{2,1,0:T(8,128)(2,1)S(1)} %get-tuple-element.13), channel_id=1, replica_groups=mesh['row_0'=4,'row_1'=2,'row_2'=4,'col_0'=4,'col_1'=2] {'col_0','col_1'}, dimensions={0} | all-to-all | bytes 131072 | tf_op jit(solution)/shard_map/all_to_all | solution.py:25
  52.0 2.4 %collective-permute-start.6 = (bf16[8,16,256]{2,1,0:T(8,128)(2,1)S(1)}, bf16[8,16,256]{2,1,0:T(8,128)(2,1)S(1)}, u32[]{:S(2)}, u32[]{:S(2)}) collective-permute-start(bf16[8,16,256]{2,1,0:T(8,128)(2,1)S(1)} %all_to_all.21.table), channel_id=1, source_target_pairs={{0,8},{8,16},{16,24},{24,32},{32,40},{40,48},{48,56},{56,64},{64,7... | collective-permute-start | bytes 196616 | tf_op jit(solution)/shard_map/ppermute | solution.py:339
  54.4 0.0 copy-done.4
  54.4 0.0 copy-done.6
  54.4 1.5 %own.1.base = f32[8,4096]{1,0:T(8,128)S(1)} custom-call(bf16[8,16,256]{2,1,0:T(8,128)(2,1)S(1)} %all_to_all.21.table, s32[1,4096]{1,0:T(1,128)S(1)} %bitcast.25, s32[1,4096]{1,0:T(1,128)S(1)} %bitcast.23), custom_call_target="tpu_custom_call" | custom-call | flops 67108864 | bytes 1048576 | tf_op jit(solution)/shard_map/own/pallas_call | solution.py:48
  56.0 0.0 collective-permute-done.6.prev
  56.0 1.3 %bins.1 = f32[16,1,1152]{2,1,0:T(1,128)S(1)} custom-call(bf16[8,16,256]{2,1,0:T(8,128)(2,1)S(1)} %collective-permute-done.6.prev, s32[1,4096]{1,0:T(1,128)S(1)} %bitcast.24, f32[8,4096]{1,0:T(8,128)S(1)} %own.1.base, bf16[128,4096]{1,0:T(8,128)(2,1)S(1)} %get-tuple-element.14.onehot, f32[8,128]{1,0:T(8,128)S(1)} %get-tuple-element.15.counts), custom_call_target="tpu_custom_call" | custom-call | flops 67108864 | bytes 1048576 | tf_op jit(solution)/shard_map/bins/pallas_call | solution.py:48
  57.3 14.7 %all_to_all.22.parts = f32[16,1,1152]{2,1,0:T(1,128)S(1)} all-to-all(f32[16,1,1152]{2,1,0:T(1,128)S(1)} %bins.1), channel_id=1, replica_groups=mesh['row_0'=4,'row_1'=2,'row_2'=4,'col_0'=4,'col_1'=2] {'row_1','col_0'..., dimensions={0} | all-to-all | bytes 147456 | tf_op jit(solution)/shard_map/all_to_all | solution.py:25
  72.0 0.7 merge.1
  72.7 4.0 %all-to-all-start.3 = ((f32[16,1,1152]{2,1,0:T(1,128)}), f32[16,1,1152]{2,1,0:T(1,128)S(1)}, u32[]{:S(2)}, u32[]{:S(2)}) async-start(f32[16,1,1152]{2,1,0:T(1,128)} %merge.1), calls=%async_computation.3 | async-start | bytes 147456 | tf_op jit(solution)/shard_map/all_to_all | solution.py:25
  76.7 0.6 emit.1
  77.4 5.9 %all-to-all-done.3.parts = f32[16,1,1152]{2,1,0:T(1,128)S(1)} async-done(((f32[16,1,1152]{2,1,0:T(1,128)}), f32[16,1,1152]{2,1,0:T(1,128)S(1)}, u32[]{:S(2)}, u32[]{:S(2)}) %all-to-all-start.3) | async-done | bytes 73760 | tf_op jit(solution)/shard_map/all_to_all | solution.py:25
  83.3 0.6 finish.1
  (8 shorter events, 0.1 us)
Async XLA Ops:
  0.6 17.9 %copy-start = (bf16[1,64,64,256]{3,2,1,0:T(8,128)(2,1)S(1)}, bf16[1,64,64,256]{3,2,1,0:T(8,128)(2,1)}, u32[]{:S(2)}) copy-start(bf16[1,64,64,256]{3,2,1,0:T(8,128)(2,1)} %param.11) | copy-start | bytes 6291460
  1.5 19.9 %copy-start.3 = (s32[1,1,4096]{2,1,0:T(1,128)S(1)}, s32[1,1,4096]{2,1,0:T(1,128)}, u32[]{:S(2)}) copy-start(s32[1,1,4096]{2,1,0:T(1,128)} %param.15) | copy-start | bytes 49156
  1.5 19.9 %copy-start.5 = (s32[1,64]{1,0:T(1,128)S(1)}, s32[1,64]{1,0:T(1,128)}, u32[]{:S(2)}) copy-start(s32[1,64]{1,0:T(1,128)} %ranks.1) | copy-start | bytes 772
  19.1 18.3 %copy-start.1 = (bf16[2,1,256,2048]{3,2,1,0:T(8,128)(2,1)S(1)}, bf16[2,1,256,2048]{3,2,1,0:T(8,128)(2,1)}, u32[]{:S(2)}) copy-start(bf16[2,1,256,2048]{3,2,1,0:T(8,128)(2,1)} %param.9) | copy-start | bytes 6291460
  19.2 4.2 %collective-permute-start = (f32[8,8,256]{2,1,0:T(8,128)S(1)}, f32[8,8,256]{2,1,0:T(8,128)S(1)}, u32[]{:S(2)}, u32[]{:S(2)}) collective-permute-start(f32[8,8,256]{2,1,0:T(8,128)S(1)} %send.1), channel_id=1, source_target_pairs={{0,1},{1,0},{2,3},{3,2},{4,5},{5,4},{6,7},{7,6},{8,9},{9,8},{10,11... | collective-permute-start | bytes 196616 | tf_op jit(solution)/shard_map/ppermute | solution.py:311
  21.3 2.0 %collective-permute-start.1 = (bf16[16,256]{1,0:T(8,128)(2,1)S(1)}, bf16[16,256]{1,0:T(8,128)(2,1)S(1)}, u32[]{:S(2)}, u32[]{:S(2)}) collective-permute-start(bf16[16,256]{1,0:T(8,128)(2,1)S(1)} %get-tuple-element.11.local), channel_id=1, source_target_pairs={{0,1},{1,0},{2,3},{3,2},{4,5},{5,4},{6,7},{7,6},{8,9},{9,8},{10,11... | collective-permute-start | bytes 24584 | tf_op jit(solution)/shard_map/ppermute | solution.py:299
  22.7 15.5 %copy-start.2 = (bf16[1,64,64,256]{3,2,1,0:T(8,128)(2,1)S(1)}, bf16[1,64,64,256]{3,2,1,0:T(8,128)(2,1)}, u32[]{:S(2)}) copy-start(bf16[1,64,64,256]{3,2,1,0:T(8,128)(2,1)} %param.10) | copy-start | bytes 6291460
  23.4 8.5 %collective-permute-start.4 = (f16[96,256]{1,0:T(8,128)(2,1)S(1)}, f16[96,256]{1,0:T(8,128)(2,1)S(1)}, u32[]{:S(2)}, u32[]{:S(2)}) collective-permute-start(f16[96,256]{1,0:T(8,128)(2,1)S(1)} %convert_element_type.33), channel_id=1, source_target_pairs={{0,6},{2,0},{4,2},{6,4},{1,7},{3,1},{5,3},{7,5},{8,14},{10,8},{12,... | collective-permute-start | bytes 147464 | tf_op jit(solution)/shard_map/ppermute | solution.py:319
  28.6 5.7 %collective-permute-start.3 = (f16[96,256]{1,0:T(8,128)(2,1)S(1)}, f16[96,256]{1,0:T(8,128)(2,1)S(1)}, u32[]{:S(2)}, u32[]{:S(2)}) collective-permute-start(f16[96,256]{1,0:T(8,128)(2,1)S(1)} %convert_element_type.33), channel_id=1, source_target_pairs={{0,2},{2,4},{4,6},{6,0},{1,3},{3,5},{5,7},{7,1},{8,10},{10,12},{12... | collective-permute-start | bytes 147464 | tf_op jit(solution)/shard_map/ppermute | solution.py:319
  28.6 7.2 %collective-permute-start.2 = (f16[96,256]{1,0:T(8,128)(2,1)S(1)}, f16[96,256]{1,0:T(8,128)(2,1)S(1)}, u32[]{:S(2)}, u32[]{:S(2)}) collective-permute-start(f16[96,256]{1,0:T(8,128)(2,1)S(1)} %convert_element_type.33), channel_id=1, source_target_pairs={{0,4},{2,6},{4,0},{6,2},{1,5},{3,7},{5,1},{7,3},{8,12},{10,14},{12... | collective-permute-start | bytes 147464 | tf_op jit(solution)/shard_map/ppermute | solution.py:319
  35.8 2.4 %collective-permute-start.5 = (bf16[8,8,256]{2,1,0:T(8,128)(2,1)S(1)}, bf16[8,8,256]{2,1,0:T(8,128)(2,1)S(1)}, u32[]{:S(2)}, u32[]{:S(2)}) collective-permute-start(bf16[8,8,256]{2,1,0:T(8,128)(2,1)S(1)} %fusion.2.mine), channel_id=1, source_target_pairs={{0,1},{1,0},{2,3},{3,2},{4,5},{5,4},{6,7},{7,6},{8,9},{9,8},{10,11... | collective-permute-start | bytes 98312 | tf_op jit(solution)/shard_map/ppermute | solution.py:327
  37.4 17.0 %copy-start.4 = (s32[1,1,4096]{2,1,0:T(1,128)S(1)}, s32[1,1,4096]{2,1,0:T(1,128)}, u32[]{:S(2)}) copy-start(s32[1,1,4096]{2,1,0:T(1,128)} %param.14) | copy-start | bytes 49156
  37.4 17.0 %copy-start.6 = (s32[1,1,4096]{2,1,0:T(1,128)S(1)}, s32[1,1,4096]{2,1,0:T(1,128)}, u32[]{:S(2)}) copy-start(s32[1,1,4096]{2,1,0:T(1,128)} %param.13) | copy-start | bytes 49156
  52.0 4.0 %collective-permute-start.6 = (bf16[8,16,256]{2,1,0:T(8,128)(2,1)S(1)}, bf16[8,16,256]{2,1,0:T(8,128)(2,1)S(1)}, u32[]{:S(2)}, u32[]{:S(2)}) collective-permute-start(bf16[8,16,256]{2,1,0:T(8,128)(2,1)S(1)} %all_to_all.21.table), channel_id=1, source_target_pairs={{0,8},{8,16},{16,24},{24,32},{32,40},{40,48},{48,56},{56,64},{64,7... | collective-permute-start | bytes 196616 | tf_op jit(solution)/shard_map/ppermute | solution.py:339
  72.7 10.6 %all-to-all-start.3 = ((f32[16,1,1152]{2,1,0:T(1,128)}), f32[16,1,1152]{2,1,0:T(1,128)S(1)}, u32[]{:S(2)}, u32[]{:S(2)}) async-start(f32[16,1,1152]{2,1,0:T(1,128)} %merge.1), calls=%async_computation.3 | async-start | bytes 147456 | tf_op jit(solution)/shard_map/all_to_all | solution.py:25

commit v11 on v10

--- a/solution.py
+++ b/solution.py
@@ -168,23 +168,25 @@
         factor = left[pl.ds(half * blocks, blocks)].reshape(blocks * 256, left.shape[2])
         acc = acc + jnp.dot(weights, factor, preferred_element_type=F32)
     samples[...] = acc
-    for n in range(out.shape[0]):
-        out[n] = acc.astype(BF16)
-
-
-def pack(table, words):
-    tiles = [
-        [table[p, 8 * h : 8 * h + 8].astype(F32) for h in range(2)] for p in range(table.shape[0])
-    ]
+    out[...] = acc.astype(BF16)
+
+
+def pack(mine, theirs, words):
+    chip, core = lax.axis_index("col_0"), lax.axis_index("col_1")
+    tiles, places = [], []
+    for part, side in ((mine, core), (theirs, 1 - core)):
+        for n, turn in enumerate((0, *TURNS)):
+            tiles.append([part[n, 8 * h : 8 * h + 8].astype(F32) for h in range(2)])
+            places.append(2 * lax.rem(chip + 4 - turn, 4) + side)
     top = jnp.abs(tiles[0][0])
     for pair in tiles:
         for tile in pair:
             top = jnp.maximum(top, jnp.abs(tile))
     top = jnp.maximum(jnp.max(top, axis=1, keepdims=True), 1e-30)
     scale = 32700.0 / top
-    for p, pair in enumerate(tiles):
+    for place, pair in zip(places, tiles):
         upper, lower = (jnp.round(tile * scale).astype(jnp.int32) for tile in pair)
-        words[p] = (upper << 16) | (lower & 0xFFFF)
+        words[place] = (upper << 16) | (lower & 0xFFFF)
     return jnp.broadcast_to(top * (1.0 / 32700.0), (8, 128))
 
 
@@ -203,8 +205,8 @@
     return (jnp.where(bit[4], word << 16, word) >> 16).astype(F32) * unit
 
 
-def own_kernel(table, first, partner, out, words):
-    unit = pack(table, words)
+def own_kernel(mine, theirs, first, partner, out, words):
+    unit = pack(mine, theirs, words)
 
     def step(n, carry):
         at = pl.multiple_of(n * 128, 128)
@@ -229,8 +231,8 @@
             out[n, :, 128 * i : 128 * i + 128] = rows[i]
 
 
-def bin_kernel(prev, partner, base, onehot, counts, out, words, pieces):
-    unit = pack(prev, words)
+def bin_kernel(mine, theirs, partner, base, onehot, counts, out, words, pieces):
+    unit = pack(mine, theirs, words)
 
     def step(n, carry):
         at = pl.multiple_of(n * 128, 128)
@@ -328,37 +330,44 @@
     on_diag = call(
         on_diag_kernel, vmem((16, span), F32), [VM] * 6, flops=1 << 28, name="ondiag"
     )(local, other_noise, *all_noise, diag_factor[:, 0])
-    copies, own_samples = call(
+    piece, own_samples = call(
         sample_kernel,
-        (vmem((cols, 16, span), BF16), vmem((16, span), F32)),
+        (vmem((16, span), BF16), vmem((16, span), F32)),
         [VM, VM, VM, VM],
         flops=1 << 26,
         name="samples",
     )(mine, theirs, left_factor[0].reshape(16, 256, span), on_diag)
-    own_tiles = exchange(copies, COL)
-    prev_tiles = lax.ppermute(own_tiles, ROW, [(source, source + 1) for source in range(rows - 1)])
+    pieces = [piece]
+    for turn in TURNS:
+        pieces.append(
+            lax.ppermute(piece, "col_0", [(chip, (chip + turn) % 4) for chip in range(4)])
+        )
+    own_mine = jnp.stack(pieces)
+    prev_mine = lax.ppermute(own_mine, ROW, [(source, source + 1) for source in range(rows - 1)])
+    own_theirs = lax.ppermute(own_mine, "col_1", swap)
+    prev_theirs = lax.ppermute(prev_mine, "col_1", swap)
     samples = call(
         emit_kernel, jax.ShapeDtypeStruct((8, 2, 1, span), F32), [VM], name="emit"
     )(own_samples)
     base = call(
         own_kernel,
         vmem((8, pairs), F32),
-        [VM, VM, VM],
+        [VM] * 4,
         flops=1 << 26,
         scratch_shapes=[pltpu.VMEM((cols, 8, span), jnp.int32)],
         name="own",
-    )(own_tiles, first, partner)
+    )(own_mine, own_theirs, first, partner)
     partial = call(
         bin_kernel,
         vmem((lax.axis_size(ZC), 1, 9 * NBIN), F32),
-        [VM, VM, VM, VM, VM],
+        [VM] * 6,
         flops=1 << 26,
         scratch_shapes=[
             pltpu.VMEM((cols, 8, span), jnp.int32),
             pltpu.VMEM((16, pairs), BF16),
         ],
         name="bins",
-    )(prev_tiles, partner, base, onehot, counts)
+    )(prev_mine, prev_theirs, partner, base, onehot, counts)
     merged = call(merge_kernel, vmem((lax.axis_size(XY), 1, 9 * NBIN), F32), [VM], name="merge")(
         exchange(partial, ZC)
     )

time: 84.2 us -> 86.6 us (1.029)
  blocking collectives: 45 us -> 32.7 us
  starting transfers between devices: 18.8 us -> 29.2 us
  waiting for transfers between devices: 9.93 us -> 14.2 us
    all_to_all x3 -> x2, blocking collectives: 45 us -> 32.7 us  [exchange(): return lax.all_to_all(copies, axis, 0, 0, tiled=True)]
    ppermute x1 -> x6, starting transfers between devices: 2.45 us -> 12.5 us  [the longest x3 6.36 us: body(): lax.ppermute(piece, 'col_0', [(chip, (chip + turn) % 4) for chip in range...]
    ppermute x1 -> x6, waiting for transfers between devices: 0.01 us -> 4.27 us  [the longest x3 4.27 us: body(): lax.ppermute(piece, 'col_0', [(chip, (chip + turn) % 4) for chip in range...]
  transfers between devices with their start and end apart: 8 -> 13, of which waited for: 4 -> 6; matrix products, arithmetic and copies ran while one was open for 0% -> 0% of each run, Pallas kernels for 6% -> 5%
where the time goes in v11:
time: 86.6 us; the launch traced here: 86.3 us
  blocking collectives  32.7 us (38%)
  starting transfers between devices  29.2 us (34%)
  waiting for transfers between devices  14.2 us (16%)
  Pallas kernels  9.2 us (11%)
    all_to_all x2, blocking collectives, exchange(): return lax.all_to_all(copies, axis, 0, 0, tiled=True)  32.7 us
    pallas_call x12, Pallas kernels, held(): run(*(a if spec is SM else pltpu.with_memory_space_constraint(a, spec.mem...  9.2 us
    ppermute x3, starting transfers between devices, body(): lax.ppermute(payload, 'col_0', [(chip, (chip + turn) % 4) for chip in ran...  8.46 us
    ppermute x3, starting transfers between devices, body(): lax.ppermute(piece, 'col_0', [(chip, (chip + turn) % 4) for chip in range...  6.36 us
    all_to_all x1, waiting for transfers between devices, exchange(): return lax.all_to_all(copies, axis, 0, 0, tiled=True)  5.92 us
    all_to_all x1, starting transfers between devices, exchange(): return lax.all_to_all(copies, axis, 0, 0, tiled=True)  4.47 us
    ppermute x3, waiting for transfers between devices, body(): lax.ppermute(piece, 'col_0', [(chip, (chip + turn) % 4) for chip in range...  4.27 us
    ppermute x3, waiting for transfers between devices, body(): lax.ppermute(payload, 'col_0', [(chip, (chip + turn) % 4) for chip in ran...  3.94 us
  transfers between devices with their start and end apart: 13, of which 6 were waited for; matrix products, arithmetic and copies ran while one was open for 0% of the time, Pallas kernels for 5%

profile of v11, /device:TPU:1, one launch (start us, length us, event | category | flops | bytes accessed | tf_op | source)
XLA Modules:
  0.0 86.3 jit_solution(1138648457602875316)
XLA Ops:
  0.6 0.0 copy-start
  0.6 0.9 %copies.1 = (bf16[16,256]{1,0:T(8,128)(2,1)S(1)}, bf16[32,16,256]{2,1,0:T(8,128)(2,1)S(1)}) custom-call(bf16[8,2,256]{2,1,0:T(2,128)(2,1)} %bitcast.35), custom_call_target="tpu_custom_call" | custom-call | flops 1073741824 | bytes 1048576 | tf_op jit(solution)/shard_map/copies/pallas_call | solution.py:48
  1.5 0.0 copy-start.3
  1.5 0.0 copy-start.5
  1.6 17.0 %all_to_all.15.columns = bf16[32,16,256]{2,1,0:T(8,128)(2,1)S(1)} all-to-all(bf16[32,16,256]{2,1,0:T(8,128)(2,1)S(1)} %get-tuple-element.10), channel_id=1, replica_groups=mesh['row_0'=4,'row_1'=2,'row_2'=4,'col_0'=4,'col_1'=2] {'row_0','row_1'..., dimensions={0} | all-to-all | bytes 524288 | tf_op jit(solution)/shard_map/all_to_all | solution.py:25
  18.6 0.0 copy-done
  18.6 0.6 send.1
  19.1 0.0 copy-start.1
  19.2 2.2 %collective-permute-start = (f32[8,8,256]{2,1,0:T(8,128)S(1)}, f32[8,8,256]{2,1,0:T(8,128)S(1)}, u32[]{:S(2)}, u32[]{:S(2)}) collective-permute-start(f32[8,8,256]{2,1,0:T(8,128)S(1)} %send.1), channel_id=1, source_target_pairs={{0,1},{1,0},{2,3},{3,2},{4,5},{5,4},{6,7},{7,6},{8,9},{9,8},{10,11... | collective-permute-start | bytes 196616 | tf_op jit(solution)/shard_map/ppermute | solution.py:313
  21.3 0.1 collective-permute-start.1
  21.4 0.0 copy-done.3
  21.4 0.0 copy-done.5
  21.4 1.3 %prepare.1 = (bf16[128,4096]{1,0:T(8,128)(2,1)S(1)}, f32[8,1,256]{2,1,0:T(1,128)S(1)}, f32[8,128]{1,0:T(8,128)S(1)}) custom-call(s32[1,4096]{1,0:T(1,128)S(1)} %bitcast.26, s32[1,64]{1,0:T(1,128)S(1)} %copy-done.5), custom_call_target="tpu_custom_call" | custom-call | flops 1048576 | bytes 1048576 | tf_op jit(solution)/shard_map/prepare/pallas_call | solution.py:48
  22.7 0.0 copy-start.2
  22.7 0.6 keep.1
  23.3 0.0 collective-permute-done.1.other
  23.3 0.0 collective-permute-done.received
  23.4 5.2 %collective-permute-start.4 = (f16[96,256]{1,0:T(8,128)(2,1)S(1)}, f16[96,256]{1,0:T(8,128)(2,1)S(1)}, u32[]{:S(2)}, u32[]{:S(2)}) collective-permute-start(f16[96,256]{1,0:T(8,128)(2,1)S(1)} %convert_element_type.33), channel_id=1, source_target_pairs={{0,6},{2,0},{4,2},{6,4},{1,7},{3,1},{5,3},{7,5},{8,14},{10,8},{12,... | collective-permute-start | bytes 147464 | tf_op jit(solution)/shard_map/ppermute | solution.py:321
  28.6 0.0 collective-permute-start.3
  28.6 3.3 %collective-permute-start.2 = (f16[96,256]{1,0:T(8,128)(2,1)S(1)}, f16[96,256]{1,0:T(8,128)(2,1)S(1)}, u32[]{:S(2)}, u32[]{:S(2)}) collective-permute-start(f16[96,256]{1,0:T(8,128)(2,1)S(1)} %convert_element_type.33), channel_id=1, source_target_pairs={{0,4},{2,6},{4,0},{6,2},{1,5},{3,7},{5,1},{7,3},{8,12},{10,14},{12... | collective-permute-start | bytes 147464 | tf_op jit(solution)/shard_map/ppermute | solution.py:321
  31.8 0.0 collective-permute-done.4
  31.8 2.4 %collective-permute-done.3 = f16[96,256]{1,0:T(8,128)(2,1)S(1)} collective-permute-done((f16[96,256]{1,0:T(8,128)(2,1)S(1)}, f16[96,256]{1,0:T(8,128)(2,1)S(1)}, u32[]{:S(2)}, u32[]{:S(2)}) %collective-permute-start.3) | collective-permute-done | bytes 49184 | tf_op jit(solution)/shard_map/ppermute | solution.py:321
  34.2 1.6 %collective-permute-done.2 = f16[96,256]{1,0:T(8,128)(2,1)S(1)} collective-permute-done((f16[96,256]{1,0:T(8,128)(2,1)S(1)}, f16[96,256]{1,0:T(8,128)(2,1)S(1)}, u32[]{:S(2)}, u32[]{:S(2)}) %collective-permute-start.2) | collective-permute-done | bytes 49184 | tf_op jit(solution)/shard_map/ppermute | solution.py:321
  35.8 1.6 %collective-permute-start.5 = (bf16[8,8,256]{2,1,0:T(8,128)(2,1)S(1)}, bf16[8,8,256]{2,1,0:T(8,128)(2,1)S(1)}, u32[]{:S(2)}, u32[]{:S(2)}) collective-permute-start(bf16[8,8,256]{2,1,0:T(8,128)(2,1)S(1)} %fusion.2.mine), channel_id=1, source_target_pairs={{0,1},{1,0},{2,3},{3,2},{4,5},{5,4},{6,7},{7,6},{8,9},{9,8},{10,11... | collective-permute-start | bytes 98312 | tf_op jit(solution)/shard_map/ppermute | solution.py:329
  37.4 0.0 copy-done.1
  37.4 0.0 copy-start.4
  37.4 0.0 copy-start.6
  37.4 0.7 ondiag.1.on_diag
  38.2 0.1 collective-permute-done.5.theirs
  38.2 0.0 copy-done.2
  38.2 0.4 samples.1
  38.6 4.2 %collective-permute-start.8 = (bf16[16,256]{1,0:T(8,128)(2,1)S(1)}, bf16[16,256]{1,0:T(8,128)(2,1)S(1)}, u32[]{:S(2)}, u32[]{:S(2)}) collective-permute-start(bf16[16,256]{1,0:T(8,128)(2,1)S(1)} %get-tuple-element.13), channel_id=1, source_target_pairs={{0,6},{2,0},{4,2},{6,4},{1,7},{3,1},{5,3},{7,5},{8,14},{10,8},{12,... | collective-permute-start | bytes 24584 | tf_op jit(solution)/shard_map/ppermute | solution.py:343
  42.8 0.0 collective-permute-start.7
  42.9 2.1 %collective-permute-start.6 = (bf16[16,256]{1,0:T(8,128)(2,1)S(1)}, bf16[16,256]{1,0:T(8,128)(2,1)S(1)}, u32[]{:S(2)}, u32[]{:S(2)}) collective-permute-start(bf16[16,256]{1,0:T(8,128)(2,1)S(1)} %get-tuple-element.13), channel_id=1, source_target_pairs={{0,4},{2,6},{4,0},{6,2},{1,5},{3,7},{5,1},{7,3},{8,12},{10,14},{12... | collective-permute-start | bytes 24584 | tf_op jit(solution)/shard_map/ppermute | solution.py:343
  45.0 0.0 collective-permute-done.8
  45.0 2.5 %collective-permute-done.7 = bf16[16,256]{1,0:T(8,128)(2,1)S(1)} collective-permute-done((bf16[16,256]{1,0:T(8,128)(2,1)S(1)}, bf16[16,256]{1,0:T(8,128)(2,1)S(1)}, u32[]{:S(2)}, u32[]{:S(2)}) %collective-permute-start.7) | collective-permute-done | bytes 8224 | tf_op jit(solution)/shard_map/ppermute | solution.py:343
  47.5 1.8 %collective-permute-done.6 = bf16[16,256]{1,0:T(8,128)(2,1)S(1)} collective-permute-done((bf16[16,256]{1,0:T(8,128)(2,1)S(1)}, bf16[16,256]{1,0:T(8,128)(2,1)S(1)}, u32[]{:S(2)}, u32[]{:S(2)}) %collective-permute-start.6) | collective-permute-done | bytes 8224 | tf_op jit(solution)/shard_map/ppermute | solution.py:343
  49.3 2.5 %collective-permute-start.9 = (bf16[4,16,256]{2,1,0:T(8,128)(2,1)S(1)}, bf16[4,16,256]{2,1,0:T(8,128)(2,1)S(1)}, u32[]{:S(2)}, u32[]{:S(2)}) collective-permute-start(bf16[4,16,256]{2,1,0:T(8,128)(2,1)S(1)} %pad_maximum_fusion.mine), channel_id=1, source_target_pairs={{0,8},{8,16},{16,24},{24,32},{32,40},{40,48},{48,56},{56,64},{64,7... | collective-permute-start | bytes 98312 | tf_op jit(solution)/shard_map/ppermute | solution.py:346
  51.7 2.2 %collective-permute-start.11 = (bf16[4,16,256]{2,1,0:T(8,128)(2,1)S(1)}, bf16[4,16,256]{2,1,0:T(8,128)(2,1)S(1)}, u32[]{:S(2)}, u32[]{:S(2)}) collective-permute-start(bf16[4,16,256]{2,1,0:T(8,128)(2,1)S(1)} %pad_maximum_fusion.mine), channel_id=1, source_target_pairs={{0,1},{1,0},{2,3},{3,2},{4,5},{5,4},{6,7},{7,6},{8,9},{9,8},{10,11... | collective-permute-start | bytes 98312 | tf_op jit(solution)/shard_map/ppermute | solution.py:347
  53.9 0.0 collective-permute-done.9.mine
  53.9 1.5 %collective-permute-start.10 = (bf16[4,16,256]{2,1,0:T(8,128)(2,1)S(1)}, bf16[4,16,256]{2,1,0:T(8,128)(2,1)S(1)}, u32[]{:S(2)}, u32[]{:S(2)}) collective-permute-start(bf16[4,16,256]{2,1,0:T(8,128)(2,1)S(1)} %collective-permute-done.9.mine), channel_id=1, source_target_pairs={{0,1},{1,0},{2,3},{3,2},{4,5},{5,4},{6,7},{7,6},{8,9},{9,8},{10,11... | collective-permute-start | bytes 98312 | tf_op jit(solution)/shard_map/ppermute | solution.py:348
  55.4 0.0 collective-permute-done.11.theirs
  55.4 0.0 copy-done.4
  55.4 0.0 copy-done.6
  55.4 1.5 %own.1.base = f32[8,4096]{1,0:T(8,128)S(1)} custom-call(bf16[4,16,256]{2,1,0:T(8,128)(2,1)S(1)} %pad_maximum_fusion.mine, bf16[4,16,256]{2,1,0:T(8,128)(2,1)S(1)} %collective-permute-done.11.theirs, s32[1,4096]{1,0:T(1,128)S(1)} %bitcast.30, s32[1,4096]{1,0:T(1,128)S(1)} %bitcast.27), custom_call_target="tpu_custom_call" | custom-call | flops 67108864 | bytes 1048576 | tf_op jit(solution)/shard_map/own/pallas_call | solution.py:48
  57.0 0.0 collective-permute-done.10.theirs
  57.0 1.3 %bins.1 = f32[16,1,1152]{2,1,0:T(1,128)S(1)} custom-call(bf16[4,16,256]{2,1,0:T(8,128)(2,1)S(1)} %collective-permute-done.9.mine, bf16[4,16,256]{2,1,0:T(8,128)(2,1)S(1)} %collective-permute-done.10.theirs, s32[1,4096]{1,0:T(1,128)S(1)} %bitcast.28, f32[8,4096]{1,0:T(8,128)S(1)} %own.1.base, bf16[128,4096]{1,0:T(8,128)(2,1)S(1)} %get-tuple-element.14.onehot, ...), custom_call_target="tpu_custom_call" | custom-call | flops 67108864 | bytes 1048576 | tf_op jit(solution)/shard_map/bins/pallas_call | solution.py:48
  58.3 15.7 %all_to_all.16.parts = f32[16,1,1152]{2,1,0:T(1,128)S(1)} all-to-all(f32[16,1,1152]{2,1,0:T(1,128)S(1)} %bins.1), channel_id=1, replica_groups=mesh['row_0'=4,'row_1'=2,'row_2'=4,'col_0'=4,'col_1'=2] {'row_1','col_0'..., dimensions={0} | all-to-all | bytes 147456 | tf_op jit(solution)/shard_map/all_to_all | solution.py:25
  74.0 0.7 merge.1
  74.7 4.5 %all-to-all-start.2 = ((f32[16,1,1152]{2,1,0:T(1,128)}), f32[16,1,1152]{2,1,0:T(1,128)S(1)}, u32[]{:S(2)}, u32[]{:S(2)}) async-start(f32[16,1,1152]{2,1,0:T(1,128)} %merge.1), calls=%async_computation.2 | async-start | bytes 147456 | tf_op jit(solution)/shard_map/all_to_all | solution.py:25
  79.2 0.6 emit.1
  79.8 5.9 %all-to-all-done.2.parts = f32[16,1,1152]{2,1,0:T(1,128)S(1)} async-done(((f32[16,1,1152]{2,1,0:T(1,128)}), f32[16,1,1152]{2,1,0:T(1,128)S(1)}, u32[]{:S(2)}, u32[]{:S(2)}) %all-to-all-start.2) | async-done | bytes 73760 | tf_op jit(solution)/shard_map/all_to_all | solution.py:25
  85.7 0.6 finish.1
  (9 shorter events, 0.1 us)
Async XLA Ops:
  0.6 17.9 %copy-start = (bf16[1,64,64,256]{3,2,1,0:T(8,128)(2,1)S(1)}, bf16[1,64,64,256]{3,2,1,0:T(8,128)(2,1)}, u32[]{:S(2)}) copy-start(bf16[1,64,64,256]{3,2,1,0:T(8,128)(2,1)} %param.11) | copy-start | bytes 6291460
  1.5 19.9 %copy-start.3 = (s32[1,1,4096]{2,1,0:T(1,128)S(1)}, s32[1,1,4096]{2,1,0:T(1,128)}, u32[]{:S(2)}) copy-start(s32[1,1,4096]{2,1,0:T(1,128)} %param.15) | copy-start | bytes 49156
  1.5 19.9 %copy-start.5 = (s32[1,64]{1,0:T(1,128)S(1)}, s32[1,64]{1,0:T(1,128)}, u32[]{:S(2)}) copy-start(s32[1,64]{1,0:T(1,128)} %ranks.1) | copy-start | bytes 772
  19.1 18.3 %copy-start.1 = (bf16[2,1,256,2048]{3,2,1,0:T(8,128)(2,1)S(1)}, bf16[2,1,256,2048]{3,2,1,0:T(8,128)(2,1)}, u32[]{:S(2)}) copy-start(bf16[2,1,256,2048]{3,2,1,0:T(8,128)(2,1)} %param.9) | copy-start | bytes 6291460
  19.2 4.2 %collective-permute-start = (f32[8,8,256]{2,1,0:T(8,128)S(1)}, f32[8,8,256]{2,1,0:T(8,128)S(1)}, u32[]{:S(2)}, u32[]{:S(2)}) collective-permute-start(f32[8,8,256]{2,1,0:T(8,128)S(1)} %send.1), channel_id=1, source_target_pairs={{0,1},{1,0},{2,3},{3,2},{4,5},{5,4},{6,7},{7,6},{8,9},{9,8},{10,11... | collective-permute-start | bytes 196616 | tf_op jit(solution)/shard_map/ppermute | solution.py:313
  21.3 2.0 %collective-permute-start.1 = (bf16[16,256]{1,0:T(8,128)(2,1)S(1)}, bf16[16,256]{1,0:T(8,128)(2,1)S(1)}, u32[]{:S(2)}, u32[]{:S(2)}) collective-permute-start(bf16[16,256]{1,0:T(8,128)(2,1)S(1)} %get-tuple-element.11.local), channel_id=1, source_target_pairs={{0,1},{1,0},{2,3},{3,2},{4,5},{5,4},{6,7},{7,6},{8,9},{9,8},{10,11... | collective-permute-start | bytes 24584 | tf_op jit(solution)/shard_map/ppermute | solution.py:301
  22.7 15.5 %copy-start.2 = (bf16[1,64,64,256]{3,2,1,0:T(8,128)(2,1)S(1)}, bf16[1,64,64,256]{3,2,1,0:T(8,128)(2,1)}, u32[]{:S(2)}) copy-start(bf16[1,64,64,256]{3,2,1,0:T(8,128)(2,1)} %param.10) | copy-start | bytes 6291460
  23.4 8.5 %collective-permute-start.4 = (f16[96,256]{1,0:T(8,128)(2,1)S(1)}, f16[96,256]{1,0:T(8,128)(2,1)S(1)}, u32[]{:S(2)}, u32[]{:S(2)}) collective-permute-start(f16[96,256]{1,0:T(8,128)(2,1)S(1)} %convert_element_type.33), channel_id=1, source_target_pairs={{0,6},{2,0},{4,2},{6,4},{1,7},{3,1},{5,3},{7,5},{8,14},{10,8},{12,... | collective-permute-start | bytes 147464 | tf_op jit(solution)/shard_map/ppermute | solution.py:321
  28.6 5.7 %collective-permute-start.3 = (f16[96,256]{1,0:T(8,128)(2,1)S(1)}, f16[96,256]{1,0:T(8,128)(2,1)S(1)}, u32[]{:S(2)}, u32[]{:S(2)}) collective-permute-start(f16[96,256]{1,0:T(8,128)(2,1)S(1)} %convert_element_type.33), channel_id=1, source_target_pairs={{0,2},{2,4},{4,6},{6,0},{1,3},{3,5},{5,7},{7,1},{8,10},{10,12},{12... | collective-permute-start | bytes 147464 | tf_op jit(solution)/shard_map/ppermute | solution.py:321
  28.6 7.2 %collective-permute-start.2 = (f16[96,256]{1,0:T(8,128)(2,1)S(1)}, f16[96,256]{1,0:T(8,128)(2,1)S(1)}, u32[]{:S(2)}, u32[]{:S(2)}) collective-permute-start(f16[96,256]{1,0:T(8,128)(2,1)S(1)} %convert_element_type.33), channel_id=1, source_target_pairs={{0,4},{2,6},{4,0},{6,2},{1,5},{3,7},{5,1},{7,3},{8,12},{10,14},{12... | collective-permute-start | bytes 147464 | tf_op jit(solution)/shard_map/ppermute | solution.py:321
  35.8 2.4 %collective-permute-start.5 = (bf16[8,8,256]{2,1,0:T(8,128)(2,1)S(1)}, bf16[8,8,256]{2,1,0:T(8,128)(2,1)S(1)}, u32[]{:S(2)}, u32[]{:S(2)}) collective-permute-start(bf16[8,8,256]{2,1,0:T(8,128)(2,1)S(1)} %fusion.2.mine), channel_id=1, source_target_pairs={{0,1},{1,0},{2,3},{3,2},{4,5},{5,4},{6,7},{7,6},{8,9},{9,8},{10,11... | collective-permute-start | bytes 98312 | tf_op jit(solution)/shard_map/ppermute | solution.py:329
  37.4 18.0 %copy-start.4 = (s32[1,1,4096]{2,1,0:T(1,128)S(1)}, s32[1,1,4096]{2,1,0:T(1,128)}, u32[]{:S(2)}) copy-start(s32[1,1,4096]{2,1,0:T(1,128)} %param.14) | copy-start | bytes 49156
  37.4 18.0 %copy-start.6 = (s32[1,1,4096]{2,1,0:T(1,128)S(1)}, s32[1,1,4096]{2,1,0:T(1,128)}, u32[]{:S(2)}) copy-start(s32[1,1,4096]{2,1,0:T(1,128)} %param.13) | copy-start | bytes 49156
  38.6 6.4 %collective-permute-start.8 = (bf16[16,256]{1,0:T(8,128)(2,1)S(1)}, bf16[16,256]{1,0:T(8,128)(2,1)S(1)}, u32[]{:S(2)}, u32[]{:S(2)}) collective-permute-start(bf16[16,256]{1,0:T(8,128)(2,1)S(1)} %get-tuple-element.13), channel_id=1, source_target_pairs={{0,6},{2,0},{4,2},{6,4},{1,7},{3,1},{5,3},{7,5},{8,14},{10,8},{12,... | collective-permute-start | bytes 24584 | tf_op jit(solution)/shard_map/ppermute | solution.py:343
  42.8 4.6 %collective-permute-start.7 = (bf16[16,256]{1,0:T(8,128)(2,1)S(1)}, bf16[16,256]{1,0:T(8,128)(2,1)S(1)}, u32[]{:S(2)}, u32[]{:S(2)}) collective-permute-start(bf16[16,256]{1,0:T(8,128)(2,1)S(1)} %get-tuple-element.13), channel_id=1, source_target_pairs={{0,2},{2,4},{4,6},{6,0},{1,3},{3,5},{5,7},{7,1},{8,10},{10,12},{12... | collective-permute-start | bytes 24584 | tf_op jit(solution)/shard_map/ppermute | solution.py:343
  42.9 6.4 %collective-permute-start.6 = (bf16[16,256]{1,0:T(8,128)(2,1)S(1)}, bf16[16,256]{1,0:T(8,128)(2,1)S(1)}, u32[]{:S(2)}, u32[]{:S(2)}) collective-permute-start(bf16[16,256]{1,0:T(8,128)(2,1)S(1)} %get-tuple-element.13), channel_id=1, source_target_pairs={{0,4},{2,6},{4,0},{6,2},{1,5},{3,7},{5,1},{7,3},{8,12},{10,14},{12... | collective-permute-start | bytes 24584 | tf_op jit(solution)/shard_map/ppermute | solution.py:343
  49.3 4.6 %collective-permute-start.9 = (bf16[4,16,256]{2,1,0:T(8,128)(2,1)S(1)}, bf16[4,16,256]{2,1,0:T(8,128)(2,1)S(1)}, u32[]{:S(2)}, u32[]{:S(2)}) collective-permute-start(bf16[4,16,256]{2,1,0:T(8,128)(2,1)S(1)} %pad_maximum_fusion.mine), channel_id=1, source_target_pairs={{0,8},{8,16},{16,24},{24,32},{32,40},{40,48},{48,56},{56,64},{64,7... | collective-permute-start | bytes 98312 | tf_op jit(solution)/shard_map/ppermute | solution.py:346
  51.7 3.7 %collective-permute-start.11 = (bf16[4,16,256]{2,1,0:T(8,128)(2,1)S(1)}, bf16[4,16,256]{2,1,0:T(8,128)(2,1)S(1)}, u32[]{:S(2)}, u32[]{:S(2)}) collective-permute-start(bf16[4,16,256]{2,1,0:T(8,128)(2,1)S(1)} %pad_maximum_fusion.mine), channel_id=1, source_target_pairs={{0,1},{1,0},{2,3},{3,2},{4,5},{5,4},{6,7},{7,6},{8,9},{9,8},{10,11... | collective-permute-start | bytes 98312 | tf_op jit(solution)/shard_map/ppermute | solution.py:347
  53.9 3.0 %collective-permute-start.10 = (bf16[4,16,256]{2,1,0:T(8,128)(2,1)S(1)}, bf16[4,16,256]{2,1,0:T(8,128)(2,1)S(1)}, u32[]{:S(2)}, u32[]{:S(2)}) collective-permute-start(bf16[4,16,256]{2,1,0:T(8,128)(2,1)S(1)} %collective-permute-done.9.mine), channel_id=1, source_target_pairs={{0,1},{1,0},{2,3},{3,2},{4,5},{5,4},{6,7},{7,6},{8,9},{9,8},{10,11... | collective-permute-start | bytes 98312 | tf_op jit(solution)/shard_map/ppermute | solution.py:348
  74.7 11.0 %all-to-all-start.2 = ((f32[16,1,1152]{2,1,0:T(1,128)}), f32[16,1,1152]{2,1,0:T(1,128)S(1)}, u32[]{:S(2)}, u32[]{:S(2)}) async-start(f32[16,1,1152]{2,1,0:T(1,128)} %merge.1), calls=%async_computation.2 | async-start | bytes 147456 | tf_op jit(solution)/shard_map/all_to_all | solution.py:25

commit v12 on v11

--- a/solution.py
+++ b/solution.py
@@ -66,7 +66,7 @@
         out[n] = mine
 
 
-def prepare_kernel(bins, ranks, onehot, keep, counts):
+def mask_kernel(ranks, keep):
     core = lax.axis_index("col_1")
     lane = lax.broadcasted_iota(jnp.int32, (1, 256), 1)
     for i in range(keep.shape[0]):
@@ -75,6 +75,9 @@
         for n in (2, 1, 0):
             limit = jnp.where(lane < 64 * n + 64, ranks[0, slot + n] + 64 * n, limit)
         keep[i] = jnp.where(lane < limit, 1.0, 0.0)
+
+
+def prepare_kernel(bins, onehot, counts):
     bin_at = lax.broadcasted_iota(jnp.int32, (NBIN, 128), 0)
 
     def step(n, carry):
@@ -291,13 +294,14 @@
         name="copies",
     )(jnp.transpose(noise, (0, 2, 1, 3))[:, 0])
     columns = exchange(spread_noise, ROW)
-    onehot, allowed, counts = call(
+    allowed = call(mask_kernel, vmem((8, 1, 256), F32), [SM], name="mask")(tile_ranks)
+    onehot, counts = call(
         prepare_kernel,
-        (vmem((NBIN, pairs), BF16), vmem((8, 1, 256), F32), vmem((8, NBIN), F32)),
-        [VM, SM],
+        (vmem((NBIN, pairs), BF16), vmem((8, NBIN), F32)),
+        [VM],
         flops=1 << 20,
         name="prepare",
-    )(bins, tile_ranks)
+    )(bins)
     other_noise = lax.ppermute(local, "col_1", swap)
 
     def project(away, name):

time: 86.6 us -> 86.7 us (level)
    pallas_call x12 -> x13, Pallas kernels: 9.2 us -> 9.21 us  [held(): run(*(a if spec is SM else pltpu.with_memory_space_constraint(a, spec.mem...]
where the time goes in v12:
time: 86.7 us; the launch traced here: 86.3 us
  blocking collectives  32.7 us (38%)
  starting transfers between devices  29.2 us (34%)
  waiting for transfers between devices  14.2 us (16%)
  Pallas kernels  9.21 us (11%)
    all_to_all x2, blocking collectives, exchange(): return lax.all_to_all(copies, axis, 0, 0, tiled=True)  32.7 us
    pallas_call x13, Pallas kernels, held(): run(*(a if spec is SM else pltpu.with_memory_space_constraint(a, spec.mem...  9.21 us
    ppermute x3, starting transfers between devices, body(): lax.ppermute(payload, 'col_0', [(chip, (chip + turn) % 4) for chip in ran...  8.45 us
    ppermute x3, starting transfers between devices, body(): lax.ppermute(piece, 'col_0', [(chip, (chip + turn) % 4) for chip in range...  6.36 us
    all_to_all x1, waiting for transfers between devices, exchange(): return lax.all_to_all(copies, axis, 0, 0, tiled=True)  5.92 us
    all_to_all x1, starting transfers between devices, exchange(): return lax.all_to_all(copies, axis, 0, 0, tiled=True)  4.48 us
    ppermute x3, waiting for transfers between devices, body(): lax.ppermute(piece, 'col_0', [(chip, (chip + turn) % 4) for chip in range...  4.27 us
    ppermute x3, waiting for transfers between devices, body(): lax.ppermute(payload, 'col_0', [(chip, (chip + turn) % 4) for chip in ran...  3.95 us
  transfers between devices with their start and end apart: 13, of which 6 were waited for; matrix products, arithmetic and copies ran while one was open for 0% of the time, Pallas kernels for 5%

profile of v12, /device:TPU:1, one launch (start us, length us, event | category | flops | bytes accessed | tf_op | source)
XLA Modules:
  0.0 86.3 jit_solution(10702220177601773987)
XLA Ops:
  0.6 0.0 copy-start
  0.6 0.9 %copies.1 = (bf16[16,256]{1,0:T(8,128)(2,1)S(1)}, bf16[32,16,256]{2,1,0:T(8,128)(2,1)S(1)}) custom-call(bf16[8,2,256]{2,1,0:T(2,128)(2,1)} %bitcast.35), custom_call_target="tpu_custom_call" | custom-call | flops 1073741824 | bytes 1048576 | tf_op jit(solution)/shard_map/copies/pallas_call | solution.py:48
  1.5 0.0 copy-start.5
  1.5 17.0 %all_to_all.15.columns = bf16[32,16,256]{2,1,0:T(8,128)(2,1)S(1)} all-to-all(bf16[32,16,256]{2,1,0:T(8,128)(2,1)S(1)} %get-tuple-element.8), channel_id=1, replica_groups=mesh['row_0'=4,'row_1'=2,'row_2'=4,'col_0'=4,'col_1'=2] {'row_0','row_1'..., dimensions={0} | all-to-all | bytes 524288 | tf_op jit(solution)/shard_map/all_to_all | solution.py:25
  18.6 0.0 copy-done
  18.6 0.6 send.1
  19.1 0.0 copy-start.1
  19.1 2.2 %collective-permute-start = (f32[8,8,256]{2,1,0:T(8,128)S(1)}, f32[8,8,256]{2,1,0:T(8,128)S(1)}, u32[]{:S(2)}, u32[]{:S(2)}) collective-permute-start(f32[8,8,256]{2,1,0:T(8,128)S(1)} %send.1), channel_id=1, source_target_pairs={{0,1},{1,0},{2,3},{3,2},{4,5},{5,4},{6,7},{7,6},{8,9},{9,8},{10,11... | collective-permute-start | bytes 196616 | tf_op jit(solution)/shard_map/ppermute | solution.py:317
  21.3 0.1 collective-permute-start.1
  21.4 0.0 copy-done.5
  21.4 0.6 mask.1
  22.0 0.0 copy-start.2
  22.0 0.6 keep.1
  22.6 0.0 collective-permute-done.1.other
  22.6 0.0 collective-permute-done.received
  22.7 5.2 %collective-permute-start.4 = (f16[96,256]{1,0:T(8,128)(2,1)S(1)}, f16[96,256]{1,0:T(8,128)(2,1)S(1)}, u32[]{:S(2)}, u32[]{:S(2)}) collective-permute-start(f16[96,256]{1,0:T(8,128)(2,1)S(1)} %convert_element_type.33), channel_id=1, source_target_pairs={{0,6},{2,0},{4,2},{6,4},{1,7},{3,1},{5,3},{7,5},{8,14},{10,8},{12,... | collective-permute-start | bytes 147464 | tf_op jit(solution)/shard_map/ppermute | solution.py:325
  27.9 0.0 collective-permute-start.3
  27.9 3.2 %collective-permute-start.2 = (f16[96,256]{1,0:T(8,128)(2,1)S(1)}, f16[96,256]{1,0:T(8,128)(2,1)S(1)}, u32[]{:S(2)}, u32[]{:S(2)}) collective-permute-start(f16[96,256]{1,0:T(8,128)(2,1)S(1)} %convert_element_type.33), channel_id=1, source_target_pairs={{0,4},{2,6},{4,0},{6,2},{1,5},{3,7},{5,1},{7,3},{8,12},{10,14},{12... | collective-permute-start | bytes 147464 | tf_op jit(solution)/shard_map/ppermute | solution.py:325
  31.1 0.0 collective-permute-done.4
  31.2 2.4 %collective-permute-done.3 = f16[96,256]{1,0:T(8,128)(2,1)S(1)} collective-permute-done((f16[96,256]{1,0:T(8,128)(2,1)S(1)}, f16[96,256]{1,0:T(8,128)(2,1)S(1)}, u32[]{:S(2)}, u32[]{:S(2)}) %collective-permute-start.3) | collective-permute-done | bytes 49184 | tf_op jit(solution)/shard_map/ppermute | solution.py:325
  33.5 1.6 %collective-permute-done.2 = f16[96,256]{1,0:T(8,128)(2,1)S(1)} collective-permute-done((f16[96,256]{1,0:T(8,128)(2,1)S(1)}, f16[96,256]{1,0:T(8,128)(2,1)S(1)}, u32[]{:S(2)}, u32[]{:S(2)}) %collective-permute-start.2) | collective-permute-done | bytes 49184 | tf_op jit(solution)/shard_map/ppermute | solution.py:325
  35.1 1.6 %collective-permute-start.5 = (bf16[8,8,256]{2,1,0:T(8,128)(2,1)S(1)}, bf16[8,8,256]{2,1,0:T(8,128)(2,1)S(1)}, u32[]{:S(2)}, u32[]{:S(2)}) collective-permute-start(bf16[8,8,256]{2,1,0:T(8,128)(2,1)S(1)} %fusion.2.mine), channel_id=1, source_target_pairs={{0,1},{1,0},{2,3},{3,2},{4,5},{5,4},{6,7},{7,6},{8,9},{9,8},{10,11... | collective-permute-start | bytes 98312 | tf_op jit(solution)/shard_map/ppermute | solution.py:333
  36.7 0.0 copy-done.1
  36.7 0.0 copy-start.3
  36.7 0.0 copy-start.4
  36.8 0.0 copy-start.6
  36.8 0.7 ondiag.1.on_diag
  37.5 0.1 collective-permute-done.5.theirs
  37.6 0.0 copy-done.2
  37.6 0.4 samples.1
  37.9 4.2 %collective-permute-start.8 = (bf16[16,256]{1,0:T(8,128)(2,1)S(1)}, bf16[16,256]{1,0:T(8,128)(2,1)S(1)}, u32[]{:S(2)}, u32[]{:S(2)}) collective-permute-start(bf16[16,256]{1,0:T(8,128)(2,1)S(1)} %get-tuple-element.11), channel_id=1, source_target_pairs={{0,6},{2,0},{4,2},{6,4},{1,7},{3,1},{5,3},{7,5},{8,14},{10,8},{12,... | collective-permute-start | bytes 24584 | tf_op jit(solution)/shard_map/ppermute | solution.py:347
  42.2 0.0 collective-permute-start.7
  42.2 2.1 %collective-permute-start.6 = (bf16[16,256]{1,0:T(8,128)(2,1)S(1)}, bf16[16,256]{1,0:T(8,128)(2,1)S(1)}, u32[]{:S(2)}, u32[]{:S(2)}) collective-permute-start(bf16[16,256]{1,0:T(8,128)(2,1)S(1)} %get-tuple-element.11), channel_id=1, source_target_pairs={{0,4},{2,6},{4,0},{6,2},{1,5},{3,7},{5,1},{7,3},{8,12},{10,14},{12... | collective-permute-start | bytes 24584 | tf_op jit(solution)/shard_map/ppermute | solution.py:347
  44.3 0.0 collective-permute-done.8
  44.3 2.5 %collective-permute-done.7 = bf16[16,256]{1,0:T(8,128)(2,1)S(1)} collective-permute-done((bf16[16,256]{1,0:T(8,128)(2,1)S(1)}, bf16[16,256]{1,0:T(8,128)(2,1)S(1)}, u32[]{:S(2)}, u32[]{:S(2)}) %collective-permute-start.7) | collective-permute-done | bytes 8224 | tf_op jit(solution)/shard_map/ppermute | solution.py:347
  46.8 1.8 %collective-permute-done.6 = bf16[16,256]{1,0:T(8,128)(2,1)S(1)} collective-permute-done((bf16[16,256]{1,0:T(8,128)(2,1)S(1)}, bf16[16,256]{1,0:T(8,128)(2,1)S(1)}, u32[]{:S(2)}, u32[]{:S(2)}) %collective-permute-start.6) | collective-permute-done | bytes 8224 | tf_op jit(solution)/shard_map/ppermute | solution.py:347
  48.6 2.5 %collective-permute-start.9 = (bf16[4,16,256]{2,1,0:T(8,128)(2,1)S(1)}, bf16[4,16,256]{2,1,0:T(8,128)(2,1)S(1)}, u32[]{:S(2)}, u32[]{:S(2)}) collective-permute-start(bf16[4,16,256]{2,1,0:T(8,128)(2,1)S(1)} %pad_maximum_fusion.mine), channel_id=1, source_target_pairs={{0,8},{8,16},{16,24},{24,32},{32,40},{40,48},{48,56},{56,64},{64,7... | collective-permute-start | bytes 98312 | tf_op jit(solution)/shard_map/ppermute | solution.py:350
  51.0 2.2 %collective-permute-start.11 = (bf16[4,16,256]{2,1,0:T(8,128)(2,1)S(1)}, bf16[4,16,256]{2,1,0:T(8,128)(2,1)S(1)}, u32[]{:S(2)}, u32[]{:S(2)}) collective-permute-start(bf16[4,16,256]{2,1,0:T(8,128)(2,1)S(1)} %pad_maximum_fusion.mine), channel_id=1, source_target_pairs={{0,1},{1,0},{2,3},{3,2},{4,5},{5,4},{6,7},{7,6},{8,9},{9,8},{10,11... | collective-permute-start | bytes 98312 | tf_op jit(solution)/shard_map/ppermute | solution.py:351
  53.2 0.0 collective-permute-done.9.mine
  53.2 1.5 %collective-permute-start.10 = (bf16[4,16,256]{2,1,0:T(8,128)(2,1)S(1)}, bf16[4,16,256]{2,1,0:T(8,128)(2,1)S(1)}, u32[]{:S(2)}, u32[]{:S(2)}) collective-permute-start(bf16[4,16,256]{2,1,0:T(8,128)(2,1)S(1)} %collective-permute-done.9.mine), channel_id=1, source_target_pairs={{0,1},{1,0},{2,3},{3,2},{4,5},{5,4},{6,7},{7,6},{8,9},{9,8},{10,11... | collective-permute-start | bytes 98312 | tf_op jit(solution)/shard_map/ppermute | solution.py:352
  54.7 0.0 copy-done.3
  54.7 0.7 prepare.1
  55.4 0.0 collective-permute-done.11.theirs
  55.4 0.0 copy-done.4
  55.4 0.0 copy-done.6
  55.4 1.5 %own.1.base = f32[8,4096]{1,0:T(8,128)S(1)} custom-call(bf16[4,16,256]{2,1,0:T(8,128)(2,1)S(1)} %pad_maximum_fusion.mine, bf16[4,16,256]{2,1,0:T(8,128)(2,1)S(1)} %collective-permute-done.11.theirs, s32[1,4096]{1,0:T(1,128)S(1)} %bitcast.30, s32[1,4096]{1,0:T(1,128)S(1)} %bitcast.27), custom_call_target="tpu_custom_call" | custom-call | flops 67108864 | bytes 1048576 | tf_op jit(solution)/shard_map/own/pallas_call | solution.py:48
  57.0 0.0 collective-permute-done.10.theirs
  57.0 1.3 %bins.1 = f32[16,1,1152]{2,1,0:T(1,128)S(1)} custom-call(bf16[4,16,256]{2,1,0:T(8,128)(2,1)S(1)} %collective-permute-done.9.mine, bf16[4,16,256]{2,1,0:T(8,128)(2,1)S(1)} %collective-permute-done.10.theirs, s32[1,4096]{1,0:T(1,128)S(1)} %bitcast.28, f32[8,4096]{1,0:T(8,128)S(1)} %own.1.base, bf16[128,4096]{1,0:T(8,128)(2,1)S(1)} %get-tuple-element.12.onehot, ...), custom_call_target="tpu_custom_call" | custom-call | flops 67108864 | bytes 1048576 | tf_op jit(solution)/shard_map/bins/pallas_call | solution.py:48
  58.3 15.7 %all_to_all.16.parts = f32[16,1,1152]{2,1,0:T(1,128)S(1)} all-to-all(f32[16,1,1152]{2,1,0:T(1,128)S(1)} %bins.1), channel_id=1, replica_groups=mesh['row_0'=4,'row_1'=2,'row_2'=4,'col_0'=4,'col_1'=2] {'row_1','col_0'..., dimensions={0} | all-to-all | bytes 147456 | tf_op jit(solution)/shard_map/all_to_all | solution.py:25
  74.0 0.7 merge.1
  74.7 4.5 %all-to-all-start.2 = ((f32[16,1,1152]{2,1,0:T(1,128)}), f32[16,1,1152]{2,1,0:T(1,128)S(1)}, u32[]{:S(2)}, u32[]{:S(2)}) async-start(f32[16,1,1152]{2,1,0:T(1,128)} %merge.1), calls=%async_computation.2 | async-start | bytes 147456 | tf_op jit(solution)/shard_map/all_to_all | solution.py:25
  79.2 0.6 emit.1
  79.8 5.9 %all-to-all-done.2.parts = f32[16,1,1152]{2,1,0:T(1,128)S(1)} async-done(((f32[16,1,1152]{2,1,0:T(1,128)}), f32[16,1,1152]{2,1,0:T(1,128)S(1)}, u32[]{:S(2)}, u32[]{:S(2)}) %all-to-all-start.2) | async-done | bytes 73760 | tf_op jit(solution)/shard_map/all_to_all | solution.py:25
  85.7 0.6 finish.1
  (9 shorter events, 0.1 us)
Async XLA Ops:
  0.6 17.9 %copy-start = (bf16[1,64,64,256]{3,2,1,0:T(8,128)(2,1)S(1)}, bf16[1,64,64,256]{3,2,1,0:T(8,128)(2,1)}, u32[]{:S(2)}) copy-start(bf16[1,64,64,256]{3,2,1,0:T(8,128)(2,1)} %param.11) | copy-start | bytes 6291460
  1.5 19.9 %copy-start.5 = (s32[1,64]{1,0:T(1,128)S(1)}, s32[1,64]{1,0:T(1,128)}, u32[]{:S(2)}) copy-start(s32[1,64]{1,0:T(1,128)} %ranks.1) | copy-start | bytes 772
  19.1 17.6 %copy-start.1 = (bf16[2,1,256,2048]{3,2,1,0:T(8,128)(2,1)S(1)}, bf16[2,1,256,2048]{3,2,1,0:T(8,128)(2,1)}, u32[]{:S(2)}) copy-start(bf16[2,1,256,2048]{3,2,1,0:T(8,128)(2,1)} %param.9) | copy-start | bytes 6291460
  19.1 3.5 %collective-permute-start = (f32[8,8,256]{2,1,0:T(8,128)S(1)}, f32[8,8,256]{2,1,0:T(8,128)S(1)}, u32[]{:S(2)}, u32[]{:S(2)}) collective-permute-start(f32[8,8,256]{2,1,0:T(8,128)S(1)} %send.1), channel_id=1, source_target_pairs={{0,1},{1,0},{2,3},{3,2},{4,5},{5,4},{6,7},{7,6},{8,9},{9,8},{10,11... | collective-permute-start | bytes 196616 | tf_op jit(solution)/shard_map/ppermute | solution.py:317
  21.3 1.3 %collective-permute-start.1 = (bf16[16,256]{1,0:T(8,128)(2,1)S(1)}, bf16[16,256]{1,0:T(8,128)(2,1)S(1)}, u32[]{:S(2)}, u32[]{:S(2)}) collective-permute-start(bf16[16,256]{1,0:T(8,128)(2,1)S(1)} %get-tuple-element.9.local), channel_id=1, source_target_pairs={{0,1},{1,0},{2,3},{3,2},{4,5},{5,4},{6,7},{7,6},{8,9},{9,8},{10,11... | collective-permute-start | bytes 24584 | tf_op jit(solution)/shard_map/ppermute | solution.py:305
  22.0 15.5 %copy-start.2 = (bf16[1,64,64,256]{3,2,1,0:T(8,128)(2,1)S(1)}, bf16[1,64,64,256]{3,2,1,0:T(8,128)(2,1)}, u32[]{:S(2)}) copy-start(bf16[1,64,64,256]{3,2,1,0:T(8,128)(2,1)} %param.10) | copy-start | bytes 6291460
  22.7 8.5 %collective-permute-start.4 = (f16[96,256]{1,0:T(8,128)(2,1)S(1)}, f16[96,256]{1,0:T(8,128)(2,1)S(1)}, u32[]{:S(2)}, u32[]{:S(2)}) collective-permute-start(f16[96,256]{1,0:T(8,128)(2,1)S(1)} %convert_element_type.33), channel_id=1, source_target_pairs={{0,6},{2,0},{4,2},{6,4},{1,7},{3,1},{5,3},{7,5},{8,14},{10,8},{12,... | collective-permute-start | bytes 147464 | tf_op jit(solution)/shard_map/ppermute | solution.py:325
  27.9 5.7 %collective-permute-start.3 = (f16[96,256]{1,0:T(8,128)(2,1)S(1)}, f16[96,256]{1,0:T(8,128)(2,1)S(1)}, u32[]{:S(2)}, u32[]{:S(2)}) collective-permute-start(f16[96,256]{1,0:T(8,128)(2,1)S(1)} %convert_element_type.33), channel_id=1, source_target_pairs={{0,2},{2,4},{4,6},{6,0},{1,3},{3,5},{5,7},{7,1},{8,10},{10,12},{12... | collective-permute-start | bytes 147464 | tf_op jit(solution)/shard_map/ppermute | solution.py:325
  27.9 7.2 %collective-permute-start.2 = (f16[96,256]{1,0:T(8,128)(2,1)S(1)}, f16[96,256]{1,0:T(8,128)(2,1)S(1)}, u32[]{:S(2)}, u32[]{:S(2)}) collective-permute-start(f16[96,256]{1,0:T(8,128)(2,1)S(1)} %convert_element_type.33), channel_id=1, source_target_pairs={{0,4},{2,6},{4,0},{6,2},{1,5},{3,7},{5,1},{7,3},{8,12},{10,14},{12... | collective-permute-start | bytes 147464 | tf_op jit(solution)/shard_map/ppermute | solution.py:325
  35.1 2.4 %collective-permute-start.5 = (bf16[8,8,256]{2,1,0:T(8,128)(2,1)S(1)}, bf16[8,8,256]{2,1,0:T(8,128)(2,1)S(1)}, u32[]{:S(2)}, u32[]{:S(2)}) collective-permute-start(bf16[8,8,256]{2,1,0:T(8,128)(2,1)S(1)} %fusion.2.mine), channel_id=1, source_target_pairs={{0,1},{1,0},{2,3},{3,2},{4,5},{5,4},{6,7},{7,6},{8,9},{9,8},{10,11... | collective-permute-start | bytes 98312 | tf_op jit(solution)/shard_map/ppermute | solution.py:333
  36.7 18.0 %copy-start.3 = (s32[1,1,4096]{2,1,0:T(1,128)S(1)}, s32[1,1,4096]{2,1,0:T(1,128)}, u32[]{:S(2)}) copy-start(s32[1,1,4096]{2,1,0:T(1,128)} %param.15) | copy-start | bytes 49156
  36.7 18.7 %copy-start.4 = (s32[1,1,4096]{2,1,0:T(1,128)S(1)}, s32[1,1,4096]{2,1,0:T(1,128)}, u32[]{:S(2)}) copy-start(s32[1,1,4096]{2,1,0:T(1,128)} %param.14) | copy-start | bytes 49156
  36.8 18.7 %copy-start.6 = (s32[1,1,4096]{2,1,0:T(1,128)S(1)}, s32[1,1,4096]{2,1,0:T(1,128)}, u32[]{:S(2)}) copy-start(s32[1,1,4096]{2,1,0:T(1,128)} %param.13) | copy-start | bytes 49156
  37.9 6.4 %collective-permute-start.8 = (bf16[16,256]{1,0:T(8,128)(2,1)S(1)}, bf16[16,256]{1,0:T(8,128)(2,1)S(1)}, u32[]{:S(2)}, u32[]{:S(2)}) collective-permute-start(bf16[16,256]{1,0:T(8,128)(2,1)S(1)} %get-tuple-element.11), channel_id=1, source_target_pairs={{0,6},{2,0},{4,2},{6,4},{1,7},{3,1},{5,3},{7,5},{8,14},{10,8},{12,... | collective-permute-start | bytes 24584 | tf_op jit(solution)/shard_map/ppermute | solution.py:347
  42.2 4.6 %collective-permute-start.7 = (bf16[16,256]{1,0:T(8,128)(2,1)S(1)}, bf16[16,256]{1,0:T(8,128)(2,1)S(1)}, u32[]{:S(2)}, u32[]{:S(2)}) collective-permute-start(bf16[16,256]{1,0:T(8,128)(2,1)S(1)} %get-tuple-element.11), channel_id=1, source_target_pairs={{0,2},{2,4},{4,6},{6,0},{1,3},{3,5},{5,7},{7,1},{8,10},{10,12},{12... | collective-permute-start | bytes 24584 | tf_op jit(solution)/shard_map/ppermute | solution.py:347
  42.2 6.4 %collective-permute-start.6 = (bf16[16,256]{1,0:T(8,128)(2,1)S(1)}, bf16[16,256]{1,0:T(8,128)(2,1)S(1)}, u32[]{:S(2)}, u32[]{:S(2)}) collective-permute-start(bf16[16,256]{1,0:T(8,128)(2,1)S(1)} %get-tuple-element.11), channel_id=1, source_target_pairs={{0,4},{2,6},{4,0},{6,2},{1,5},{3,7},{5,1},{7,3},{8,12},{10,14},{12... | collective-permute-start | bytes 24584 | tf_op jit(solution)/shard_map/ppermute | solution.py:347
  48.6 4.6 %collective-permute-start.9 = (bf16[4,16,256]{2,1,0:T(8,128)(2,1)S(1)}, bf16[4,16,256]{2,1,0:T(8,128)(2,1)S(1)}, u32[]{:S(2)}, u32[]{:S(2)}) collective-permute-start(bf16[4,16,256]{2,1,0:T(8,128)(2,1)S(1)} %pad_maximum_fusion.mine), channel_id=1, source_target_pairs={{0,8},{8,16},{16,24},{24,32},{32,40},{40,48},{48,56},{56,64},{64,7... | collective-permute-start | bytes 98312 | tf_op jit(solution)/shard_map/ppermute | solution.py:350
  51.0 4.4 %collective-permute-start.11 = (bf16[4,16,256]{2,1,0:T(8,128)(2,1)S(1)}, bf16[4,16,256]{2,1,0:T(8,128)(2,1)S(1)}, u32[]{:S(2)}, u32[]{:S(2)}) collective-permute-start(bf16[4,16,256]{2,1,0:T(8,128)(2,1)S(1)} %pad_maximum_fusion.mine), channel_id=1, source_target_pairs={{0,1},{1,0},{2,3},{3,2},{4,5},{5,4},{6,7},{7,6},{8,9},{9,8},{10,11... | collective-permute-start | bytes 98312 | tf_op jit(solution)/shard_map/ppermute | solution.py:351
  53.2 3.8 %collective-permute-start.10 = (bf16[4,16,256]{2,1,0:T(8,128)(2,1)S(1)}, bf16[4,16,256]{2,1,0:T(8,128)(2,1)S(1)}, u32[]{:S(2)}, u32[]{:S(2)}) collective-permute-start(bf16[4,16,256]{2,1,0:T(8,128)(2,1)S(1)} %collective-permute-done.9.mine), channel_id=1, source_target_pairs={{0,1},{1,0},{2,3},{3,2},{4,5},{5,4},{6,7},{7,6},{8,9},{9,8},{10,11... | collective-permute-start | bytes 98312 | tf_op jit(solution)/shard_map/ppermute | solution.py:352
  74.7 11.0 %all-to-all-start.2 = ((f32[16,1,1152]{2,1,0:T(1,128)}), f32[16,1,1152]{2,1,0:T(1,128)S(1)}, u32[]{:S(2)}, u32[]{:S(2)}) async-start(f32[16,1,1152]{2,1,0:T(1,128)} %merge.1), calls=%async_computation.2 | async-start | bytes 147456 | tf_op jit(solution)/shard_map/all_to_all | solution.py:25
